TPU v7x, 256 devices: a whole 4x4x8 slice. The times are simulated.
256 devices in a mesh: gx: 8 (over z), gy: 4 (over x_hi, core), gz: 8 (over x_lo, y).
Axes of the slice: x: 4 (x_hi: 2, x_lo: 2; x = x_hi * 2 + x_lo), y: 4, z: 8, core: 2. Of those that a mesh axis runs over, the one named last changes fastest.
Arguments:
- density: float32 [3, 128, 256, 1024], P(None, 'gx', 'gy', 'gz'), may hold values from -6 to 6
- efficiency: float32 [128, 256, 1024], P('gx', 'gy', 'gz'), may hold values from 0.5 to 2
Outputs:
- ionized: float32 [3, 128, 256, 1024], P(None, 'gx', 'gy', 'gz')
All inputs are finite; a program needn't handle non-finite values.
Results may differ from a plain program's by a relative error of at most 0.00005.
Values sent between devices are 32-bit elements; how exact they have to be, the bound alone decides.
No kernel may reach another device: no remote copies, remote signals or barrier semaphores. Data moves between devices by JAX's collectives and lax.ppermute only.
A program may use at most 128 MiB of HBM per device.

v0:
```python
import jax
import jax.numpy as jnp
from jax import lax
from jax.sharding import PartitionSpec as P

R_SMALL = 4
R_LARGE = 8


def extended(block, sides, width):
    for axis, dim in sides:
        count = lax.axis_size(axis)
        forward = [(i, i + 1) for i in range(count - 1)]
        forward.append((count - 1, 0))
        backward = [(target, source) for source, target in forward]
        low = lax.ppermute(
            lax.slice_in_dim(block, block.shape[dim] - width, None, axis=dim), axis, forward
        )
        high = lax.ppermute(lax.slice_in_dim(block, 0, width, axis=dim), axis, backward)
        block = jnp.concatenate([low, block, high], axis=dim)
    return block


def band_matrix(radius, length):
    rows = lax.broadcasted_iota(jnp.int32, (length, length + 2 * radius), 0)
    columns = lax.broadcasted_iota(jnp.int32, (length, length + 2 * radius), 1)
    offset = (columns - rows - radius).astype(jnp.float32)
    offsets = jnp.arange(-radius, radius + 1).astype(jnp.float32)
    raw_weights = 1.0 - (offsets / (radius + 1.0)) ** 2
    scale = jnp.sqrt(jnp.sum(raw_weights * raw_weights))
    inside = jnp.abs(offset) <= radius
    return jnp.where(inside, (1.0 - (offset / (radius + 1.0)) ** 2) / scale, 0.0)


def smooth_along(volume, radius, axis_dim):
    letters = "abcd"[: volume.ndim]
    length = volume.shape[axis_dim] - 2 * radius
    target = letters[:axis_dim] + "z" + letters[axis_dim + 1 :]
    formula = "z" + letters[axis_dim] + "," + letters + "->" + target
    return jnp.einsum(formula, band_matrix(radius, length), volume, precision=lax.Precision.HIGHEST)


def on_device(density, efficiency):
    trim = R_LARGE - R_SMALL
    slab = extended(density, (("gz", 3),), R_LARGE)
    small_part = smooth_along(slab[:, :, :, trim:-trim], R_SMALL, 3)
    large_part = smooth_along(slab, R_LARGE, 3)
    small_y = extended(small_part, (("gy", 2),), R_SMALL)
    large_y = extended(large_part, (("gy", 2),), R_LARGE)
    small_part = smooth_along(small_y, R_SMALL, 2)
    large_part = smooth_along(large_y, R_LARGE, 2)
    small_x = extended(small_part, (("gx", 1),), R_SMALL)
    large_x = extended(large_part, (("gx", 1),), R_LARGE)
    smooth_small = smooth_along(small_x, R_SMALL, 1)
    smooth_large = smooth_along(large_x, R_LARGE, 1)
    level_small = efficiency[None] * smooth_small - 0.3
    level_large = efficiency[None] * smooth_large - 0.1
    return jnp.clip(0.5 + 0.25 * jnp.maximum(level_small, level_large), 0.0, 1.0)


def solution(mesh):
    placed = (P(None, "gx", "gy", "gz"), P("gx", "gy", "gz"))
    return jax.shard_map(
        on_device, mesh=mesh, in_specs=placed, out_specs=P(None, "gx", "gy", "gz"), check_vma=False
    )
```

profile of v0, /device:TPU:1, one launch (start us, length us, event | category | flops | bytes accessed | tf_op | source)
XLA Modules:
  0.0 76.8 jit_solution(17870272203635093761)
XLA Ops:
  0.0 2.5 %fusion.171 = (f32[3,16,64,8]{3,2,1,0:T(8,128)S(1)}, f32[3,16,64,8]{3,2,1,0:T(8,128)S(1)}) fusion(f32[3,16,64,128]{3,2,1,0:T(8,128)} %param.2), kind=kLoop, calls=%fused_computation.178 | loop fusion | bytes 393216 | tf_op jit(solution)/shard_map/slice | solution.py:17
  2.5 0.5 copy.22
  2.9 4.5 %collective-permute-start.1 = (f32[3,16,64,8]{2,3,1,0:T(8,128)S(1)}, f32[3,16,64,8]{2,3,1,0:T(8,128)S(1)}, u32[]{:S(2)}, u32[]{:S(2)}) collective-permute-start(f32[3,16,64,8]{2,3,1,0:T(8,128)S(1)} %copy.22), channel_id=1, source_target_pairs={{1,0},{2,1},{3,2},{4,3},{5,4},{6,5},{7,6},{0,7},{9,8},{10,9},{11,1... | collective-permute-start | bytes 294920 | tf_op jit(solution)/shard_map/ppermute | solution.py:19
  7.4 1.1 %copy.21 = f32[3,16,64,8]{2,3,1,0:T(8,128)} copy(f32[3,16,64,8]{3,2,1,0:T(8,128)S(1)} %get-tuple-element.13) | data formatting | bytes 196608
  8.6 0.0 collective-permute-start
  8.6 0.7 multiply_reduce_fusion.1
  9.9 0.7 multiply_reduce_fusion
  11.3 0.0 copy-start
  11.3 0.0 collective-permute-done.1
  11.3 0.5 copy.11
  11.8 4.7 %collective-permute-done = f32[3,16,64,8]{2,3,1,0:T(8,128)} collective-permute-done((f32[3,16,64,8]{2,3,1,0:T(8,128)}, f32[3,16,64,8]{2,3,1,0:T(8,128)}, u32[]{:S(2)}, u32[]{:S(2)}) %collective-permute-start) | collective-permute-done | bytes 98336 | tf_op jit(solution)/shard_map/ppermute | solution.py:16
  16.5 2.6 %copy.10 = f32[3,16,64,8]{3,2,1,0:T(8,128)} copy(f32[3,16,64,8]{2,3,1,0:T(8,128)} %collective-permute-done) | data formatting | bytes 196608 | tf_op jit(solution)/shard_map/ppermute | solution.py:16
  19.1 0.0 copy-done
  19.1 2.7 %pad_maximum_fusion = f32[3,16,64,144]{3,2,1,0:T(8,128)S(1)} fusion(f32[3,16,64,8]{3,2,1,0:T(8,128)S(1)} %copy.11, f32[3,16,64,128]{3,2,1,0:T(8,128)S(1)} %copy-done, f32[3,16,64,8]{3,2,1,0:T(8,128)} %copy.10), kind=kLoop, calls=%fused_computation.2 | loop fusion | flops 884736 | bytes 3538944 | tf_op jit(solution)/shard_map/concatenate | solution.py:20
  21.8 2.7 %fusion = f32[3,16,64,128]{3,2,1,0:T(8,128)S(1)} fusion(f32[3,16,64,144]{3,2,1,0:T(8,128)S(1)} %pad_maximum_fusion, f32[]{:T(128)S(6)} %sqrt.4), kind=kOutput, calls=%fused_computation | convolution fusion | flops 641902592 | bytes 3342340 | tf_op jit(solution)/shard_map/zd,abcd->abcz/dot_general | solution.py:40
  24.5 1.9 %collective-permute-start.3 = (f32[3,16,4,128]{3,2,1,0:T(4,128)S(1)}, f32[3,16,4,128]{3,2,1,0:T(4,128)S(1)}, u32[]{:S(2)}, u32[]{:S(2)}) collective-permute-start(f32[3,16,4,128]{3,2,1,0:T(4,128)S(1)} %get-tuple-element.12), channel_id=1, source_target_pairs={{8,0},{16,8},{24,16},{0,24},{9,1},{17,9},{25,17},{1,25},{10,2},{18... | collective-permute-start | bytes 294920 | tf_op jit(solution)/shard_map/ppermute | solution.py:19
  26.4 2.4 %collective-permute-start.2 = (f32[3,16,4,128]{3,2,1,0:T(4,128)S(1)}, f32[3,16,4,128]{3,2,1,0:T(4,128)S(1)}, u32[]{:S(2)}, u32[]{:S(2)}) collective-permute-start(f32[3,16,4,128]{3,2,1,0:T(4,128)S(1)} %get-tuple-element.11), channel_id=1, source_target_pairs={{0,8},{8,16},{16,24},{24,0},{1,9},{9,17},{17,25},{25,1},{2,10},{10... | collective-permute-start | bytes 294920 | tf_op jit(solution)/shard_map/ppermute | solution.py:16
  28.8 2.7 %fusion.32 = f32[3,16,64,128]{3,2,1,0:T(8,128)S(1)} fusion(f32[3,16,64,144]{3,2,1,0:T(8,128)S(1)} %pad_maximum_fusion, f32[]{:T(128)S(6)} %sqrt.5), kind=kOutput, calls=%fused_computation.31 | convolution fusion | flops 679661568 | bytes 3342340 | tf_op jit(solution)/shard_map/zd,abcd->abcz/dot_general | solution.py:40
  31.5 0.3 collective-permute-start.7
  31.8 3.2 %collective-permute-start.6 = (f32[3,16,8,128]{3,2,1,0:T(8,128)S(1)}, f32[3,16,8,128]{3,2,1,0:T(8,128)S(1)}, u32[]{:S(2)}, u32[]{:S(2)}) collective-permute-start(f32[3,16,8,128]{3,2,1,0:T(8,128)S(1)} %get-tuple-element.7), channel_id=1, source_target_pairs={{0,8},{8,16},{16,24},{24,0},{1,9},{9,17},{17,25},{25,1},{2,10},{10... | collective-permute-start | bytes 589832 | tf_op jit(solution)/shard_map/ppermute | solution.py:16
  35.0 0.0 collective-permute-done.3
  35.0 0.0 collective-permute-done.2
  35.0 1.8 %fusion.26 = f32[3,16,64,128]{3,2,1,0:T(8,128)S(1)} fusion(f32[3,16,4,128]{3,2,1,0:T(4,128)S(1)} %collective-permute-done.3, f32[3,16,64,128]{3,2,1,0:T(8,128)S(1)} %fusion, f32[3,16,4,128]{3,2,1,0:T(4,128)S(1)} %collective-permute-done.2, f32[]{:T(128)S(6)} %sqrt.4), kind=kOutput, calls=%fused_computation.29 | convolution fusion | flops 340669440 | bytes 3342340 | tf_op jit(solution)/shard_map/zc,abcd->abzd/dot_general | solution.py:40
  36.8 0.1 fusion.169
  36.9 5.7 %collective-permute-start.5 = (f32[3,4,64,128]{3,2,1,0:T(8,128)S(1)}, f32[3,4,64,128]{3,2,1,0:T(8,128)S(1)}, u32[]{:S(2)}, u32[]{:S(2)}) collective-permute-start(f32[3,4,64,128]{3,2,1,0:T(8,128)S(1)} %get-tuple-element.10), channel_id=1, source_target_pairs={{32,0},{64,32},{96,64},{128,96},{160,128},{192,160},{224,192},{0,2... | collective-permute-start | bytes 1179656 | tf_op jit(solution)/shard_map/ppermute | solution.py:19
  42.6 0.0 collective-permute-start.4
  42.6 0.0 collective-permute-done.7
  42.6 0.0 collective-permute-done.6
  42.6 1.7 %fusion.29 = f32[3,16,64,128]{3,2,1,0:T(8,128)S(1)} fusion(f32[3,16,8,128]{3,2,1,0:T(8,128)S(1)} %collective-permute-done.7, f32[3,16,64,128]{3,2,1,0:T(8,128)S(1)} %fusion.32, f32[3,16,8,128]{3,2,1,0:T(8,128)S(1)} %collective-permute-done.6, f32[]{:T(128)S(6)} %sqrt.5), kind=kOutput, calls=%fused_computation.30 | convolution fusion | flops 378521600 | bytes 3538948 | tf_op jit(solution)/shard_map/zc,abcd->abzd/dot_general | solution.py:40
  44.2 0.0 copy-start.1
  44.3 0.1 fusion.167
  44.4 2.8 %collective-permute-start.9 = (f32[3,8,64,128]{3,2,1,0:T(8,128)S(1)}, f32[3,8,64,128]{3,2,1,0:T(8,128)S(1)}, u32[]{:S(2)}, u32[]{:S(2)}) collective-permute-start(f32[3,8,64,128]{3,2,1,0:T(8,128)S(1)} %get-tuple-element.6), channel_id=1, source_target_pairs={{32,0},{64,32},{96,64},{128,96},{160,128},{192,160},{224,192},{0,2... | collective-permute-start | bytes 2359304 | tf_op jit(solution)/shard_map/ppermute | solution.py:19
  47.2 0.0 collective-permute-start.8
  47.2 0.0 copy-done.1
  47.2 0.3 copy.7
  47.5 4.0 %collective-permute-done.5 = f32[3,4,64,128]{3,2,1,0:T(8,128)S(1)} collective-permute-done((f32[3,4,64,128]{3,2,1,0:T(8,128)S(1)}, f32[3,4,64,128]{3,2,1,0:T(8,128)S(1)}, u32[]{:S(2)}, u32[]{:S(2)}) %collective-permute-start.5) | collective-permute-done | bytes 393248 | tf_op jit(solution)/shard_map/ppermute | solution.py:19
  51.5 3.4 %collective-permute-done.4 = f32[3,4,64,128]{3,2,1,0:T(8,128)S(1)} collective-permute-done((f32[3,4,64,128]{3,2,1,0:T(8,128)S(1)}, f32[3,4,64,128]{3,2,1,0:T(8,128)S(1)}, u32[]{:S(2)}, u32[]{:S(2)}) %collective-permute-start.4) | collective-permute-done | bytes 393248 | tf_op jit(solution)/shard_map/ppermute | solution.py:16
  54.9 0.3 pad_maximum_fusion.2
  55.2 2.9 %fusion.4 = f32[3,64,128,16]{2,3,1,0:T(8,128)S(1)} fusion(f32[3,24,64,128]{3,2,1,0:T(8,128)S(1)} %pad_maximum_fusion.2, f32[]{:T(128)S(6)} %sqrt.4), kind=kOutput, calls=%fused_computation.7 | convolution fusion | flops 113250048 | bytes 3932164 | tf_op jit(solution)/shard_map/zb,abcd->azcd/dot_general | solution.py:40
  58.1 9.3 %collective-permute-done.9 = f32[3,8,64,128]{3,2,1,0:T(8,128)S(1)} collective-permute-done((f32[3,8,64,128]{3,2,1,0:T(8,128)S(1)}, f32[3,8,64,128]{3,2,1,0:T(8,128)S(1)}, u32[]{:S(2)}, u32[]{:S(2)}) %collective-permute-start.9) | collective-permute-done | bytes 786464 | tf_op jit(solution)/shard_map/ppermute | solution.py:19
  67.4 3.4 %collective-permute-done.8 = f32[3,8,64,128]{3,2,1,0:T(8,128)S(1)} collective-permute-done((f32[3,8,64,128]{3,2,1,0:T(8,128)S(1)}, f32[3,8,64,128]{3,2,1,0:T(8,128)S(1)}, u32[]{:S(2)}, u32[]{:S(2)}) %collective-permute-start.8) | collective-permute-done | bytes 786464 | tf_op jit(solution)/shard_map/ppermute | solution.py:16
  70.8 0.4 pad_maximum_fusion.1
  71.2 3.9 %fusion.22 = f32[3,16,64,128]{3,1,2,0:T(8,128)S(1)} fusion(f32[3,64,128,16]{2,3,1,0:T(8,128)S(1)} %fusion.4, f32[3,32,64,128]{3,2,1,0:T(8,128)S(1)} %pad_maximum_fusion.1, f32[16,64,128]{2,0,1:T(8,128)S(1)} %copy.7, f32[]{:T(128)S(6)} %sqrt.5), kind=kOutput, calls=%fused_computation.26 | convolution fusion | flops 154145792 | bytes 6815748 | tf_op jit(solution)/shard_map/zb,abcd->azcd/dot_general | solution.py:40
  75.2 1.6 %copy.14 = f32[3,16,64,128]{3,2,1,0:T(8,128)} copy(f32[3,16,64,128]{3,1,2,0:T(8,128)S(1)} %fusion.22) | data formatting | bytes 3145728 | tf_op jit(solution)/shard_map/jit(clip)/min | solution.py:58
  (2 shorter events, 0.1 us)
Async XLA Ops:
  2.9 8.4 %collective-permute-start.1 = (f32[3,16,64,8]{2,3,1,0:T(8,128)S(1)}, f32[3,16,64,8]{2,3,1,0:T(8,128)S(1)}, u32[]{:S(2)}, u32[]{:S(2)}) collective-permute-start(f32[3,16,64,8]{2,3,1,0:T(8,128)S(1)} %copy.22), channel_id=1, source_target_pairs={{1,0},{2,1},{3,2},{4,3},{5,4},{6,5},{7,6},{0,7},{9,8},{10,9},{11,1... | collective-permute-start | bytes 294920 | tf_op jit(solution)/shard_map/ppermute | solution.py:19
  8.6 7.9 %collective-permute-start = (f32[3,16,64,8]{2,3,1,0:T(8,128)}, f32[3,16,64,8]{2,3,1,0:T(8,128)}, u32[]{:S(2)}, u32[]{:S(2)}) collective-permute-start(f32[3,16,64,8]{2,3,1,0:T(8,128)} %copy.21), channel_id=1, source_target_pairs={{0,1},{1,2},{2,3},{3,4},{4,5},{5,6},{6,7},{7,0},{8,9},{9,10},{10,1... | collective-permute-start | bytes 294920 | tf_op jit(solution)/shard_map/ppermute | solution.py:16
  11.3 7.8 %copy-start = (f32[3,16,64,128]{3,2,1,0:T(8,128)S(1)}, f32[3,16,64,128]{3,2,1,0:T(8,128)}, u32[]{:S(2)}) copy-start(f32[3,16,64,128]{3,2,1,0:T(8,128)} %param.2) | copy-start | bytes 4718596
  24.5 10.6 %collective-permute-start.3 = (f32[3,16,4,128]{3,2,1,0:T(4,128)S(1)}, f32[3,16,4,128]{3,2,1,0:T(4,128)S(1)}, u32[]{:S(2)}, u32[]{:S(2)}) collective-permute-start(f32[3,16,4,128]{3,2,1,0:T(4,128)S(1)} %get-tuple-element.12), channel_id=1, source_target_pairs={{8,0},{16,8},{24,16},{0,24},{9,1},{17,9},{25,17},{1,25},{10,2},{18... | collective-permute-start | bytes 294920 | tf_op jit(solution)/shard_map/ppermute | solution.py:19
  26.4 8.7 %collective-permute-start.2 = (f32[3,16,4,128]{3,2,1,0:T(4,128)S(1)}, f32[3,16,4,128]{3,2,1,0:T(4,128)S(1)}, u32[]{:S(2)}, u32[]{:S(2)}) collective-permute-start(f32[3,16,4,128]{3,2,1,0:T(4,128)S(1)} %get-tuple-element.11), channel_id=1, source_target_pairs={{0,8},{8,16},{16,24},{24,0},{1,9},{9,17},{17,25},{25,1},{2,10},{10... | collective-permute-start | bytes 294920 | tf_op jit(solution)/shard_map/ppermute | solution.py:16
  31.5 11.0 %collective-permute-start.7 = (f32[3,16,8,128]{3,2,1,0:T(8,128)S(1)}, f32[3,16,8,128]{3,2,1,0:T(8,128)S(1)}, u32[]{:S(2)}, u32[]{:S(2)}) collective-permute-start(f32[3,16,8,128]{3,2,1,0:T(8,128)S(1)} %get-tuple-element.8), channel_id=1, source_target_pairs={{8,0},{16,8},{24,16},{0,24},{9,1},{17,9},{25,17},{1,25},{10,2},{18... | collective-permute-start | bytes 589832 | tf_op jit(solution)/shard_map/ppermute | solution.py:19
  31.8 10.8 %collective-permute-start.6 = (f32[3,16,8,128]{3,2,1,0:T(8,128)S(1)}, f32[3,16,8,128]{3,2,1,0:T(8,128)S(1)}, u32[]{:S(2)}, u32[]{:S(2)}) collective-permute-start(f32[3,16,8,128]{3,2,1,0:T(8,128)S(1)} %get-tuple-element.7), channel_id=1, source_target_pairs={{0,8},{8,16},{16,24},{24,0},{1,9},{9,17},{17,25},{25,1},{2,10},{10... | collective-permute-start | bytes 589832 | tf_op jit(solution)/shard_map/ppermute | solution.py:16
  36.9 14.6 %collective-permute-start.5 = (f32[3,4,64,128]{3,2,1,0:T(8,128)S(1)}, f32[3,4,64,128]{3,2,1,0:T(8,128)S(1)}, u32[]{:S(2)}, u32[]{:S(2)}) collective-permute-start(f32[3,4,64,128]{3,2,1,0:T(8,128)S(1)} %get-tuple-element.10), channel_id=1, source_target_pairs={{32,0},{64,32},{96,64},{128,96},{160,128},{192,160},{224,192},{0,2... | collective-permute-start | bytes 1179656 | tf_op jit(solution)/shard_map/ppermute | solution.py:19
  42.6 12.3 %collective-permute-start.4 = (f32[3,4,64,128]{3,2,1,0:T(8,128)S(1)}, f32[3,4,64,128]{3,2,1,0:T(8,128)S(1)}, u32[]{:S(2)}, u32[]{:S(2)}) collective-permute-start(f32[3,4,64,128]{3,2,1,0:T(8,128)S(1)} %get-tuple-element.9), channel_id=1, source_target_pairs={{0,32},{32,64},{64,96},{96,128},{128,160},{160,192},{192,224},{224... | collective-permute-start | bytes 1179656 | tf_op jit(solution)/shard_map/ppermute | solution.py:16
  44.2 2.9 %copy-start.1 = (f32[16,64,128]{2,1,0:T(8,128)S(1)}, f32[16,64,128]{2,1,0:T(8,128)}, u32[]{:S(2)}) copy-start(f32[16,64,128]{2,1,0:T(8,128)} %param.3) | copy-start | bytes 1572868
  44.4 23.0 %collective-permute-start.9 = (f32[3,8,64,128]{3,2,1,0:T(8,128)S(1)}, f32[3,8,64,128]{3,2,1,0:T(8,128)S(1)}, u32[]{:S(2)}, u32[]{:S(2)}) collective-permute-start(f32[3,8,64,128]{3,2,1,0:T(8,128)S(1)} %get-tuple-element.6), channel_id=1, source_target_pairs={{32,0},{64,32},{96,64},{128,96},{160,128},{192,160},{224,192},{0,2... | collective-permute-start | bytes 2359304 | tf_op jit(solution)/shard_map/ppermute | solution.py:19
  47.2 23.7 %collective-permute-start.8 = (f32[3,8,64,128]{3,2,1,0:T(8,128)S(1)}, f32[3,8,64,128]{3,2,1,0:T(8,128)S(1)}, u32[]{:S(2)}, u32[]{:S(2)}) collective-permute-start(f32[3,8,64,128]{3,2,1,0:T(8,128)S(1)} %get-tuple-element.5), channel_id=1, source_target_pairs={{0,32},{32,64},{64,96},{96,128},{128,160},{160,192},{192,224},{224... | collective-permute-start | bytes 2359304 | tf_op jit(solution)/shard_map/ppermute | solution.py:16
where the time goes:
time: 77 us; the launch traced here: 76.8 us
  waiting for transfers between devices  24.9 us (32%)
  starting transfers between devices  20.7 us (27%)
  matrix products  15.7 us (20%)
  local copies, waits for them, and re-layouts  9.29 us (12%)
  other arithmetic  4.69 us (6%)
  between operations  1.5 us (2%)
    dot_general x6, matrix products, smooth_along(): jnp.einsum(formula, band_matrix(radius, length), volume, precision=lax.Pr...  15.7 us
    ppermute x5, starting transfers between devices, extended(): lax.ppermute(lax.slice_in_dim(block, 0, width, axis=dim), axis, backward)  15.1 us
    ppermute x5, waiting for transfers between devices, extended(): lax.ppermute(lax.slice_in_dim(block, 0, width, axis=dim), axis, backward)  13.4 us
    ppermute x5, waiting for transfers between devices, extended(): lax.ppermute(lax.slice_in_dim(block, block.shape[dim] - width, None, axis...  11.5 us
    ppermute x5, starting transfers between devices, extended(): lax.ppermute(lax.slice_in_dim(block, block.shape[dim] - width, None, axis...  5.67 us
    concatenate x3, other arithmetic, extended(): block = jnp.concatenate([low, block, high], axis=dim)  3.35 us
    slice x5, local copies, waits for them, and re-layouts, extended(): lax.slice_in_dim(block, block.shape[dim] - width, None, axis=dim)  2.73 us
    ppermute x1, local copies, waits for them, and re-layouts, extended(): lax.ppermute(lax.slice_in_dim(block, block.shape[dim] - width, None, axis...  2.56 us
  transfers between devices with their start and end apart: 10, of which 5 were waited for; matrix products, arithmetic and copies ran while one was open for 17% of the time, Pallas kernels for 0%

commit v1 on v0

v1 whole, which is shorter than its diff:
```python
import math

import jax
import jax.numpy as jnp
from jax import lax
from jax.experimental import pallas as pl
from jax.experimental.pallas import tpu as pltpu
from jax.sharding import PartitionSpec as P


R_SMALL = 4
R_LARGE = 8
H = R_LARGE
CHUNKS = ((0, 2), (2, 3))
VMEM = pl.BlockSpec(memory_space=pltpu.VMEM)
F32 = jnp.float32
BF16 = jnp.bfloat16
PARAMS = pltpu.CompilerParams(vmem_limit_bytes=24 * 2**20)


def weight(radius, k):
    return float((radius + 1) ** 2 - k * k)


def scale_of(radius):
    n = float((radius + 1) ** 2)
    total = sum((1.0 - k * k / n) ** 2 for k in range(-radius, radius + 1))
    return (1.0 / (n * math.sqrt(total))) ** 3


def near(x):
    return pltpu.with_memory_space_constraint(x, pltpu.VMEM)


def run(body, args, outs, scratch=()):
    return pl.pallas_call(
        body,
        out_shape=[pltpu.VMEM(s, F32) for s in outs],
        in_specs=[VMEM] * len(args),
        out_specs=[VMEM] * len(outs),
        scratch_shapes=list(scratch),
        compiler_params=PARAMS,
    )(*[near(a) for a in args])


def band(edge):
    shape = (256, 256)
    row = lax.broadcasted_iota(jnp.int32, shape, 0) % 128
    col = lax.broadcasted_iota(jnp.int32, shape, 1)
    z = col % 128
    if edge:
        at = jnp.where(row < 64, row - H, 128 + row - 64)
        used = row % 64 < H
        d = at - z
    else:
        d = row - z
    reach = jnp.where(col < 128, R_SMALL + 1, R_LARGE + 1)
    value = reach * reach - d * d
    keep = value > 0
    if edge:
        keep = keep & used
    return jnp.where(keep, value, 0).astype(F32).astype(BF16)


def mul(m, w):
    hi = m.astype(BF16)
    lo = (m - hi.astype(F32)).astype(BF16)
    return jnp.dot(jnp.concatenate([hi, lo], axis=1), w, preferred_element_type=F32)


def lanes(shape):
    return lax.broadcasted_iota(jnp.int32, shape, len(shape) - 1)


def edge_of(pack, p):
    return pltpu.roll(pack, (128 - H * p) % 128, 1) if p else pack


def taps(get, radius):
    total = weight(radius, 0) * get(0)
    for k in range(1, radius + 1):
        total = total + weight(radius, k) * (get(k) + get(-k))
    return total


def x_halo(total, before, after, i, n, radius):
    for a in range(radius):
        d = i + radius - a
        if d <= radius:
            total = total + weight(radius, d) * before[a]
    for b in range(radius):
        d = n + b - i
        if d <= radius:
            total = total + weight(radius, d) * after[b]
    return total


def pack_body(d, zr, zl, xeu, xed):
    s = pl.program_id(0)
    _, nx, ny, nz = d.shape
    xeu[s, :, 0:H] = d[0, nx - H :, 0:H]
    xeu[s, :, H:] = d[0, nx - H :, ny - H :]
    xed[s, :, 0:H] = d[0, 0:H, 0:H]
    xed[s, :, H:] = d[0, 0:H, ny - H :]
    lane = lanes((ny, nz))
    right = jnp.zeros((ny, nz), F32)
    left = jnp.zeros((ny, nz), F32)
    for x in range(nx):
        r = pltpu.roll(d[0, x], (H * x + H) % nz, 1)
        right = jnp.where((lane >= H * x) & (lane < H * x + H), r, right)
        at = (H * x + H) % nz
        left = jnp.where((lane >= at) & (lane < at + H), r, left)
    zr[s] = right
    zl[s] = pltpu.roll(left, nz - H, 1)


def second_body(za, zb, xzu, xzd):
    snaps, ny, nz = za.shape
    half = nz // 2
    lane = lanes((ny, nz))
    for s in range(snaps):
        xzu[s] = jnp.where(lane < half, pltpu.roll(za[s], half, 1), zb[s])
        xzd[s] = jnp.where(lane < half, za[s], pltpu.roll(zb[s], half, 1))


def slab_body(d, *outs):
    nx, ny = d.shape[1:3]
    for (low, high), up, down in zip(CHUNKS, outs[0::2], outs[1::2]):
        up[...] = d[low:high, nx - H :, H : ny - H]
        down[...] = d[low:high, 0:H, H : ny - H]


def rim_body(d, xea, xeb, xza, xzd, xzu, xzb, ws, wl, yu, yd, zs, zl):
    snaps, nx, ny, nz = d.shape
    wm, we = band(False), band(True)

    def ends(v):
        return jnp.concatenate([v[0:H], v[ny - H :]], axis=0)

    def snap(s, carry):
        packs = [ends(p[s]) for p in (xza, xzd, xzu, xzb)]
        main = [xea[s, p] for p in range(H)]
        main += [ends(d[s, x]) for x in range(nx)]
        main += [xeb[s, p] for p in range(H)]
        side = [edge_of(packs[p // H], p % H) for p in range(nx + 2 * H)]
        out = mul(jnp.concatenate(main, axis=0), wm) + mul(jnp.concatenate(side, axis=0), we)
        out = out.reshape(nx + 2 * H, 2 * H, 2 * nz)
        zs[...] = out[:, :, :nz]
        zl[...] = out[:, :, nz:]
        small = taps(lambda k: zs[H + k : H + k + nx], R_SMALL)
        large = taps(lambda k: zl[H + k : H + k + nx], R_LARGE)
        ws[s] = small
        wl[s] = large
        yu[s, 0:nx] = large[:, H:]
        yd[s, 0:nx] = large[:, 0:H]
        half = nx // 2
        yu[s, nx:, 0:R_SMALL] = small[0:half, 2 * H - R_SMALL :]
        yu[s, nx:, R_SMALL:] = small[half:, 2 * H - R_SMALL :]
        yd[s, nx:, 0:R_SMALL] = small[0:half, 0:R_SMALL]
        yd[s, nx:, R_SMALL:] = small[half:, 0:R_SMALL]
        return carry

    lax.fori_loop(0, snaps, snap, 0)


def middle_body(d, xza, xzd, xzu, xzb, acc_s, acc_l, zs, zl):
    snaps, nx, ny, nz = d.shape
    wm, we = band(False), band(True)
    inner = ny - 2 * H

    def snap(s, carry):
        for q, pack in enumerate((xza, xzd, xzu, xzb)):
            rows = pack[s, H : ny - H]
            for p in range(H):
                z = mul(edge_of(rows, p), we)
                at = q * H + p
                if H <= at < H + nx:
                    z = z + mul(d[s, at - H, H : ny - H], wm)
                zs[at] = z[:, :nz]
                zl[at] = z[:, nz:]
        for r in range(0, inner, 8):
            acc_s[s, :, r : r + 8] = taps(lambda k: zs[H + k : H + k + nx, r : r + 8], R_SMALL)
            acc_l[s, :, r : r + 8] = taps(lambda k: zl[H + k : H + k + nx, r : r + 8], R_LARGE)
        return carry

    lax.fori_loop(0, snaps, snap, 0)


def last_body(low, xia, xib, acc_s, acc_l, ws, wl, ya, yb, eff, *rest):
    out, us, ul = rest[-3:]
    j = pl.program_id(0)
    s = j + low
    nx, inner, nz = acc_s.shape[1:]
    ny = inner + 2 * H
    wm = band(False)
    scale_s, scale_l = scale_of(R_SMALL), scale_of(R_LARGE)
    half = nx // 2
    ul[:, 0:H] = ya[s, 0:nx]
    ul[:, H : 2 * H] = wl[s, :, 0:H]
    ul[:, ny : ny + H] = wl[s, :, H:]
    ul[:, ny + H :] = yb[s, 0:nx]
    us[0:half, H - R_SMALL : H] = ya[s, nx:, 0:R_SMALL]
    us[half:, H - R_SMALL : H] = ya[s, nx:, R_SMALL:]
    us[:, H : 2 * H] = ws[s, :, 0:H]
    us[:, ny : ny + H] = ws[s, :, H:]
    us[0:half, ny + H : ny + H + R_SMALL] = yb[s, nx:, 0:R_SMALL]
    us[half:, ny + H : ny + H + R_SMALL] = yb[s, nx:, R_SMALL:]
    za = mul(xia[j].reshape(H * inner, nz), wm).reshape(H, inner, 2 * nz)
    zb = mul(xib[j].reshape(H * inner, nz), wm).reshape(H, inner, 2 * nz)
    cut = H - R_SMALL
    for r in range(0, inner, 8):
        a, b = za[:, r : r + 8], zb[:, r : r + 8]
        for i in range(nx):
            us[i, 2 * H + r : 2 * H + r + 8] = x_halo(
                acc_s[s, i, r : r + 8], a[cut:, :, :nz], b[:, :, :nz], i, nx, R_SMALL
            )
            ul[i, 2 * H + r : 2 * H + r + 8] = x_halo(
                acc_l[s, i, r : r + 8], a[:, :, nz:], b[:, :, nz:], i, nx, R_LARGE
            )
    for r in range(0, ny, 8):
        small = taps(lambda k: us[:, r + H + k : r + H + k + 8], R_SMALL)
        large = taps(lambda k: ul[:, r + H + k : r + H + k + 8], R_LARGE)
        e = eff[:, r : r + 8]
        level_small = e * (small * scale_s) - 0.3
        level_large = e * (large * scale_l) - 0.1
        top = 0.5 + 0.25 * jnp.maximum(level_small, level_large)
        out[0, :, r : r + 8] = jnp.minimum(jnp.maximum(top, 0.0), 1.0)


def last(low, high, args, before, shape):
    nx, ny, nz = shape[1:]
    extra = [] if before is None else [before]
    return pl.pallas_call(
        lambda *refs: last_body(low, *refs),
        out_shape=jax.ShapeDtypeStruct(shape, F32),
        grid=(high - low,),
        in_specs=[VMEM] * len(args) + [pl.BlockSpec(memory_space=pl.ANY)] * len(extra),
        out_specs=pl.BlockSpec((1, nx, ny, nz), lambda j: (j + low, 0, 0, 0)),
        scratch_shapes=[pltpu.VMEM((nx, ny + 2 * H, nz), F32)] * 2,
        input_output_aliases={len(args): 0} if extra else {},
        compiler_params=PARAMS,
        name="last",
    )(*[near(a) for a in args], *extra)


def shift(block, axis, step):
    n = lax.axis_size(axis)
    return lax.ppermute(block, axis, [(i, (i + step) % n) for i in range(n)])


def both(axis, up, down):
    return shift(up, axis, 1), shift(down, axis, -1)


def steps(density, efficiency):
    block = density.shape
    snaps, nx, ny, nz = block
    inner = ny - 2 * H
    zpack = (snaps, ny, nz)
    xe = (snaps, H, 2 * H, nz)
    zr, zl, xeu, xed = pl.pallas_call(
        pack_body,
        out_shape=[pltpu.VMEM(s, F32) for s in (zpack, zpack, xe, xe)],
        grid=(snaps,),
        in_specs=[pl.BlockSpec((1, nx, ny, nz), lambda s: (s, 0, 0, 0))],
        out_specs=[VMEM] * 4,
        compiler_params=PARAMS,
        name="pack",
    )(density)
    za, zb = both("gz", zr, zl)
    xea, xeb = both("gx", xeu, xed)
    slabs = []
    for low, high in CHUNKS:
        slabs += [(high - low, H, inner, nz)] * 2
    slabs = run(slab_body, (density,), slabs)
    xzu, xzd = run(second_body, (za, zb), (zpack, zpack))
    xza, xzb = both("gx", xzu, xzd)
    halos = [both("gx", *slabs[2 * c : 2 * c + 2]) for c in range(len(CHUNKS))]
    wide = nx + 2 * H
    rim = [(snaps, nx, 2 * H, nz)] * 2 + [(snaps, nx + nx // 2, H, nz)] * 2
    ws, wl, yu, yd = run(
        rim_body,
        (density, xea, xeb, xza, xzd, xzu, xzb),
        rim,
        [pltpu.VMEM((wide, 2 * H, nz), F32)] * 2,
    )
    ya, yb = both("gy", yu, yd)
    acc_s, acc_l = run(
        middle_body,
        (density, xza, xzd, xzu, xzb),
        [(snaps, nx, inner, nz)] * 2,
        [pltpu.VMEM((wide, inner, nz), F32)] * 2,
    )
    out = None
    for (low, high), (xia, xib) in zip(CHUNKS, halos):
        args = (xia, xib, acc_s, acc_l, ws, wl, ya, yb, efficiency)
        out = last(low, high, args, out, block)
    return out


def solution(mesh):
    placed = (P(None, "gx", "gy", "gz"), P("gx", "gy", "gz"))
    return jax.shard_map(
        steps, mesh=mesh, in_specs=placed, out_specs=P(None, "gx", "gy", "gz"), check_vma=False
    )
```

time: 77 us -> 48.1 us (0.62)
  matrix products: 15.7 us -> 0 us
  waiting for transfers between devices: 24.9 us -> 13 us
  Pallas kernels: 0 us -> 11.7 us
  local copies, waits for them, and re-layouts: 9.29 us -> 1.42 us
  other arithmetic: 4.69 us -> 0 us
  between operations: 1.5 us -> 0.08 us
  starting transfers between devices: 20.7 us -> 21.8 us
    dot_general x6 -> x0, matrix products: 15.7 us -> none  [smooth_along(): jnp.einsum(formula, band_matrix(radius, length), volume, precision=lax.Pr...]
    ppermute x10 -> x12, waiting for transfers between devices: 24.9 us -> 13 us  [shift(): return lax.ppermute(block, axis, [(i, (i + step) % n) for i in range(n)])]
    pallas_call x0 -> x7, Pallas kernels: none -> 11.7 us  [the longest x2 5.74 us: last(): pl.pallas_call(lambda *refs: last_body(low, *refs), out_shape=jax.ShapeDt...]
    concatenate x3 -> x0, other arithmetic: 3.35 us -> none  [extended(): block = jnp.concatenate([low, block, high], axis=dim)]
    ppermute x2 -> x0, local copies, waits for them, and re-layouts: 3.04 us -> none  [the longest x1 2.56 us: extended(): lax.ppermute(lax.slice_in_dim(block, block.shape[dim] - width, None, axis...]
    slice x5 -> x0, local copies, waits for them, and re-layouts: 2.73 us -> none  [extended(): lax.slice_in_dim(block, block.shape[dim] - width, None, axis=dim)]
    min x1 -> x0, local copies, waits for them, and re-layouts: 1.62 us -> none  [on_device(): jnp.clip(0.5 + 0.25 * jnp.maximum(level_small, level_large), 0.0, 1.0)]
    reduce_sum x2 -> x0, other arithmetic: 1.35 us -> none  [band_matrix(): scale = jnp.sqrt(jnp.sum(raw_weights * raw_weights))]
  transfers between devices with their start and end apart: 10 -> 12, of which waited for: 5 -> 2; matrix products, arithmetic and copies ran while one was open for 17% -> 0% of each run, Pallas kernels for 0% -> 18%
where the time goes in v1:
time: 48.1 us; the launch traced here: 48 us
  starting transfers between devices  21.8 us (45%)
  waiting for transfers between devices  13 us (27%)
  Pallas kernels  11.7 us (24%)
  local copies, waits for them, and re-layouts  1.42 us (3%)
    ppermute x12, starting transfers between devices, shift(): return lax.ppermute(block, axis, [(i, (i + step) % n) for i in range(n)])  21.8 us
    ppermute x12, waiting for transfers between devices, shift(): return lax.ppermute(block, axis, [(i, (i + step) % n) for i in range(n)])  13 us
    pallas_call x2, Pallas kernels, last(): pl.pallas_call(lambda *refs: last_body(low, *refs), out_shape=jax.ShapeDt...  5.74 us
    pallas_call x4, Pallas kernels, run(): pl.pallas_call(body, out_shape=[pltpu.VMEM(s, F32) for s in outs], in_spe...  5.18 us
    unnamed x6, local copies, waits for them, and re-layouts  1.42 us
  transfers between devices with their start and end apart: 12, of which 2 were waited for; matrix products, arithmetic and copies ran while one was open for 0% of the time, Pallas kernels for 18%

profile of v1, /device:TPU:1, one launch (start us, length us, event | category | flops | bytes accessed | tf_op | source)
XLA Modules:
  0.0 48.0 jit_solution(13073766143143261139)
XLA Ops:
  0.0 0.0 copy-start
  0.0 1.4 %copy-done = f32[3,16,64,128]{3,2,1,0:T(8,128)S(1)} copy-done((f32[3,16,64,128]{3,2,1,0:T(8,128)S(1)}, f32[3,16,64,128]{3,2,1,0:T(8,128)}, u32[]{:S(2)}) %copy-start) | copy-done | bytes 1572888
  1.4 0.0 copy-start.1
  1.4 0.8 %pack.1 = (f32[3,64,128]{2,1,0:T(8,128)S(1)}, f32[3,64,128]{2,1,0:T(8,128)S(1)}, f32[3,8,16,128]{3,2,1,0:T(8,128)S(1)}, f32[3,8,16,128]{3,2,1,0:T(8,128)S(1)}) custom-call(f32[3,16,64,128]{3,2,1,0:T(8,128)S(1)} %copy-done), custom_call_target="tpu_custom_call" | custom-call | tf_op jit(solution)/shard_map/pack/pallas_call | solution.py:261
  2.2 2.2 %collective-permute-start.2 = (f32[3,64,128]{2,1,0:T(8,128)S(1)}, f32[3,64,128]{2,1,0:T(8,128)S(1)}, u32[]{:S(2)}, u32[]{:S(2)}) collective-permute-start(f32[3,64,128]{2,1,0:T(8,128)S(1)} %get-tuple-element.23), channel_id=1, source_target_pairs={{0,1},{1,2},{2,3},{3,4},{4,5},{5,6},{6,7},{7,0},{8,9},{9,10},{10,1... | collective-permute-start | bytes 294920 | tf_op jit(solution)/shard_map/ppermute | solution.py:248
  4.3 2.5 %collective-permute-start.3 = (f32[3,64,128]{2,1,0:T(8,128)S(1)}, f32[3,64,128]{2,1,0:T(8,128)S(1)}, u32[]{:S(2)}, u32[]{:S(2)}) collective-permute-start(f32[3,64,128]{2,1,0:T(8,128)S(1)} %get-tuple-element.24), channel_id=1, source_target_pairs={{0,7},{1,0},{2,1},{3,2},{4,3},{5,4},{6,5},{7,6},{8,15},{9,8},{10,9... | collective-permute-start | bytes 294920 | tf_op jit(solution)/shard_map/ppermute | solution.py:248
  6.8 0.1 shard_map.28
  6.9 1.7 %collective-permute-start.10 = (f32[2,8,48,128]{3,2,1,0:T(8,128)S(1)}, f32[2,8,48,128]{3,2,1,0:T(8,128)S(1)}, u32[]{:S(2)}, u32[]{:S(2)}) collective-permute-start(f32[2,8,48,128]{3,2,1,0:T(8,128)S(1)} %get-tuple-element.35), channel_id=1, source_target_pairs={{0,32},{32,64},{64,96},{96,128},{128,160},{160,192},{192,224},{224... | collective-permute-start | bytes 1179656 | tf_op jit(solution)/shard_map/ppermute | solution.py:248
  8.6 1.6 %collective-permute-start.6 = (f32[3,8,16,128]{3,2,1,0:T(8,128)S(1)}, f32[3,8,16,128]{3,2,1,0:T(8,128)S(1)}, u32[]{:S(2)}, u32[]{:S(2)}) collective-permute-start(f32[3,8,16,128]{3,2,1,0:T(8,128)S(1)} %get-tuple-element.29), channel_id=1, source_target_pairs={{0,32},{32,64},{64,96},{96,128},{128,160},{160,192},{192,224},{224... | collective-permute-start | bytes 589832 | tf_op jit(solution)/shard_map/ppermute | solution.py:248
  10.2 2.5 %collective-permute-start.7 = (f32[3,8,16,128]{3,2,1,0:T(8,128)S(1)}, f32[3,8,16,128]{3,2,1,0:T(8,128)S(1)}, u32[]{:S(2)}, u32[]{:S(2)}) collective-permute-start(f32[3,8,16,128]{3,2,1,0:T(8,128)S(1)} %get-tuple-element.30), channel_id=1, source_target_pairs={{0,224},{32,0},{64,32},{96,64},{128,96},{160,128},{192,160},{224,1... | collective-permute-start | bytes 589832 | tf_op jit(solution)/shard_map/ppermute | solution.py:248
  12.7 0.0 collective-permute-done.2.za
  12.7 0.0 collective-permute-done.3.zb
  12.7 0.1 shard_map.29
  12.8 0.1 collective-permute-start.4
  12.9 2.7 %collective-permute-start.5 = (f32[3,64,128]{2,1,0:T(8,128)S(1)}, f32[3,64,128]{2,1,0:T(8,128)S(1)}, u32[]{:S(2)}, u32[]{:S(2)}) collective-permute-start(f32[3,64,128]{2,1,0:T(8,128)S(1)} %get-tuple-element.26.xzd), channel_id=1, source_target_pairs={{0,224},{32,0},{64,32},{96,64},{128,96},{160,128},{192,160},{224,1... | collective-permute-start | bytes 294920 | tf_op jit(solution)/shard_map/ppermute | solution.py:248
  15.6 11.7 %collective-permute-done.4.xza = f32[3,64,128]{2,1,0:T(8,128)S(1)} collective-permute-done((f32[3,64,128]{2,1,0:T(8,128)S(1)}, f32[3,64,128]{2,1,0:T(8,128)S(1)}, u32[]{:S(2)}, u32[]{:S(2)}) %collective-permute-start.4) | collective-permute-done | bytes 98336 | tf_op jit(solution)/shard_map/ppermute | solution.py:248
  27.3 1.2 %collective-permute-start.11 = (f32[2,8,48,128]{3,2,1,0:T(8,128)S(1)}, f32[2,8,48,128]{3,2,1,0:T(8,128)S(1)}, u32[]{:S(2)}, u32[]{:S(2)}) collective-permute-start(f32[2,8,48,128]{3,2,1,0:T(8,128)S(1)} %get-tuple-element.36), channel_id=1, source_target_pairs={{0,224},{32,0},{64,32},{96,64},{128,96},{160,128},{192,160},{224,1... | collective-permute-start | bytes 1179656 | tf_op jit(solution)/shard_map/ppermute | solution.py:248
  28.5 0.0 collective-permute-done.5.xzb
  28.5 0.0 collective-permute-done.6.xea
  28.5 0.0 collective-permute-done.7.xeb
  28.5 0.0 copy-done.1
  28.5 1.3 %shard_map.31 = (f32[3,16,16,128]{3,2,1,0:T(8,128)S(1)}, f32[3,16,16,128]{3,2,1,0:T(8,128)S(1)}, f32[3,24,8,128]{3,2,1,0:T(8,128)S(1)}, f32[3,24,8,128]{3,2,1,0:T(8,128)S(1)}) custom-call(f32[3,16,64,128]{3,2,1,0:T(8,128)S(1)} %copy-done.1, f32[3,8,16,128]{3,2,1,0:T(8,128)S(1)} %collective-permute-done.6.xea, ...), custom_call_target="tpu_custom_call" | custom-call | tf_op jit(solution)/shard_map/pallas_call | solution.py:36
  29.8 0.0 copy-start.2
  29.8 4.7 %collective-permute-start.8 = (f32[3,24,8,128]{3,2,1,0:T(8,128)S(1)}, f32[3,24,8,128]{3,2,1,0:T(8,128)S(1)}, u32[]{:S(2)}, u32[]{:S(2)}) collective-permute-start(f32[3,24,8,128]{3,2,1,0:T(8,128)S(1)} %get-tuple-element.33), channel_id=1, source_target_pairs={{0,8},{8,16},{16,24},{24,0},{1,9},{9,17},{17,25},{25,1},{2,10},{10... | collective-permute-start | bytes 884744 | tf_op jit(solution)/shard_map/ppermute | solution.py:248
  34.6 0.0 collective-permute-start.9
  34.6 0.0 collective-permute-start
  34.6 0.0 collective-permute-done.10.refs_0_
  34.6 2.7 %collective-permute-start.1 = (f32[1,8,48,128]{3,2,1,0:T(8,128)S(1)}, f32[1,8,48,128]{3,2,1,0:T(8,128)S(1)}, u32[]{:S(2)}, u32[]{:S(2)}) collective-permute-start(f32[1,8,48,128]{3,2,1,0:T(8,128)S(1)} %get-tuple-element.22), channel_id=1, source_target_pairs={{0,224},{32,0},{64,32},{96,64},{128,96},{160,128},{192,160},{224,1... | collective-permute-start | bytes 589832 | tf_op jit(solution)/shard_map/ppermute | solution.py:248
  37.3 3.7 %shard_map.30 = (f32[3,16,48,128]{3,2,1,0:T(8,128)S(1)}, f32[3,16,48,128]{3,2,1,0:T(8,128)S(1)}) custom-call(f32[3,16,64,128]{3,2,1,0:T(8,128)S(1)} %copy-done.1, f32[3,64,128]{2,1,0:T(8,128)S(1)} %collective-permute-done.4.xza, f32[3,64,128]{2,1,0:T(8,128)S(1)} %get-tuple-element.26.xzd, f32[3,64,128]{2,1,0:T(8,128)S(1)} %get-tuple-element.25.xzu, ...), custom_call_target="tpu_custom_call" | custom-call | tf_op jit(solution)/shard_map/pallas_call | solution.py:36
  40.9 0.0 collective-permute-done.11.refs_1_
  40.9 0.0 collective-permute-done.8.refs_6_
  40.9 1.3 %collective-permute-done.9.refs_7_ = f32[3,24,8,128]{3,2,1,0:T(8,128)S(1)} collective-permute-done((f32[3,24,8,128]{3,2,1,0:T(8,128)S(1)}, f32[3,24,8,128]{3,2,1,0:T(8,128)S(1)}, u32[]{:S(2)}, u32[]{:S(2)}) %collective-permute-start.9) | collective-permute-done | bytes 294944 | tf_op jit(solution)/shard_map/ppermute | solution.py:248
  42.2 0.0 copy-done.2
  42.2 3.6 %last.2.refs_9_ = f32[3,16,64,128]{3,2,1,0:T(8,128)} custom-call(f32[2,8,48,128]{3,2,1,0:T(8,128)S(1)} %collective-permute-done.10.refs_0_, f32[2,8,48,128]{3,2,1,0:T(8,128)S(1)} %collective-permute-done.11.refs_1_, f32[3,16,48,128]{3,2,1,0:T(8,128)S(1)} %get-tuple-element.27.refs_2_, f32[3,16,48,128]{3,2,1,0:T(8,128)S(1)} %get-tuple-element.28.refs_3_, ...), custom_call_target="tpu_custom_call" | custom-call | tf_op jit(solution)/shard_map/last/pallas_call | solution.py:233
  45.8 0.0 collective-permute-done.refs_0_
  45.8 0.0 collective-permute-done.1.refs_1_
  45.8 2.2 %last.3 = f32[3,16,64,128]{3,2,1,0:T(8,128)} custom-call(f32[1,8,48,128]{3,2,1,0:T(8,128)S(1)} %collective-permute-done.refs_0_, f32[1,8,48,128]{3,2,1,0:T(8,128)S(1)} %collective-permute-done.1.refs_1_, f32[3,16,48,128]{3,2,1,0:T(8,128)S(1)} %get-tuple-element.27.refs_2_, ...), custom_call_target="tpu_custom_call", output_to_operand_aliasing={{}: (9, {})} | custom-call | tf_op jit(solution)/shard_map/last/pallas_call | solution.py:233
Async XLA Ops:
  0.0 1.4 %copy-start = (f32[3,16,64,128]{3,2,1,0:T(8,128)S(1)}, f32[3,16,64,128]{3,2,1,0:T(8,128)}, u32[]{:S(2)}) copy-start(f32[3,16,64,128]{3,2,1,0:T(8,128)} %d.7) | copy-start | bytes 4718596
  1.4 27.1 %copy-start.1 = (f32[3,16,64,128]{3,2,1,0:T(8,128)S(1)}, f32[3,16,64,128]{3,2,1,0:T(8,128)}, u32[]{:S(2)}) copy-start(f32[3,16,64,128]{3,2,1,0:T(8,128)} %d.7) | copy-start | bytes 4718596
  2.2 10.5 %collective-permute-start.2 = (f32[3,64,128]{2,1,0:T(8,128)S(1)}, f32[3,64,128]{2,1,0:T(8,128)S(1)}, u32[]{:S(2)}, u32[]{:S(2)}) collective-permute-start(f32[3,64,128]{2,1,0:T(8,128)S(1)} %get-tuple-element.23), channel_id=1, source_target_pairs={{0,1},{1,2},{2,3},{3,4},{4,5},{5,6},{6,7},{7,0},{8,9},{9,10},{10,1... | collective-permute-start | bytes 294920 | tf_op jit(solution)/shard_map/ppermute | solution.py:248
  4.3 8.4 %collective-permute-start.3 = (f32[3,64,128]{2,1,0:T(8,128)S(1)}, f32[3,64,128]{2,1,0:T(8,128)S(1)}, u32[]{:S(2)}, u32[]{:S(2)}) collective-permute-start(f32[3,64,128]{2,1,0:T(8,128)S(1)} %get-tuple-element.24), channel_id=1, source_target_pairs={{0,7},{1,0},{2,1},{3,2},{4,3},{5,4},{6,5},{7,6},{8,15},{9,8},{10,9... | collective-permute-start | bytes 294920 | tf_op jit(solution)/shard_map/ppermute | solution.py:248
  6.9 27.7 %collective-permute-start.10 = (f32[2,8,48,128]{3,2,1,0:T(8,128)S(1)}, f32[2,8,48,128]{3,2,1,0:T(8,128)S(1)}, u32[]{:S(2)}, u32[]{:S(2)}) collective-permute-start(f32[2,8,48,128]{3,2,1,0:T(8,128)S(1)} %get-tuple-element.35), channel_id=1, source_target_pairs={{0,32},{32,64},{64,96},{96,128},{128,160},{160,192},{192,224},{224... | collective-permute-start | bytes 1179656 | tf_op jit(solution)/shard_map/ppermute | solution.py:248
  8.6 19.9 %collective-permute-start.6 = (f32[3,8,16,128]{3,2,1,0:T(8,128)S(1)}, f32[3,8,16,128]{3,2,1,0:T(8,128)S(1)}, u32[]{:S(2)}, u32[]{:S(2)}) collective-permute-start(f32[3,8,16,128]{3,2,1,0:T(8,128)S(1)} %get-tuple-element.29), channel_id=1, source_target_pairs={{0,32},{32,64},{64,96},{96,128},{128,160},{160,192},{192,224},{224... | collective-permute-start | bytes 589832 | tf_op jit(solution)/shard_map/ppermute | solution.py:248
  10.2 18.2 %collective-permute-start.7 = (f32[3,8,16,128]{3,2,1,0:T(8,128)S(1)}, f32[3,8,16,128]{3,2,1,0:T(8,128)S(1)}, u32[]{:S(2)}, u32[]{:S(2)}) collective-permute-start(f32[3,8,16,128]{3,2,1,0:T(8,128)S(1)} %get-tuple-element.30), channel_id=1, source_target_pairs={{0,224},{32,0},{64,32},{96,64},{128,96},{160,128},{192,160},{224,1... | collective-permute-start | bytes 589832 | tf_op jit(solution)/shard_map/ppermute | solution.py:248
  12.8 14.4 %collective-permute-start.4 = (f32[3,64,128]{2,1,0:T(8,128)S(1)}, f32[3,64,128]{2,1,0:T(8,128)S(1)}, u32[]{:S(2)}, u32[]{:S(2)}) collective-permute-start(f32[3,64,128]{2,1,0:T(8,128)S(1)} %get-tuple-element.25.xzu), channel_id=1, source_target_pairs={{0,32},{32,64},{64,96},{96,128},{128,160},{160,192},{192,224},{224... | collective-permute-start | bytes 294920 | tf_op jit(solution)/shard_map/ppermute | solution.py:248
  12.9 15.5 %collective-permute-start.5 = (f32[3,64,128]{2,1,0:T(8,128)S(1)}, f32[3,64,128]{2,1,0:T(8,128)S(1)}, u32[]{:S(2)}, u32[]{:S(2)}) collective-permute-start(f32[3,64,128]{2,1,0:T(8,128)S(1)} %get-tuple-element.26.xzd), channel_id=1, source_target_pairs={{0,224},{32,0},{64,32},{96,64},{128,96},{160,128},{192,160},{224,1... | collective-permute-start | bytes 294920 | tf_op jit(solution)/shard_map/ppermute | solution.py:248
  27.3 13.6 %collective-permute-start.11 = (f32[2,8,48,128]{3,2,1,0:T(8,128)S(1)}, f32[2,8,48,128]{3,2,1,0:T(8,128)S(1)}, u32[]{:S(2)}, u32[]{:S(2)}) collective-permute-start(f32[2,8,48,128]{3,2,1,0:T(8,128)S(1)} %get-tuple-element.36), channel_id=1, source_target_pairs={{0,224},{32,0},{64,32},{96,64},{128,96},{160,128},{192,160},{224,1... | collective-permute-start | bytes 1179656 | tf_op jit(solution)/shard_map/ppermute | solution.py:248
  29.8 12.4 %copy-start.2 = (f32[16,64,128]{2,1,0:T(8,128)S(1)}, f32[16,64,128]{2,1,0:T(8,128)}, u32[]{:S(2)}) copy-start(f32[16,64,128]{2,1,0:T(8,128)} %refs_8_.3) | copy-start | bytes 1572868
  29.8 11.1 %collective-permute-start.8 = (f32[3,24,8,128]{3,2,1,0:T(8,128)S(1)}, f32[3,24,8,128]{3,2,1,0:T(8,128)S(1)}, u32[]{:S(2)}, u32[]{:S(2)}) collective-permute-start(f32[3,24,8,128]{3,2,1,0:T(8,128)S(1)} %get-tuple-element.33), channel_id=1, source_target_pairs={{0,8},{8,16},{16,24},{24,0},{1,9},{9,17},{17,25},{25,1},{2,10},{10... | collective-permute-start | bytes 884744 | tf_op jit(solution)/shard_map/ppermute | solution.py:248
  34.6 7.7 %collective-permute-start.9 = (f32[3,24,8,128]{3,2,1,0:T(8,128)S(1)}, f32[3,24,8,128]{3,2,1,0:T(8,128)S(1)}, u32[]{:S(2)}, u32[]{:S(2)}) collective-permute-start(f32[3,24,8,128]{3,2,1,0:T(8,128)S(1)} %get-tuple-element.34), channel_id=1, source_target_pairs={{0,24},{8,0},{16,8},{24,16},{1,25},{9,1},{17,9},{25,17},{2,26},{10... | collective-permute-start | bytes 884744 | tf_op jit(solution)/shard_map/ppermute | solution.py:248
  34.6 11.2 %collective-permute-start = (f32[1,8,48,128]{3,2,1,0:T(8,128)S(1)}, f32[1,8,48,128]{3,2,1,0:T(8,128)S(1)}, u32[]{:S(2)}, u32[]{:S(2)}) collective-permute-start(f32[1,8,48,128]{3,2,1,0:T(8,128)S(1)} %get-tuple-element.21), channel_id=1, source_target_pairs={{0,32},{32,64},{64,96},{96,128},{128,160},{160,192},{192,224},{224... | collective-permute-start | bytes 589832 | tf_op jit(solution)/shard_map/ppermute | solution.py:248
  34.6 11.2 %collective-permute-start.1 = (f32[1,8,48,128]{3,2,1,0:T(8,128)S(1)}, f32[1,8,48,128]{3,2,1,0:T(8,128)S(1)}, u32[]{:S(2)}, u32[]{:S(2)}) collective-permute-start(f32[1,8,48,128]{3,2,1,0:T(8,128)S(1)} %get-tuple-element.22), channel_id=1, source_target_pairs={{0,224},{32,0},{64,32},{96,64},{128,96},{160,128},{192,160},{224,1... | collective-permute-start | bytes 589832 | tf_op jit(solution)/shard_map/ppermute | solution.py:248

commit v2 on v1

v2 whole, which is shorter than its diff:
```python
import math

import jax
import jax.numpy as jnp
from jax import lax
from jax.experimental import pallas as pl
from jax.experimental.pallas import tpu as pltpu
from jax.sharding import PartitionSpec as P


R_SMALL = 4
R_LARGE = 8
H = R_LARGE
CHUNKS = ((0, 2), (2, 3))
VMEM = pl.BlockSpec(memory_space=pltpu.VMEM)
F32 = jnp.float32
BF16 = jnp.bfloat16
PARAMS = pltpu.CompilerParams(vmem_limit_bytes=24 * 2**20)


def weight(radius, k):
    return float((radius + 1) ** 2 - k * k)


def scale_of(radius):
    n = float((radius + 1) ** 2)
    total = sum((1.0 - k * k / n) ** 2 for k in range(-radius, radius + 1))
    return (1.0 / (n * math.sqrt(total))) ** 3


def near(x):
    return pltpu.with_memory_space_constraint(x, pltpu.VMEM)


def run(body, args, outs, scratch=()):
    return pl.pallas_call(
        body,
        out_shape=[pltpu.VMEM(s, F32) for s in outs],
        in_specs=[VMEM] * len(args),
        out_specs=[VMEM] * len(outs),
        scratch_shapes=list(scratch),
        compiler_params=PARAMS,
    )(*[near(a) for a in args])


def band(edge):
    shape = (256, 256)
    row = lax.broadcasted_iota(jnp.int32, shape, 0) % 128
    col = lax.broadcasted_iota(jnp.int32, shape, 1)
    z = col % 128
    if edge:
        at = jnp.where(row < 64, row - H, 128 + row - 64)
        used = row % 64 < H
        d = at - z
    else:
        d = row - z
    reach = jnp.where(col < 128, R_SMALL + 1, R_LARGE + 1)
    value = reach * reach - d * d
    keep = value > 0
    if edge:
        keep = keep & used
    return jnp.where(keep, value, 0).astype(F32).astype(BF16)


def mul(m, w):
    hi = m.astype(BF16)
    lo = (m - hi.astype(F32)).astype(BF16)
    return jnp.dot(jnp.concatenate([hi, lo], axis=1), w, preferred_element_type=F32)


def lanes(shape):
    return lax.broadcasted_iota(jnp.int32, shape, len(shape) - 1)


def edge_of(pack, p):
    return pltpu.roll(pack, (128 - H * p) % 128, 1) if p else pack


def taps(get, radius):
    total = weight(radius, 0) * get(0)
    for k in range(1, radius + 1):
        total = total + weight(radius, k) * (get(k) + get(-k))
    return total


def rows_band(radius, ny):
    wide = ny + 2 * H
    y = lax.broadcasted_iota(jnp.int32, (ny, 2 * wide), 0)
    c = lax.broadcasted_iota(jnp.int32, (ny, 2 * wide), 1)
    d = jnp.where(c < wide, c, c - wide) - H - y
    value = (radius + 1) ** 2 - d * d
    return jnp.where(value > 0, value, 0).astype(F32).astype(BF16)


def stack(m):
    hi = m.astype(BF16)
    lo = (m - hi.astype(F32)).astype(BF16)
    return jnp.concatenate([hi, lo], axis=0)


def x_halo(total, before, after, i, n, radius):
    for a in range(radius):
        d = i + radius - a
        if d <= radius:
            total = total + weight(radius, d) * before[a]
    for b in range(radius):
        d = n + b - i
        if d <= radius:
            total = total + weight(radius, d) * after[b]
    return total


def pack_body(d_hbm, zr, zl, xeu, xed, d_all, sems):
    snaps, nx, ny, nz = d_all.shape
    copies = [
        pltpu.make_async_copy(d_hbm.at[s], d_all.at[s], sems.at[s]) for s in range(snaps)
    ]
    for copy in copies:
        copy.start()
    lane = lanes((ny, nz))
    for s in range(snaps):
        copies[s].wait()
        d = d_all.at[s]
        xeu[s, :, 0:H] = d[nx - H :, 0:H]
        xeu[s, :, H:] = d[nx - H :, ny - H :]
        xed[s, :, 0:H] = d[0:H, 0:H]
        xed[s, :, H:] = d[0:H, ny - H :]
        right = jnp.zeros((ny, nz), F32)
        left = jnp.zeros((ny, nz), F32)
        for x in range(nx):
            r = pltpu.roll(d[x], (H * x + H) % nz, 1)
            right = jnp.where((lane >= H * x) & (lane < H * x + H), r, right)
            at = (H * x + H) % nz
            left = jnp.where((lane >= at) & (lane < at + H), r, left)
        zr[s] = right
        zl[s] = pltpu.roll(left, nz - H, 1)


def second_body(za, zb, xzu, xzd):
    snaps, ny, nz = za.shape
    half = nz // 2
    lane = lanes((ny, nz))
    for s in range(snaps):
        xzu[s] = jnp.where(lane < half, pltpu.roll(za[s], half, 1), zb[s])
        xzd[s] = jnp.where(lane < half, za[s], pltpu.roll(zb[s], half, 1))


def slab_body(d, *outs):
    nx, ny = d.shape[1:3]
    for (low, high), up, down in zip(CHUNKS, outs[0::2], outs[1::2]):
        up[...] = d[low:high, nx - H :, H : ny - H]
        down[...] = d[low:high, 0:H, H : ny - H]


def put(ref, s, i, r, value):
    ref[s, i, r : r + 8] = value


def x_sums(planes, store, radius):
    n = planes.shape[0] - 2 * H
    v = [planes[j] for j in range(n + 2 * H)]
    for i in range(n):
        store(i, taps(lambda k: v[H + i + k], radius))


def rim_body(d, xea, xeb, xza, xzd, xzu, xzb, ws, wl, yu, yd):
    snaps, nx, ny, nz = d.shape
    wm, we = band(False), band(True)

    def ends(v):
        return jnp.concatenate([v[0:H], v[ny - H :]], axis=0)

    for s in range(snaps):
        packs = [ends(p[s]) for p in (xza, xzd, xzu, xzb)]
        main = [xea[s, p] for p in range(H)]
        main += [ends(d[s, x]) for x in range(nx)]
        main += [xeb[s, p] for p in range(H)]
        side = [edge_of(packs[p // H], p % H) for p in range(nx + 2 * H)]
        out = mul(jnp.concatenate(main, axis=0), wm) + mul(jnp.concatenate(side, axis=0), we)
        out = out.reshape(nx + 2 * H, 2 * H, 2 * nz)
        for r in (0, H):
            x_sums(out[:, r : r + 8, :nz], lambda i, v: put(ws, s, i, r, v), R_SMALL)
            x_sums(out[:, r : r + 8, nz:], lambda i, v: put(wl, s, i, r, v), R_LARGE)
        small, large = ws[s], wl[s]
        yu[s, 0:nx] = large[:, H:]
        yd[s, 0:nx] = large[:, 0:H]
        half = nx // 2
        yu[s, nx:, 0:R_SMALL] = small[0:half, 2 * H - R_SMALL :]
        yu[s, nx:, R_SMALL:] = small[half:, 2 * H - R_SMALL :]
        yd[s, nx:, 0:R_SMALL] = small[0:half, 0:R_SMALL]
        yd[s, nx:, R_SMALL:] = small[half:, 0:R_SMALL]


def middle_body(d, xza, xzd, xzu, xzb, acc_s, acc_l, zs_all, zl_all):
    snaps, nx, ny, nz = d.shape
    wm, we = band(False), band(True)
    inner = ny - 2 * H

    for s in range(snaps):
        zs, zl = zs_all.at[s], zl_all.at[s]
        side = [edge_of(p[s, H : ny - H], k) for p in (xza, xzd, xzu, xzb) for k in range(H)]
        edge = mul(jnp.concatenate(side, axis=0), we).reshape(nx + 2 * H, inner, 2 * nz)
        main = mul(d[s, :, H : ny - H].reshape(nx * inner, nz), wm).reshape(nx, inner, 2 * nz)
        for ref, cut in ((zs, slice(0, nz)), (zl, slice(nz, 2 * nz))):
            ref[0:H] = edge[0:H, :, cut]
            ref[H : H + nx] = edge[H : H + nx, :, cut] + main[:, :, cut]
            ref[H + nx :] = edge[H + nx :, :, cut]
        for r in range(0, inner, 8):
            x_sums(zs[:, r : r + 8], lambda i, v: put(acc_s, s, i, r, v), R_SMALL)
            x_sums(zl[:, r : r + 8], lambda i, v: put(acc_l, s, i, r, v), R_LARGE)


def fill_body(low, xia, xib, acc_s, acc_l, us, ul):
    n, _, _, _ = us.shape
    wm = band(False)
    for j in range(n):
        add_planes(xia[j], xib[j], acc_s.at[low + j], acc_l.at[low + j], us.at[j], ul.at[j], 0, wm)


def add_planes(xia, xib, acc_s, acc_l, us, ul, first, wm):
    nx, inner, nz = acc_s.shape
    cut = H - R_SMALL
    za = mul(xia.reshape(H * inner, nz), wm).reshape(H, inner, 2 * nz)
    zb = mul(xib.reshape(H * inner, nz), wm).reshape(H, inner, 2 * nz)
    for r in range(0, inner, 8):
        a, b = za[:, r : r + 8], zb[:, r : r + 8]
        at = slice(first + r, first + r + 8)
        for i in range(nx):
            us[i, at] = x_halo(
                acc_s[i, r : r + 8], a[cut:, :, :nz], b[:, :, :nz], i, nx, R_SMALL
            )
            ul[i, at] = x_halo(acc_l[i, r : r + 8], a[:, :, nz:], b[:, :, nz:], i, nx, R_LARGE)


def last_body(low, fused, *refs):
    if fused:
        xia, xib = refs[:2]
        refs = refs[2:]
    u_s, u_l, ws, wl, ya, yb, eff, *rest = refs
    out, us, ul = rest[-3:]
    j = pl.program_id(0)
    s = j + low
    nx, inner, nz = u_s.shape[1:]
    ny = inner + 2 * H
    half = nx // 2
    if fused:
        add_planes(xia[j], xib[j], u_s.at[s], u_l.at[s], us, ul, 2 * H, band(False))
    else:
        us[:, 2 * H : ny] = u_s[j]
        ul[:, 2 * H : ny] = u_l[j]
    ul[:, 0:H] = ya[s, 0:nx]
    ul[:, H : 2 * H] = wl[s, :, 0:H]
    ul[:, ny : ny + H] = wl[s, :, H:]
    ul[:, ny + H :] = yb[s, 0:nx]
    us[:, 0:H] = jnp.zeros((nx, H, nz), F32)
    us[:, ny + H :] = jnp.zeros((nx, H, nz), F32)
    us[0:half, H - R_SMALL : H] = ya[s, nx:, 0:R_SMALL]
    us[half:, H - R_SMALL : H] = ya[s, nx:, R_SMALL:]
    us[:, H : 2 * H] = ws[s, :, 0:H]
    us[:, ny : ny + H] = ws[s, :, H:]
    us[0:half, ny + H : ny + H + R_SMALL] = yb[s, nx:, 0:R_SMALL]
    us[half:, ny + H : ny + H + R_SMALL] = yb[s, nx:, R_SMALL:]
    band_s, band_l = rows_band(R_SMALL, ny), rows_band(R_LARGE, ny)
    scale_s, scale_l = 0.25 * scale_of(R_SMALL), 0.25 * scale_of(R_LARGE)

    def y_sum(ref, w, i):
        pair = jnp.concatenate([stack(ref[i]), stack(ref[i + half])], axis=1)
        return jnp.dot(w, pair, preferred_element_type=F32)

    for i in range(half):
        small, large = y_sum(us, band_s, i), y_sum(ul, band_l, i)
        for at, col in ((i, slice(0, nz)), (i + half, slice(nz, 2 * nz))):
            e = eff[at]
            low_r = e * (small[:, col] * scale_s) + (0.5 - 0.25 * 0.3)
            high_r = e * (large[:, col] * scale_l) + (0.5 - 0.25 * 0.1)
            out[0, at] = jnp.minimum(jnp.maximum(jnp.maximum(low_r, high_r), 0.0), 1.0)


def last(low, high, fused, args, before, shape):
    nx, ny, nz = shape[1:]
    extra = [] if before is None else [before]
    return pl.pallas_call(
        lambda *refs: last_body(low, fused, *refs),
        out_shape=jax.ShapeDtypeStruct(shape, F32),
        grid=(high - low,),
        in_specs=[VMEM] * len(args) + [pl.BlockSpec(memory_space=pl.ANY)] * len(extra),
        out_specs=pl.BlockSpec((1, nx, ny, nz), lambda j: (j + low, 0, 0, 0)),
        scratch_shapes=[pltpu.VMEM((nx, ny + 2 * H, nz), F32)] * 2,
        input_output_aliases={len(args): 0} if extra else {},
        compiler_params=PARAMS,
        name="last",
    )(*[near(a) for a in args], *extra)


def shift(block, axis, step):
    n = lax.axis_size(axis)
    return lax.ppermute(block, axis, [(i, (i + step) % n) for i in range(n)])


def both(axis, up, down):
    return shift(up, axis, 1), shift(down, axis, -1)


def steps(density, efficiency):
    block = density.shape
    snaps, nx, ny, nz = block
    inner = ny - 2 * H
    zpack = (snaps, ny, nz)
    xe = (snaps, H, 2 * H, nz)
    zr, zl, xeu, xed = pl.pallas_call(
        pack_body,
        out_shape=[pltpu.VMEM(s, F32) for s in (zpack, zpack, xe, xe)],
        in_specs=[pl.BlockSpec(memory_space=pl.ANY)],
        out_specs=[VMEM] * 4,
        scratch_shapes=[pltpu.VMEM(block, F32), pltpu.SemaphoreType.DMA((snaps,))],
        compiler_params=PARAMS,
        name="pack",
    )(pltpu.with_memory_space_constraint(density, pltpu.HBM))
    za, zb = both("gz", zr, zl)
    xea, xeb = both("gx", xeu, xed)
    slabs = []
    for low, high in CHUNKS:
        slabs += [(high - low, H, inner, nz)] * 2
    slabs = run(slab_body, (density,), slabs)
    xzu, xzd = run(second_body, (za, zb), (zpack, zpack))
    xza, xzb = both("gx", xzu, xzd)
    halos = [both("gx", *slabs[2 * c : 2 * c + 2]) for c in range(len(CHUNKS))]
    wide = nx + 2 * H
    rim = [(snaps, nx, 2 * H, nz)] * 2 + [(snaps, nx + nx // 2, H, nz)] * 2
    ws, wl, yu, yd = run(rim_body, (density, xea, xeb, xza, xzd, xzu, xzb), rim)
    ya, yb = both("gy", yu, yd)
    acc_s, acc_l = run(
        middle_body,
        (density, xza, xzd, xzu, xzb),
        [(snaps, nx, inner, nz)] * 2,
        [pltpu.VMEM((snaps, wide, inner, nz), F32)] * 2,
    )
    out = None
    for c, ((low, high), (xia, xib)) in enumerate(zip(CHUNKS, halos)):
        rest = (ws, wl, ya, yb, efficiency)
        if c == len(CHUNKS) - 1:
            out = last(low, high, True, (xia, xib, acc_s, acc_l) + rest, out, block)
        else:
            part = [(high - low, nx, inner, nz)] * 2
            filled = run(lambda *refs: fill_body(low, *refs), (xia, xib, acc_s, acc_l), part)
            out = last(low, high, False, tuple(filled) + rest, out, block)
    return out


def solution(mesh):
    placed = (P(None, "gx", "gy", "gz"), P("gx", "gy", "gz"))
    return jax.shard_map(
        steps, mesh=mesh, in_specs=placed, out_specs=P(None, "gx", "gy", "gz"), check_vma=False
    )
```

time: 48.1 us -> 45 us (0.936)
  Pallas kernels: 11.7 us -> 9.27 us
  local copies, waits for them, and re-layouts: 1.42 us -> 0.01 us
  starting transfers between devices: 21.8 us -> 22.5 us
    pallas_call x2, Pallas kernels: 5.74 us -> 3.13 us  [last(): pl.pallas_call(lambda *refs: last_body(low, fused, *refs), out_shape=jax....]
    unnamed x6 -> x4, local copies, waits for them, and re-layouts: 1.42 us -> 0.01 us
    pallas_call x1, Pallas kernels: 0.78 us -> 2 us  [steps(): pl.pallas_call(pack_body, out_shape=[pltpu.VMEM(s, F32) for s in (zpack,...]
    pallas_call x4 -> x5, Pallas kernels: 5.18 us -> 4.14 us  [run(): pl.pallas_call(body, out_shape=[pltpu.VMEM(s, F32) for s in outs], in_spe...]
    ppermute x12, starting transfers between devices: 21.8 us -> 22.5 us  [shift(): return lax.ppermute(block, axis, [(i, (i + step) % n) for i in range(n)])]
  transfers between devices with their start and end apart: 12 -> 12, of which waited for: 2 -> 3; matrix products, arithmetic and copies ran while one was open for 0% -> 0% of each run, Pallas kernels for 18% -> 13%
where the time goes in v2:
time: 45 us; the launch traced here: 44.9 us
  starting transfers between devices  22.5 us (50%)
  waiting for transfers between devices  13 us (29%)
  Pallas kernels  9.27 us (21%)
    ppermute x12, starting transfers between devices, shift(): return lax.ppermute(block, axis, [(i, (i + step) % n) for i in range(n)])  22.5 us
    ppermute x12, waiting for transfers between devices, shift(): return lax.ppermute(block, axis, [(i, (i + step) % n) for i in range(n)])  13 us
    pallas_call x5, Pallas kernels, run(): pl.pallas_call(body, out_shape=[pltpu.VMEM(s, F32) for s in outs], in_spe...  4.14 us
    pallas_call x2, Pallas kernels, last(): pl.pallas_call(lambda *refs: last_body(low, fused, *refs), out_shape=jax....  3.13 us
    pallas_call x1, Pallas kernels, steps(): pl.pallas_call(pack_body, out_shape=[pltpu.VMEM(s, F32) for s in (zpack,...  2 us
  transfers between devices with their start and end apart: 12, of which 3 were waited for; matrix products, arithmetic and copies ran while one was open for 0% of the time, Pallas kernels for 13%

profile of v2, /device:TPU:1, one launch (start us, length us, event | category | flops | bytes accessed | tf_op | source)
XLA Modules:
  0.0 44.9 jit_solution(5578336919672414498)
XLA Ops:
  0.0 0.0 copy-start
  0.0 2.0 %pack.1 = (f32[3,64,128]{2,1,0:T(8,128)S(1)}, f32[3,64,128]{2,1,0:T(8,128)S(1)}, f32[3,8,16,128]{3,2,1,0:T(8,128)S(1)}, f32[3,8,16,128]{3,2,1,0:T(8,128)S(1)}) custom-call(f32[3,16,64,128]{3,2,1,0:T(8,128)} %d.5), custom_call_target="tpu_custom_call" | custom-call | tf_op jit(solution)/shard_map/pack/pallas_call | solution.py:310
  2.0 2.2 %collective-permute-start.2 = (f32[3,64,128]{2,1,0:T(8,128)S(1)}, f32[3,64,128]{2,1,0:T(8,128)S(1)}, u32[]{:S(2)}, u32[]{:S(2)}) collective-permute-start(f32[3,64,128]{2,1,0:T(8,128)S(1)} %get-tuple-element.25), channel_id=1, source_target_pairs={{0,1},{1,2},{2,3},{3,4},{4,5},{5,6},{6,7},{7,0},{8,9},{9,10},{10,1... | collective-permute-start | bytes 294920 | tf_op jit(solution)/shard_map/ppermute | solution.py:297
  4.2 2.5 %collective-permute-start.3 = (f32[3,64,128]{2,1,0:T(8,128)S(1)}, f32[3,64,128]{2,1,0:T(8,128)S(1)}, u32[]{:S(2)}, u32[]{:S(2)}) collective-permute-start(f32[3,64,128]{2,1,0:T(8,128)S(1)} %get-tuple-element.26), channel_id=1, source_target_pairs={{0,7},{1,0},{2,1},{3,2},{4,3},{5,4},{6,5},{7,6},{8,15},{9,8},{10,9... | collective-permute-start | bytes 294920 | tf_op jit(solution)/shard_map/ppermute | solution.py:297
  6.7 0.0 copy-done
  6.7 0.1 shard_map.28
  6.7 1.7 %collective-permute-start.10 = (f32[2,8,48,128]{3,2,1,0:T(8,128)S(1)}, f32[2,8,48,128]{3,2,1,0:T(8,128)S(1)}, u32[]{:S(2)}, u32[]{:S(2)}) collective-permute-start(f32[2,8,48,128]{3,2,1,0:T(8,128)S(1)} %get-tuple-element.37), channel_id=1, source_target_pairs={{0,32},{32,64},{64,96},{96,128},{128,160},{160,192},{192,224},{224... | collective-permute-start | bytes 1179656 | tf_op jit(solution)/shard_map/ppermute | solution.py:297
  8.5 1.6 %collective-permute-start.6 = (f32[3,8,16,128]{3,2,1,0:T(8,128)S(1)}, f32[3,8,16,128]{3,2,1,0:T(8,128)S(1)}, u32[]{:S(2)}, u32[]{:S(2)}) collective-permute-start(f32[3,8,16,128]{3,2,1,0:T(8,128)S(1)} %get-tuple-element.31), channel_id=1, source_target_pairs={{0,32},{32,64},{64,96},{96,128},{128,160},{160,192},{192,224},{224... | collective-permute-start | bytes 589832 | tf_op jit(solution)/shard_map/ppermute | solution.py:297
  10.1 0.0 collective-permute-done.2.za
  10.1 0.0 collective-permute-done.3.zb
  10.1 0.1 shard_map.29
  10.2 1.7 %collective-permute-start.4 = (f32[3,64,128]{2,1,0:T(8,128)S(1)}, f32[3,64,128]{2,1,0:T(8,128)S(1)}, u32[]{:S(2)}, u32[]{:S(2)}) collective-permute-start(f32[3,64,128]{2,1,0:T(8,128)S(1)} %get-tuple-element.27.xzu), channel_id=1, source_target_pairs={{0,32},{32,64},{64,96},{96,128},{128,160},{160,192},{192,224},{224... | collective-permute-start | bytes 294920 | tf_op jit(solution)/shard_map/ppermute | solution.py:297
  11.9 2.8 %collective-permute-start.7 = (f32[3,8,16,128]{3,2,1,0:T(8,128)S(1)}, f32[3,8,16,128]{3,2,1,0:T(8,128)S(1)}, u32[]{:S(2)}, u32[]{:S(2)}) collective-permute-start(f32[3,8,16,128]{3,2,1,0:T(8,128)S(1)} %get-tuple-element.32), channel_id=1, source_target_pairs={{0,224},{32,0},{64,32},{96,64},{128,96},{160,128},{192,160},{224,1... | collective-permute-start | bytes 589832 | tf_op jit(solution)/shard_map/ppermute | solution.py:297
  14.7 1.4 %collective-permute-start.5 = (f32[3,64,128]{2,1,0:T(8,128)S(1)}, f32[3,64,128]{2,1,0:T(8,128)S(1)}, u32[]{:S(2)}, u32[]{:S(2)}) collective-permute-start(f32[3,64,128]{2,1,0:T(8,128)S(1)} %get-tuple-element.28.xzd), channel_id=1, source_target_pairs={{0,224},{32,0},{64,32},{96,64},{128,96},{160,128},{192,160},{224,1... | collective-permute-start | bytes 294920 | tf_op jit(solution)/shard_map/ppermute | solution.py:297
  16.1 11.0 %collective-permute-done.4.xza = f32[3,64,128]{2,1,0:T(8,128)S(1)} collective-permute-done((f32[3,64,128]{2,1,0:T(8,128)S(1)}, f32[3,64,128]{2,1,0:T(8,128)S(1)}, u32[]{:S(2)}, u32[]{:S(2)}) %collective-permute-start.4) | collective-permute-done | bytes 98336 | tf_op jit(solution)/shard_map/ppermute | solution.py:297
  27.1 1.2 %collective-permute-start.11 = (f32[2,8,48,128]{3,2,1,0:T(8,128)S(1)}, f32[2,8,48,128]{3,2,1,0:T(8,128)S(1)}, u32[]{:S(2)}, u32[]{:S(2)}) collective-permute-start(f32[2,8,48,128]{3,2,1,0:T(8,128)S(1)} %get-tuple-element.38), channel_id=1, source_target_pairs={{0,224},{32,0},{64,32},{96,64},{128,96},{160,128},{192,160},{224,1... | collective-permute-start | bytes 1179656 | tf_op jit(solution)/shard_map/ppermute | solution.py:297
  28.3 0.0 collective-permute-done.5.xzb
  28.3 0.0 collective-permute-done.6.xea
  28.3 0.0 collective-permute-done.7.xeb
  28.3 1.0 %shard_map.31 = (f32[3,16,16,128]{3,2,1,0:T(8,128)S(1)}, f32[3,16,16,128]{3,2,1,0:T(8,128)S(1)}, f32[3,24,8,128]{3,2,1,0:T(8,128)S(1)}, f32[3,24,8,128]{3,2,1,0:T(8,128)S(1)}) custom-call(f32[3,16,64,128]{3,2,1,0:T(8,128)S(1)} %copy-done, f32[3,8,16,128]{3,2,1,0:T(8,128)S(1)} %collective-permute-done.6.xea, ...), custom_call_target="tpu_custom_call" | custom-call | tf_op jit(solution)/shard_map/pallas_call | solution.py:36
  29.3 4.7 %collective-permute-start.8 = (f32[3,24,8,128]{3,2,1,0:T(8,128)S(1)}, f32[3,24,8,128]{3,2,1,0:T(8,128)S(1)}, u32[]{:S(2)}, u32[]{:S(2)}) collective-permute-start(f32[3,24,8,128]{3,2,1,0:T(8,128)S(1)} %get-tuple-element.35), channel_id=1, source_target_pairs={{0,8},{8,16},{16,24},{24,0},{1,9},{9,17},{17,25},{25,1},{2,10},{10... | collective-permute-start | bytes 884744 | tf_op jit(solution)/shard_map/ppermute | solution.py:297
  34.0 0.0 collective-permute-start.9
  34.0 0.0 collective-permute-start
  34.1 0.0 collective-permute-done.10.refs_0_
  34.1 2.7 %collective-permute-start.1 = (f32[1,8,48,128]{3,2,1,0:T(8,128)S(1)}, f32[1,8,48,128]{3,2,1,0:T(8,128)S(1)}, u32[]{:S(2)}, u32[]{:S(2)}) collective-permute-start(f32[1,8,48,128]{3,2,1,0:T(8,128)S(1)} %get-tuple-element.24), channel_id=1, source_target_pairs={{0,224},{32,0},{64,32},{96,64},{128,96},{160,128},{192,160},{224,1... | collective-permute-start | bytes 589832 | tf_op jit(solution)/shard_map/ppermute | solution.py:297
  36.7 2.4 %shard_map.30 = (f32[3,16,48,128]{3,2,1,0:T(8,128)S(1)}, f32[3,16,48,128]{3,2,1,0:T(8,128)S(1)}) custom-call(f32[3,16,64,128]{3,2,1,0:T(8,128)S(1)} %copy-done, f32[3,64,128]{2,1,0:T(8,128)S(1)} %collective-permute-done.4.xza, f32[3,64,128]{2,1,0:T(8,128)S(1)} %get-tuple-element.28.xzd, f32[3,64,128]{2,1,0:T(8,128)S(1)} %get-tuple-element.27.xzu, ...), custom_call_target="tpu_custom_call" | custom-call | tf_op jit(solution)/shard_map/pallas_call | solution.py:36
  39.2 0.0 collective-permute-done.11.refs_1_
  39.2 0.0 copy-start.1
  39.2 0.6 %shard_map.32 = (f32[2,16,48,128]{3,2,1,0:T(8,128)S(1)}, f32[2,16,48,128]{3,2,1,0:T(8,128)S(1)}) custom-call(f32[2,8,48,128]{3,2,1,0:T(8,128)S(1)} %collective-permute-done.10.refs_0_, f32[2,8,48,128]{3,2,1,0:T(8,128)S(1)} %collective-permute-done.11.refs_1_, f32[3,16,48,128]{3,2,1,0:T(8,128)S(1)} %get-tuple-element.29.refs_2_, ...), custom_call_target="tpu_custom_call" | custom-call | tf_op jit(solution)/shard_map/pallas_call | solution.py:36
  39.7 0.1 collective-permute-done.8.refs_4_.refs_6_
  39.9 1.8 %collective-permute-done.9.refs_5_.refs_7_ = f32[3,24,8,128]{3,2,1,0:T(8,128)S(1)} collective-permute-done((f32[3,24,8,128]{3,2,1,0:T(8,128)S(1)}, f32[3,24,8,128]{3,2,1,0:T(8,128)S(1)}, u32[]{:S(2)}, u32[]{:S(2)}) %collective-permute-start.9) | collective-permute-done | bytes 294944 | tf_op jit(solution)/shard_map/ppermute | solution.py:297
  41.7 0.0 copy-done.1
  41.7 1.6 %last.2.refs_9_ = f32[3,16,64,128]{3,2,1,0:T(8,128)} custom-call(f32[2,16,48,128]{3,2,1,0:T(8,128)S(1)} %get-tuple-element.39.refs_0_, f32[2,16,48,128]{3,2,1,0:T(8,128)S(1)} %get-tuple-element.40.refs_1_, f32[3,16,16,128]{3,2,1,0:T(8,128)S(1)} %get-tuple-element.33.refs_2_.refs_4_, f32[3,16,16,128]{3,2,1,0:T(8,128)S(1)} %get-tuple-element.34.refs_3_.refs_5_, ...), custom_call_target="tpu_custom_call" | custom-call | tf_op jit(solution)/shard_map/last/pallas_call | solution.py:282
  43.3 0.0 collective-permute-done.refs_0_
  43.3 0.0 collective-permute-done.1.refs_1_
  43.3 1.5 %last.3 = f32[3,16,64,128]{3,2,1,0:T(8,128)} custom-call(f32[1,8,48,128]{3,2,1,0:T(8,128)S(1)} %collective-permute-done.refs_0_, f32[1,8,48,128]{3,2,1,0:T(8,128)S(1)} %collective-permute-done.1.refs_1_, f32[3,16,48,128]{3,2,1,0:T(8,128)S(1)} %get-tuple-element.29.refs_2_, ...), custom_call_target="tpu_custom_call", output_to_operand_aliasing={{}: (9, {})} | custom-call | tf_op jit(solution)/shard_map/last/pallas_call | solution.py:282
Async XLA Ops:
  0.0 6.7 %copy-start = (f32[3,16,64,128]{3,2,1,0:T(8,128)S(1)}, f32[3,16,64,128]{3,2,1,0:T(8,128)}, u32[]{:S(2)}) copy-start(f32[3,16,64,128]{3,2,1,0:T(8,128)} %d.5) | copy-start | bytes 4718596
  2.0 8.1 %collective-permute-start.2 = (f32[3,64,128]{2,1,0:T(8,128)S(1)}, f32[3,64,128]{2,1,0:T(8,128)S(1)}, u32[]{:S(2)}, u32[]{:S(2)}) collective-permute-start(f32[3,64,128]{2,1,0:T(8,128)S(1)} %get-tuple-element.25), channel_id=1, source_target_pairs={{0,1},{1,2},{2,3},{3,4},{4,5},{5,6},{6,7},{7,0},{8,9},{9,10},{10,1... | collective-permute-start | bytes 294920 | tf_op jit(solution)/shard_map/ppermute | solution.py:297
  4.2 5.9 %collective-permute-start.3 = (f32[3,64,128]{2,1,0:T(8,128)S(1)}, f32[3,64,128]{2,1,0:T(8,128)S(1)}, u32[]{:S(2)}, u32[]{:S(2)}) collective-permute-start(f32[3,64,128]{2,1,0:T(8,128)S(1)} %get-tuple-element.26), channel_id=1, source_target_pairs={{0,7},{1,0},{2,1},{3,2},{4,3},{5,4},{6,5},{7,6},{8,15},{9,8},{10,9... | collective-permute-start | bytes 294920 | tf_op jit(solution)/shard_map/ppermute | solution.py:297
  6.7 27.3 %collective-permute-start.10 = (f32[2,8,48,128]{3,2,1,0:T(8,128)S(1)}, f32[2,8,48,128]{3,2,1,0:T(8,128)S(1)}, u32[]{:S(2)}, u32[]{:S(2)}) collective-permute-start(f32[2,8,48,128]{3,2,1,0:T(8,128)S(1)} %get-tuple-element.37), channel_id=1, source_target_pairs={{0,32},{32,64},{64,96},{96,128},{128,160},{160,192},{192,224},{224... | collective-permute-start | bytes 1179656 | tf_op jit(solution)/shard_map/ppermute | solution.py:297
  8.5 19.9 %collective-permute-start.6 = (f32[3,8,16,128]{3,2,1,0:T(8,128)S(1)}, f32[3,8,16,128]{3,2,1,0:T(8,128)S(1)}, u32[]{:S(2)}, u32[]{:S(2)}) collective-permute-start(f32[3,8,16,128]{3,2,1,0:T(8,128)S(1)} %get-tuple-element.31), channel_id=1, source_target_pairs={{0,32},{32,64},{64,96},{96,128},{128,160},{160,192},{192,224},{224... | collective-permute-start | bytes 589832 | tf_op jit(solution)/shard_map/ppermute | solution.py:297
  10.2 16.9 %collective-permute-start.4 = (f32[3,64,128]{2,1,0:T(8,128)S(1)}, f32[3,64,128]{2,1,0:T(8,128)S(1)}, u32[]{:S(2)}, u32[]{:S(2)}) collective-permute-start(f32[3,64,128]{2,1,0:T(8,128)S(1)} %get-tuple-element.27.xzu), channel_id=1, source_target_pairs={{0,32},{32,64},{64,96},{96,128},{128,160},{160,192},{192,224},{224... | collective-permute-start | bytes 294920 | tf_op jit(solution)/shard_map/ppermute | solution.py:297
  11.9 16.4 %collective-permute-start.7 = (f32[3,8,16,128]{3,2,1,0:T(8,128)S(1)}, f32[3,8,16,128]{3,2,1,0:T(8,128)S(1)}, u32[]{:S(2)}, u32[]{:S(2)}) collective-permute-start(f32[3,8,16,128]{3,2,1,0:T(8,128)S(1)} %get-tuple-element.32), channel_id=1, source_target_pairs={{0,224},{32,0},{64,32},{96,64},{128,96},{160,128},{192,160},{224,1... | collective-permute-start | bytes 589832 | tf_op jit(solution)/shard_map/ppermute | solution.py:297
  14.7 13.6 %collective-permute-start.5 = (f32[3,64,128]{2,1,0:T(8,128)S(1)}, f32[3,64,128]{2,1,0:T(8,128)S(1)}, u32[]{:S(2)}, u32[]{:S(2)}) collective-permute-start(f32[3,64,128]{2,1,0:T(8,128)S(1)} %get-tuple-element.28.xzd), channel_id=1, source_target_pairs={{0,224},{32,0},{64,32},{96,64},{128,96},{160,128},{192,160},{224,1... | collective-permute-start | bytes 294920 | tf_op jit(solution)/shard_map/ppermute | solution.py:297
  27.1 12.0 %collective-permute-start.11 = (f32[2,8,48,128]{3,2,1,0:T(8,128)S(1)}, f32[2,8,48,128]{3,2,1,0:T(8,128)S(1)}, u32[]{:S(2)}, u32[]{:S(2)}) collective-permute-start(f32[2,8,48,128]{3,2,1,0:T(8,128)S(1)} %get-tuple-element.38), channel_id=1, source_target_pairs={{0,224},{32,0},{64,32},{96,64},{128,96},{160,128},{192,160},{224,1... | collective-permute-start | bytes 1179656 | tf_op jit(solution)/shard_map/ppermute | solution.py:297
  29.3 10.6 %collective-permute-start.8 = (f32[3,24,8,128]{3,2,1,0:T(8,128)S(1)}, f32[3,24,8,128]{3,2,1,0:T(8,128)S(1)}, u32[]{:S(2)}, u32[]{:S(2)}) collective-permute-start(f32[3,24,8,128]{3,2,1,0:T(8,128)S(1)} %get-tuple-element.35), channel_id=1, source_target_pairs={{0,8},{8,16},{16,24},{24,0},{1,9},{9,17},{17,25},{25,1},{2,10},{10... | collective-permute-start | bytes 884744 | tf_op jit(solution)/shard_map/ppermute | solution.py:297
  34.0 7.7 %collective-permute-start.9 = (f32[3,24,8,128]{3,2,1,0:T(8,128)S(1)}, f32[3,24,8,128]{3,2,1,0:T(8,128)S(1)}, u32[]{:S(2)}, u32[]{:S(2)}) collective-permute-start(f32[3,24,8,128]{3,2,1,0:T(8,128)S(1)} %get-tuple-element.36), channel_id=1, source_target_pairs={{0,24},{8,0},{16,8},{24,16},{1,25},{9,1},{17,9},{25,17},{2,26},{10... | collective-permute-start | bytes 884744 | tf_op jit(solution)/shard_map/ppermute | solution.py:297
  34.0 9.3 %collective-permute-start = (f32[1,8,48,128]{3,2,1,0:T(8,128)S(1)}, f32[1,8,48,128]{3,2,1,0:T(8,128)S(1)}, u32[]{:S(2)}, u32[]{:S(2)}) collective-permute-start(f32[1,8,48,128]{3,2,1,0:T(8,128)S(1)} %get-tuple-element.23), channel_id=1, source_target_pairs={{0,32},{32,64},{64,96},{96,128},{128,160},{160,192},{192,224},{224... | collective-permute-start | bytes 589832 | tf_op jit(solution)/shard_map/ppermute | solution.py:297
  34.1 9.3 %collective-permute-start.1 = (f32[1,8,48,128]{3,2,1,0:T(8,128)S(1)}, f32[1,8,48,128]{3,2,1,0:T(8,128)S(1)}, u32[]{:S(2)}, u32[]{:S(2)}) collective-permute-start(f32[1,8,48,128]{3,2,1,0:T(8,128)S(1)} %get-tuple-element.24), channel_id=1, source_target_pairs={{0,224},{32,0},{64,32},{96,64},{128,96},{160,128},{192,160},{224,1... | collective-permute-start | bytes 589832 | tf_op jit(solution)/shard_map/ppermute | solution.py:297
  39.2 2.5 %copy-start.1 = (f32[16,64,128]{2,1,0:T(8,128)S(1)}, f32[16,64,128]{2,1,0:T(8,128)}, u32[]{:S(2)}) copy-start(f32[16,64,128]{2,1,0:T(8,128)} %refs_8_.1) | copy-start | bytes 1572868

commit v3 on v2

--- a/solution.py
+++ b/solution.py
@@ -84,12 +84,29 @@
 
 
 def rows_band(radius, ny):
-    wide = ny + 2 * H
-    y = lax.broadcasted_iota(jnp.int32, (ny, 2 * wide), 0)
-    c = lax.broadcasted_iota(jnp.int32, (ny, 2 * wide), 1)
-    d = jnp.where(c < wide, c, c - wide) - H - y
+    y = lax.broadcasted_iota(jnp.int32, (ny, 2 * ny), 0)
+    c = lax.broadcasted_iota(jnp.int32, (ny, 2 * ny), 1)
+    d = jnp.where(c < ny, c, c - ny) - y
     value = (radius + 1) ** 2 - d * d
     return jnp.where(value > 0, value, 0).astype(F32).astype(BF16)
+
+
+def ends_band():
+    y = lax.broadcasted_iota(jnp.int32, (4 * H, 8 * H), 0)
+    c = lax.broadcasted_iota(jnp.int32, (4 * H, 8 * H), 1)
+    reach = jnp.where(y < 2 * H, R_SMALL + 1, R_LARGE + 1)
+    same = (y < 2 * H) == (c < 4 * H)
+    row, col = y % (2 * H), c % (2 * H)
+    top = (row < H) == (col < H)
+    d = jnp.where(row < H, col - H - row, col - row + H)
+    value = reach * reach - d * d
+    return jnp.where(same & top & (value > 0), value, 0).astype(F32).astype(BF16)
+
+
+def level(small, large, e):
+    low = e * (small * (0.25 * scale_of(R_SMALL))) + (0.5 - 0.25 * 0.3)
+    high = e * (large * (0.25 * scale_of(R_LARGE))) + (0.5 - 0.25 * 0.1)
+    return jnp.minimum(jnp.maximum(jnp.maximum(low, high), 0.0), 1.0)
 
 
 def stack(m):
@@ -110,30 +127,34 @@
     return total
 
 
-def pack_body(d_hbm, zr, zl, xeu, xed, d_all, sems):
-    snaps, nx, ny, nz = d_all.shape
+def pack_body(d_hbm, d, zr, zl, xeu, xed, sems):
+    snaps, nx, ny, nz = d.shape
+    parts = [(s, p * H) for s in range(snaps) for p in range(nx // H)]
     copies = [
-        pltpu.make_async_copy(d_hbm.at[s], d_all.at[s], sems.at[s]) for s in range(snaps)
+        pltpu.make_async_copy(d_hbm.at[s, pl.ds(p, H)], d.at[s, pl.ds(p, H)], sems.at[k])
+        for k, (s, p) in enumerate(parts)
     ]
     for copy in copies:
         copy.start()
     lane = lanes((ny, nz))
-    for s in range(snaps):
-        copies[s].wait()
-        d = d_all.at[s]
-        xeu[s, :, 0:H] = d[nx - H :, 0:H]
-        xeu[s, :, H:] = d[nx - H :, ny - H :]
-        xed[s, :, 0:H] = d[0:H, 0:H]
-        xed[s, :, H:] = d[0:H, ny - H :]
-        right = jnp.zeros((ny, nz), F32)
-        left = jnp.zeros((ny, nz), F32)
-        for x in range(nx):
-            r = pltpu.roll(d[x], (H * x + H) % nz, 1)
+    for (s, p), copy in zip(parts, copies):
+        copy.wait()
+        if p == 0:
+            right = jnp.zeros((ny, nz), F32)
+            left = jnp.zeros((ny, nz), F32)
+            xed[s, :, 0:H] = d[s, 0:H, 0:H]
+            xed[s, :, H:] = d[s, 0:H, ny - H :]
+        if p == nx - H:
+            xeu[s, :, 0:H] = d[s, p:, 0:H]
+            xeu[s, :, H:] = d[s, p:, ny - H :]
+        for x in range(p, p + H):
+            r = pltpu.roll(d[s, x], (H * x + H) % nz, 1)
             right = jnp.where((lane >= H * x) & (lane < H * x + H), r, right)
             at = (H * x + H) % nz
             left = jnp.where((lane >= at) & (lane < at + H), r, left)
-        zr[s] = right
-        zl[s] = pltpu.roll(left, nz - H, 1)
+        if p == nx - H:
+            zr[s] = right
+            zl[s] = pltpu.roll(left, nz - H, 1)
 
 
 def second_body(za, zb, xzu, xzd):
@@ -210,13 +231,6 @@
             x_sums(zl[:, r : r + 8], lambda i, v: put(acc_l, s, i, r, v), R_LARGE)
 
 
-def fill_body(low, xia, xib, acc_s, acc_l, us, ul):
-    n, _, _, _ = us.shape
-    wm = band(False)
-    for j in range(n):
-        add_planes(xia[j], xib[j], acc_s.at[low + j], acc_l.at[low + j], us.at[j], ul.at[j], 0, wm)
-
-
 def add_planes(xia, xib, acc_s, acc_l, us, ul, first, wm):
     nx, inner, nz = acc_s.shape
     cut = H - R_SMALL
@@ -232,64 +246,135 @@
             ul[i, at] = x_halo(acc_l[i, r : r + 8], a[:, :, nz:], b[:, :, nz:], i, nx, R_LARGE)
 
 
-def last_body(low, fused, *refs):
-    if fused:
-        xia, xib = refs[:2]
-        refs = refs[2:]
-    u_s, u_l, ws, wl, ya, yb, eff, *rest = refs
-    out, us, ul = rest[-3:]
-    j = pl.program_id(0)
-    s = j + low
-    nx, inner, nz = u_s.shape[1:]
-    ny = inner + 2 * H
+def own_sums(us, ul, band_s, band_l, i):
+    half = us.shape[0] // 2
+    sums = []
+    for ref, w in ((us, band_s), (ul, band_l)):
+        pair = jnp.concatenate([stack(ref[i]), stack(ref[i + half])], axis=1)
+        sums.append(jnp.dot(w, pair, preferred_element_type=F32))
+    return sums
+
+
+def halo_sums(ya, yb, s, i, half, w):
+    top, bottom = ya[s, 2 * half + i], yb[s, 2 * half + i]
+    first = jnp.concatenate([pltpu.roll(top, R_SMALL, 0), bottom], axis=0)
+    second = jnp.concatenate([top, pltpu.roll(bottom, R_SMALL, 0)], axis=0)
+    cols = []
+    for at, small in ((i, first), (i + half, second)):
+        large = jnp.concatenate([ya[s, at], yb[s, at]], axis=0)
+        cols.append(jnp.concatenate([stack(small), stack(large)], axis=0))
+    return jnp.dot(w, jnp.concatenate(cols, axis=1), preferred_element_type=F32)
+
+
+def rim_rows(v):
+    return jnp.concatenate([v[0:H], v[v.shape[0] - H :]], axis=0)
+
+
+def prepare(xia, xib, acc_s, acc_l, ws, wl, us, ul, wm):
+    ny = us.shape[1]
+    add_planes(xia, xib, acc_s, acc_l, us, ul, H, wm)
+    for ref, w in ((us, ws), (ul, wl)):
+        ref[:, 0:H] = w[:, 0:H]
+        ref[:, ny - H :] = w[:, H:]
+
+
+def inner_body(low, xia, xib, acc_s, acc_l, ws, wl, eff, out, es, el, us, ul, done, sems):
+    n, nx, ny, nz = us.shape
     half = nx // 2
-    if fused:
-        add_planes(xia[j], xib[j], u_s.at[s], u_l.at[s], us, ul, 2 * H, band(False))
-    else:
-        us[:, 2 * H : ny] = u_s[j]
-        ul[:, 2 * H : ny] = u_l[j]
-    ul[:, 0:H] = ya[s, 0:nx]
-    ul[:, H : 2 * H] = wl[s, :, 0:H]
-    ul[:, ny : ny + H] = wl[s, :, H:]
-    ul[:, ny + H :] = yb[s, 0:nx]
-    us[:, 0:H] = jnp.zeros((nx, H, nz), F32)
-    us[:, ny + H :] = jnp.zeros((nx, H, nz), F32)
-    us[0:half, H - R_SMALL : H] = ya[s, nx:, 0:R_SMALL]
-    us[half:, H - R_SMALL : H] = ya[s, nx:, R_SMALL:]
-    us[:, H : 2 * H] = ws[s, :, 0:H]
-    us[:, ny : ny + H] = ws[s, :, H:]
-    us[0:half, ny + H : ny + H + R_SMALL] = yb[s, nx:, 0:R_SMALL]
-    us[half:, ny + H : ny + H + R_SMALL] = yb[s, nx:, R_SMALL:]
+    rows = slice(H, ny - H)
+    wm = band(False)
     band_s, band_l = rows_band(R_SMALL, ny), rows_band(R_LARGE, ny)
-    scale_s, scale_l = 0.25 * scale_of(R_SMALL), 0.25 * scale_of(R_LARGE)
-
-    def y_sum(ref, w, i):
-        pair = jnp.concatenate([stack(ref[i]), stack(ref[i + half])], axis=1)
-        return jnp.dot(w, pair, preferred_element_type=F32)
-
-    for i in range(half):
-        small, large = y_sum(us, band_s, i), y_sum(ul, band_l, i)
-        for at, col in ((i, slice(0, nz)), (i + half, slice(nz, 2 * nz))):
-            e = eff[at]
-            low_r = e * (small[:, col] * scale_s) + (0.5 - 0.25 * 0.3)
-            high_r = e * (large[:, col] * scale_l) + (0.5 - 0.25 * 0.1)
-            out[0, at] = jnp.minimum(jnp.maximum(jnp.maximum(low_r, high_r), 0.0), 1.0)
-
-
-def last(low, high, fused, args, before, shape):
-    nx, ny, nz = shape[1:]
-    extra = [] if before is None else [before]
+    copies = []
+    for j in range(n):
+        s = low + j
+        here = (acc_s.at[s], acc_l.at[s], ws.at[s], wl.at[s], us.at[j], ul.at[j])
+        prepare(xia[j], xib[j], *here, wm)
+        for i in range(half):
+            sums = own_sums(us.at[j], ul.at[j], band_s, band_l, i)
+            for at, col in ((i, slice(0, nz)), (i + half, slice(nz, 2 * nz))):
+                small, large = sums[0][:, col], sums[1][:, col]
+                done[j, at] = level(small[rows], large[rows], eff[at, rows])
+                es[j, at] = rim_rows(small)
+                el[j, at] = rim_rows(large)
+        copy = pltpu.make_async_copy(done.at[j], out.at[s, :, pl.ds(H, ny - 2 * H), :], sems.at[j])
+        copy.start()
+        copies.append(copy)
+    for copy in copies:
+        copy.wait()
+
+
+def final_body(low, xia, xib, acc_s, acc_l, ws, wl, eff, ya, yb, es, el, _, out, us, ul, rim, done, sems):
+    n, nx, ny, nz = us.shape
+    half = nx // 2
+    wm, w = band(False), ends_band()
+    band_s, band_l = rows_band(R_SMALL, ny), rows_band(R_LARGE, ny)
+    sides = ((0, slice(0, nz)), (half, slice(nz, 2 * nz)))
+    copies = []
+    for j in range(n):
+        s = low + j
+        here = (acc_s.at[s], acc_l.at[s], ws.at[s], wl.at[s], us.at[j], ul.at[j])
+        prepare(xia[j], xib[j], *here, wm)
+        for i in range(half):
+            sums = own_sums(us.at[j], ul.at[j], band_s, band_l, i)
+            more = halo_sums(ya, yb, s, i, half, w)
+            for step, col in sides:
+                at = i + step
+                small, large = sums[0][:, col], sums[1][:, col]
+                add_s, add_l = more[0 : 2 * H, col], more[2 * H :, col]
+                rows = slice(H, ny - H)
+                done[j, at, rows] = level(small[rows], large[rows], eff[at, rows])
+                ends = level(rim_rows(small) + add_s, rim_rows(large) + add_l, rim_rows(eff[at]))
+                done[j, at, 0:H] = ends[0:H]
+                done[j, at, ny - H :] = ends[H:]
+        copies.append(pltpu.make_async_copy(done.at[j], out.at[s], sems.at[len(copies)]))
+        copies[-1].start()
+    for s in range(low):
+        for i in range(half):
+            more = halo_sums(ya, yb, s, i, half, w)
+            for step, col in sides:
+                at = i + step
+                add_s, add_l = more[0 : 2 * H, col], more[2 * H :, col]
+                rim[s, at] = level(es[s, at] + add_s, el[s, at] + add_l, rim_rows(eff[at]))
+        for k, start in enumerate((0, ny - H)):
+            source = rim.at[s, :, pl.ds(k * H, H), :]
+            target = out.at[s, :, pl.ds(start, H), :]
+            copies.append(pltpu.make_async_copy(source, target, sems.at[len(copies)]))
+            copies[-1].start()
+    for copy in copies:
+        copy.wait()
+
+
+def inner_call(high, args, shape):
+    _, nx, ny, nz = shape
+    ends = (high, nx, 2 * H, nz)
     return pl.pallas_call(
-        lambda *refs: last_body(low, fused, *refs),
+        lambda *refs: inner_body(0, *refs),
+        out_shape=[jax.ShapeDtypeStruct(shape, F32), pltpu.VMEM(ends, F32), pltpu.VMEM(ends, F32)],
+        in_specs=[VMEM] * len(args),
+        out_specs=[pl.BlockSpec(memory_space=pl.ANY), VMEM, VMEM],
+        scratch_shapes=[pltpu.VMEM((high, nx, ny, nz), F32)] * 2
+        + [pltpu.VMEM((high, nx, ny - 2 * H, nz), F32), pltpu.SemaphoreType.DMA((high,))],
+        compiler_params=PARAMS,
+        name="inner",
+    )(*[near(a) for a in args])
+
+
+def final_call(low, args, before, shape):
+    snaps, nx, ny, nz = shape
+    n = snaps - low
+    any_space = pl.BlockSpec(memory_space=pl.ANY)
+    return pl.pallas_call(
+        lambda *refs: final_body(low, *refs),
         out_shape=jax.ShapeDtypeStruct(shape, F32),
-        grid=(high - low,),
-        in_specs=[VMEM] * len(args) + [pl.BlockSpec(memory_space=pl.ANY)] * len(extra),
-        out_specs=pl.BlockSpec((1, nx, ny, nz), lambda j: (j + low, 0, 0, 0)),
-        scratch_shapes=[pltpu.VMEM((nx, ny + 2 * H, nz), F32)] * 2,
-        input_output_aliases={len(args): 0} if extra else {},
+        in_specs=[VMEM] * len(args) + [any_space],
+        out_specs=any_space,
+        scratch_shapes=[pltpu.VMEM((n, nx, ny, nz), F32)] * 2
+        + [pltpu.VMEM((low, nx, 2 * H, nz), F32), pltpu.VMEM((n, nx, ny, nz), F32)]
+        + [pltpu.SemaphoreType.DMA((n + 2 * low,))],
+        input_output_aliases={len(args): 0},
         compiler_params=PARAMS,
-        name="last",
-    )(*[near(a) for a in args], *extra)
+        name="final",
+    )(*[near(a) for a in args], before)
 
 
 def shift(block, axis, step):
@@ -307,12 +392,12 @@
     inner = ny - 2 * H
     zpack = (snaps, ny, nz)
     xe = (snaps, H, 2 * H, nz)
-    zr, zl, xeu, xed = pl.pallas_call(
+    own, zr, zl, xeu, xed = pl.pallas_call(
         pack_body,
-        out_shape=[pltpu.VMEM(s, F32) for s in (zpack, zpack, xe, xe)],
+        out_shape=[pltpu.VMEM(s, F32) for s in (block, zpack, zpack, xe, xe)],
         in_specs=[pl.BlockSpec(memory_space=pl.ANY)],
-        out_specs=[VMEM] * 4,
-        scratch_shapes=[pltpu.VMEM(block, F32), pltpu.SemaphoreType.DMA((snaps,))],
+        out_specs=[VMEM] * 5,
+        scratch_shapes=[pltpu.SemaphoreType.DMA((snaps * nx // H,))],
         compiler_params=PARAMS,
         name="pack",
     )(pltpu.with_memory_space_constraint(density, pltpu.HBM))
@@ -321,29 +406,24 @@
     slabs = []
     for low, high in CHUNKS:
         slabs += [(high - low, H, inner, nz)] * 2
-    slabs = run(slab_body, (density,), slabs)
+    slabs = run(slab_body, (own,), slabs)
     xzu, xzd = run(second_body, (za, zb), (zpack, zpack))
     xza, xzb = both("gx", xzu, xzd)
     halos = [both("gx", *slabs[2 * c : 2 * c + 2]) for c in range(len(CHUNKS))]
     wide = nx + 2 * H
     rim = [(snaps, nx, 2 * H, nz)] * 2 + [(snaps, nx + nx // 2, H, nz)] * 2
-    ws, wl, yu, yd = run(rim_body, (density, xea, xeb, xza, xzd, xzu, xzb), rim)
+    ws, wl, yu, yd = run(rim_body, (own, xea, xeb, xza, xzd, xzu, xzb), rim)
     ya, yb = both("gy", yu, yd)
     acc_s, acc_l = run(
         middle_body,
-        (density, xza, xzd, xzu, xzb),
+        (own, xza, xzd, xzu, xzb),
         [(snaps, nx, inner, nz)] * 2,
         [pltpu.VMEM((snaps, wide, inner, nz), F32)] * 2,
     )
-    out = None
-    for c, ((low, high), (xia, xib)) in enumerate(zip(CHUNKS, halos)):
-        rest = (ws, wl, ya, yb, efficiency)
-        if c == len(CHUNKS) - 1:
-            out = last(low, high, True, (xia, xib, acc_s, acc_l) + rest, out, block)
-        else:
-            part = [(high - low, nx, inner, nz)] * 2
-            filled = run(lambda *refs: fill_body(low, *refs), (xia, xib, acc_s, acc_l), part)
-            out = last(low, high, False, tuple(filled) + rest, out, block)
+    shared = (acc_s, acc_l, ws, wl, efficiency)
+    (_, split_at), _ = CHUNKS
+    out, es, el = inner_call(split_at, halos[0] + shared, block)
+    out = final_call(split_at, halos[1] + shared + (ya, yb, es, el), out, block)
     return out
 
 

time: 45 us -> 45.2 us (level)
  the two profiles are of different devices: /device:TPU:1 before, /device:TPU:56 now
where the time goes in v3:
time: 45.2 us; the launch traced here: 45.1 us
  starting transfers between devices  19.6 us (43%)
  waiting for transfers between devices  16 us (35%)
  Pallas kernels  9.28 us (21%)
    ppermute x12, starting transfers between devices, shift(): return lax.ppermute(block, axis, [(i, (i + step) % n) for i in range(n)])  19.6 us
    ppermute x12, waiting for transfers between devices, shift(): return lax.ppermute(block, axis, [(i, (i + step) % n) for i in range(n)])  16 us
    pallas_call x4, Pallas kernels, run(): pl.pallas_call(body, out_shape=[pltpu.VMEM(s, F32) for s in outs], in_spe...  3.59 us
    pallas_call x1, Pallas kernels, steps(): pl.pallas_call(pack_body, out_shape=[pltpu.VMEM(s, F32) for s in (block,...  2.02 us
    pallas_call x1, Pallas kernels, inner_call(): pl.pallas_call(lambda *refs: inner_body(0, *refs), out_shape=[jax.ShapeDt...  1.97 us
    pallas_call x1, Pallas kernels, final_call(): pl.pallas_call(lambda *refs: final_body(low, *refs), out_shape=jax.ShapeD...  1.69 us
  transfers between devices with their start and end apart: 12, of which 5 were waited for; matrix products, arithmetic and copies ran while one was open for 0% of the time, Pallas kernels for 12%

profile of v3, /device:TPU:56, one launch (start us, length us, event | category | flops | bytes accessed | tf_op | source)
XLA Modules:
  0.0 45.1 jit_solution(15605273674922637370)
XLA Ops:
  0.0 2.0 %pack.1 = (f32[3,16,64,128]{3,2,1,0:T(8,128)S(1)}, f32[3,64,128]{2,1,0:T(8,128)S(1)}, f32[3,64,128]{2,1,0:T(8,128)S(1)}, f32[3,8,16,128]{3,2,1,0:T(8,128)S(1)}, f32[3,8,16,128]{3,2,1,0:T(8,128)S(1)}) custom-call(f32[3,16,64,128]{3,2,1,0:T(8,128)} %d_hbm.1), custom_call_target="tpu_custom_call" | custom-call | tf_op jit(solution)/shard_map/pack/pallas_call | solution.py:395
  2.0 1.2 %collective-permute-start.2 = (f32[3,64,128]{2,1,0:T(8,128)S(1)}, f32[3,64,128]{2,1,0:T(8,128)S(1)}, u32[]{:S(2)}, u32[]{:S(2)}) collective-permute-start(f32[3,64,128]{2,1,0:T(8,128)S(1)} %get-tuple-element.28), channel_id=1, source_target_pairs={{0,1},{1,2},{2,3},{3,4},{4,5},{5,6},{6,7},{7,0},{8,9},{9,10},{10,1... | collective-permute-start | bytes 294920 | tf_op jit(solution)/shard_map/ppermute | solution.py:382
  3.3 0.9 %collective-permute-start.3 = (f32[3,64,128]{2,1,0:T(8,128)S(1)}, f32[3,64,128]{2,1,0:T(8,128)S(1)}, u32[]{:S(2)}, u32[]{:S(2)}) collective-permute-start(f32[3,64,128]{2,1,0:T(8,128)S(1)} %get-tuple-element.29), channel_id=1, source_target_pairs={{0,7},{1,0},{2,1},{3,2},{4,3},{5,4},{6,5},{7,6},{8,15},{9,8},{10,9... | collective-permute-start | bytes 294920 | tf_op jit(solution)/shard_map/ppermute | solution.py:382
  4.1 0.1 shard_map.28
  4.2 2.0 %collective-permute-start.10 = (f32[2,8,48,128]{3,2,1,0:T(8,128)S(1)}, f32[2,8,48,128]{3,2,1,0:T(8,128)S(1)}, u32[]{:S(2)}, u32[]{:S(2)}) collective-permute-start(f32[2,8,48,128]{3,2,1,0:T(8,128)S(1)} %get-tuple-element.40), channel_id=1, source_target_pairs={{0,32},{32,64},{64,96},{96,128},{128,160},{160,192},{192,224},{224... | collective-permute-start | bytes 1179656 | tf_op jit(solution)/shard_map/ppermute | solution.py:382
  6.2 0.5 %collective-permute-done.2.za = f32[3,64,128]{2,1,0:T(8,128)S(1)} collective-permute-done((f32[3,64,128]{2,1,0:T(8,128)S(1)}, f32[3,64,128]{2,1,0:T(8,128)S(1)}, u32[]{:S(2)}, u32[]{:S(2)}) %collective-permute-start.2) | collective-permute-done | bytes 98336 | tf_op jit(solution)/shard_map/ppermute | solution.py:382
  6.7 3.3 %collective-permute-done.3.zb = f32[3,64,128]{2,1,0:T(8,128)S(1)} collective-permute-done((f32[3,64,128]{2,1,0:T(8,128)S(1)}, f32[3,64,128]{2,1,0:T(8,128)S(1)}, u32[]{:S(2)}, u32[]{:S(2)}) %collective-permute-start.3) | collective-permute-done | bytes 98336 | tf_op jit(solution)/shard_map/ppermute | solution.py:382
  10.0 0.1 shard_map.29
  10.1 2.0 %collective-permute-start.4 = (f32[3,64,128]{2,1,0:T(8,128)S(1)}, f32[3,64,128]{2,1,0:T(8,128)S(1)}, u32[]{:S(2)}, u32[]{:S(2)}) collective-permute-start(f32[3,64,128]{2,1,0:T(8,128)S(1)} %get-tuple-element.30.xzu), channel_id=1, source_target_pairs={{0,32},{32,64},{64,96},{96,128},{128,160},{160,192},{192,224},{224... | collective-permute-start | bytes 294920 | tf_op jit(solution)/shard_map/ppermute | solution.py:382
  12.1 1.9 %collective-permute-start.6 = (f32[3,8,16,128]{3,2,1,0:T(8,128)S(1)}, f32[3,8,16,128]{3,2,1,0:T(8,128)S(1)}, u32[]{:S(2)}, u32[]{:S(2)}) collective-permute-start(f32[3,8,16,128]{3,2,1,0:T(8,128)S(1)} %get-tuple-element.34), channel_id=1, source_target_pairs={{0,32},{32,64},{64,96},{96,128},{128,160},{160,192},{192,224},{224... | collective-permute-start | bytes 589832 | tf_op jit(solution)/shard_map/ppermute | solution.py:382
  14.0 0.1 collective-permute-start.7
  14.1 2.2 %collective-permute-start.11 = (f32[2,8,48,128]{3,2,1,0:T(8,128)S(1)}, f32[2,8,48,128]{3,2,1,0:T(8,128)S(1)}, u32[]{:S(2)}, u32[]{:S(2)}) collective-permute-start(f32[2,8,48,128]{3,2,1,0:T(8,128)S(1)} %get-tuple-element.41), channel_id=1, source_target_pairs={{0,224},{32,0},{64,32},{96,64},{128,96},{160,128},{192,160},{224,1... | collective-permute-start | bytes 1179656 | tf_op jit(solution)/shard_map/ppermute | solution.py:382
  16.3 2.1 %collective-permute-done.4.xza = f32[3,64,128]{2,1,0:T(8,128)S(1)} collective-permute-done((f32[3,64,128]{2,1,0:T(8,128)S(1)}, f32[3,64,128]{2,1,0:T(8,128)S(1)}, u32[]{:S(2)}, u32[]{:S(2)}) %collective-permute-start.4) | collective-permute-done | bytes 98336 | tf_op jit(solution)/shard_map/ppermute | solution.py:382
  18.4 3.9 %collective-permute-start.5 = (f32[3,64,128]{2,1,0:T(8,128)S(1)}, f32[3,64,128]{2,1,0:T(8,128)S(1)}, u32[]{:S(2)}, u32[]{:S(2)}) collective-permute-start(f32[3,64,128]{2,1,0:T(8,128)S(1)} %get-tuple-element.31.xzd), channel_id=1, source_target_pairs={{0,224},{32,0},{64,32},{96,64},{128,96},{160,128},{192,160},{224,1... | collective-permute-start | bytes 294920 | tf_op jit(solution)/shard_map/ppermute | solution.py:382
  22.3 8.3 %collective-permute-done.5.xzb = f32[3,64,128]{2,1,0:T(8,128)S(1)} collective-permute-done((f32[3,64,128]{2,1,0:T(8,128)S(1)}, f32[3,64,128]{2,1,0:T(8,128)S(1)}, u32[]{:S(2)}, u32[]{:S(2)}) %collective-permute-start.5) | collective-permute-done | bytes 98336 | tf_op jit(solution)/shard_map/ppermute | solution.py:382
  30.6 0.0 collective-permute-done.6.xea
  30.6 0.0 collective-permute-done.7.xeb
  30.6 1.0 %shard_map.31 = (f32[3,16,16,128]{3,2,1,0:T(8,128)S(1)}, f32[3,16,16,128]{3,2,1,0:T(8,128)S(1)}, f32[3,24,8,128]{3,2,1,0:T(8,128)S(1)}, f32[3,24,8,128]{3,2,1,0:T(8,128)S(1)}) custom-call(f32[3,16,64,128]{3,2,1,0:T(8,128)S(1)} %get-tuple-element.25.d, f32[3,8,16,128]{3,2,1,0:T(8,128)S(1)} %collective-permute-done.6.xea, ...), custom_call_target="tpu_custom_call" | custom-call | tf_op jit(solution)/shard_map/pallas_call | solution.py:36
  31.6 0.0 copy-start
  31.6 0.1 collective-permute-start.8
  31.7 3.2 %collective-permute-start.9 = (f32[3,24,8,128]{3,2,1,0:T(8,128)S(1)}, f32[3,24,8,128]{3,2,1,0:T(8,128)S(1)}, u32[]{:S(2)}, u32[]{:S(2)}) collective-permute-start(f32[3,24,8,128]{3,2,1,0:T(8,128)S(1)} %get-tuple-element.39), channel_id=1, source_target_pairs={{0,24},{8,0},{16,8},{24,16},{1,25},{9,1},{17,9},{25,17},{2,26},{10... | collective-permute-start | bytes 884744 | tf_op jit(solution)/shard_map/ppermute | solution.py:382
  34.9 1.7 %collective-permute-start = (f32[1,8,48,128]{3,2,1,0:T(8,128)S(1)}, f32[1,8,48,128]{3,2,1,0:T(8,128)S(1)}, u32[]{:S(2)}, u32[]{:S(2)}) collective-permute-start(f32[1,8,48,128]{3,2,1,0:T(8,128)S(1)} %get-tuple-element.26), channel_id=1, source_target_pairs={{0,32},{32,64},{64,96},{96,128},{128,160},{160,192},{192,224},{224... | collective-permute-start | bytes 589832 | tf_op jit(solution)/shard_map/ppermute | solution.py:382
  36.6 0.0 collective-permute-done.10.refs_0_
  36.6 0.3 collective-permute-start.1
  36.9 2.4 %shard_map.30 = (f32[3,16,48,128]{3,2,1,0:T(8,128)S(1)}, f32[3,16,48,128]{3,2,1,0:T(8,128)S(1)}) custom-call(f32[3,16,64,128]{3,2,1,0:T(8,128)S(1)} %get-tuple-element.25.d, f32[3,64,128]{2,1,0:T(8,128)S(1)} %collective-permute-done.4.xza, f32[3,64,128]{2,1,0:T(8,128)S(1)} %get-tuple-element.31.xzd, f32[3,64,128]{2,1,0:T(8,128)S(1)} %get-tuple-element.30.xzu, ...), custom_call_target="tpu_custom_call" | custom-call | tf_op jit(solution)/shard_map/pallas_call | solution.py:36
  39.4 0.0 collective-permute-done.11.refs_1_
  39.4 0.0 copy-done
  39.4 2.0 %inner.1 = (f32[3,16,64,128]{3,2,1,0:T(8,128)}, f32[2,16,16,128]{3,2,1,0:T(8,128)S(1)}, f32[2,16,16,128]{3,2,1,0:T(8,128)S(1)}) custom-call(f32[2,8,48,128]{3,2,1,0:T(8,128)S(1)} %collective-permute-done.10.refs_0_, f32[2,8,48,128]{3,2,1,0:T(8,128)S(1)} %collective-permute-done.11.refs_1_, f32[3,16,48,128]{3,2,1,0:T(8,128)S(1)} %get-tuple-element.32.refs_2_, ...), custom_call_target="tpu_custom_call" | custom-call | tf_op jit(solution)/shard_map/inner/pallas_call | solution.py:350
  41.4 0.0 collective-permute-done.refs_0_
  41.4 1.9 %collective-permute-done.1.refs_1_ = f32[1,8,48,128]{3,2,1,0:T(8,128)S(1)} collective-permute-done((f32[1,8,48,128]{3,2,1,0:T(8,128)S(1)}, f32[1,8,48,128]{3,2,1,0:T(8,128)S(1)}, u32[]{:S(2)}, u32[]{:S(2)}) %collective-permute-start.1) | collective-permute-done | bytes 196640 | tf_op jit(solution)/shard_map/ppermute | solution.py:382
  43.3 0.0 collective-permute-done.8.refs_7_
  43.3 0.0 collective-permute-done.9.refs_8_
  43.3 1.7 %final.1 = f32[3,16,64,128]{3,2,1,0:T(8,128)} custom-call(f32[1,8,48,128]{3,2,1,0:T(8,128)S(1)} %collective-permute-done.refs_0_, f32[1,8,48,128]{3,2,1,0:T(8,128)S(1)} %collective-permute-done.1.refs_1_, f32[3,16,48,128]{3,2,1,0:T(8,128)S(1)} %get-tuple-element.32.refs_2_, ...), custom_call_target="tpu_custom_call", output_to_operand_aliasing={{}: (11, {})} | custom-call | tf_op jit(solution)/shard_map/final/pallas_call | solution.py:366
Async XLA Ops:
  2.0 4.7 %collective-permute-start.2 = (f32[3,64,128]{2,1,0:T(8,128)S(1)}, f32[3,64,128]{2,1,0:T(8,128)S(1)}, u32[]{:S(2)}, u32[]{:S(2)}) collective-permute-start(f32[3,64,128]{2,1,0:T(8,128)S(1)} %get-tuple-element.28), channel_id=1, source_target_pairs={{0,1},{1,2},{2,3},{3,4},{4,5},{5,6},{6,7},{7,0},{8,9},{9,10},{10,1... | collective-permute-start | bytes 294920 | tf_op jit(solution)/shard_map/ppermute | solution.py:382
  3.3 6.7 %collective-permute-start.3 = (f32[3,64,128]{2,1,0:T(8,128)S(1)}, f32[3,64,128]{2,1,0:T(8,128)S(1)}, u32[]{:S(2)}, u32[]{:S(2)}) collective-permute-start(f32[3,64,128]{2,1,0:T(8,128)S(1)} %get-tuple-element.29), channel_id=1, source_target_pairs={{0,7},{1,0},{2,1},{3,2},{4,3},{5,4},{6,5},{7,6},{8,15},{9,8},{10,9... | collective-permute-start | bytes 294920 | tf_op jit(solution)/shard_map/ppermute | solution.py:382
  4.2 32.4 %collective-permute-start.10 = (f32[2,8,48,128]{3,2,1,0:T(8,128)S(1)}, f32[2,8,48,128]{3,2,1,0:T(8,128)S(1)}, u32[]{:S(2)}, u32[]{:S(2)}) collective-permute-start(f32[2,8,48,128]{3,2,1,0:T(8,128)S(1)} %get-tuple-element.40), channel_id=1, source_target_pairs={{0,32},{32,64},{64,96},{96,128},{128,160},{160,192},{192,224},{224... | collective-permute-start | bytes 1179656 | tf_op jit(solution)/shard_map/ppermute | solution.py:382
  10.1 8.3 %collective-permute-start.4 = (f32[3,64,128]{2,1,0:T(8,128)S(1)}, f32[3,64,128]{2,1,0:T(8,128)S(1)}, u32[]{:S(2)}, u32[]{:S(2)}) collective-permute-start(f32[3,64,128]{2,1,0:T(8,128)S(1)} %get-tuple-element.30.xzu), channel_id=1, source_target_pairs={{0,32},{32,64},{64,96},{96,128},{128,160},{160,192},{192,224},{224... | collective-permute-start | bytes 294920 | tf_op jit(solution)/shard_map/ppermute | solution.py:382
  12.1 18.5 %collective-permute-start.6 = (f32[3,8,16,128]{3,2,1,0:T(8,128)S(1)}, f32[3,8,16,128]{3,2,1,0:T(8,128)S(1)}, u32[]{:S(2)}, u32[]{:S(2)}) collective-permute-start(f32[3,8,16,128]{3,2,1,0:T(8,128)S(1)} %get-tuple-element.34), channel_id=1, source_target_pairs={{0,32},{32,64},{64,96},{96,128},{128,160},{160,192},{192,224},{224... | collective-permute-start | bytes 589832 | tf_op jit(solution)/shard_map/ppermute | solution.py:382
  14.0 16.6 %collective-permute-start.7 = (f32[3,8,16,128]{3,2,1,0:T(8,128)S(1)}, f32[3,8,16,128]{3,2,1,0:T(8,128)S(1)}, u32[]{:S(2)}, u32[]{:S(2)}) collective-permute-start(f32[3,8,16,128]{3,2,1,0:T(8,128)S(1)} %get-tuple-element.35), channel_id=1, source_target_pairs={{0,224},{32,0},{64,32},{96,64},{128,96},{160,128},{192,160},{224,1... | collective-permute-start | bytes 589832 | tf_op jit(solution)/shard_map/ppermute | solution.py:382
  14.1 25.3 %collective-permute-start.11 = (f32[2,8,48,128]{3,2,1,0:T(8,128)S(1)}, f32[2,8,48,128]{3,2,1,0:T(8,128)S(1)}, u32[]{:S(2)}, u32[]{:S(2)}) collective-permute-start(f32[2,8,48,128]{3,2,1,0:T(8,128)S(1)} %get-tuple-element.41), channel_id=1, source_target_pairs={{0,224},{32,0},{64,32},{96,64},{128,96},{160,128},{192,160},{224,1... | collective-permute-start | bytes 1179656 | tf_op jit(solution)/shard_map/ppermute | solution.py:382
  18.4 12.2 %collective-permute-start.5 = (f32[3,64,128]{2,1,0:T(8,128)S(1)}, f32[3,64,128]{2,1,0:T(8,128)S(1)}, u32[]{:S(2)}, u32[]{:S(2)}) collective-permute-start(f32[3,64,128]{2,1,0:T(8,128)S(1)} %get-tuple-element.31.xzd), channel_id=1, source_target_pairs={{0,224},{32,0},{64,32},{96,64},{128,96},{160,128},{192,160},{224,1... | collective-permute-start | bytes 294920 | tf_op jit(solution)/shard_map/ppermute | solution.py:382
  31.6 7.8 %copy-start = (f32[16,64,128]{2,1,0:T(8,128)S(1)}, f32[16,64,128]{2,1,0:T(8,128)}, u32[]{:S(2)}) copy-start(f32[16,64,128]{2,1,0:T(8,128)} %refs_6_.3) | copy-start | bytes 1572868
  31.6 11.7 %collective-permute-start.8 = (f32[3,24,8,128]{3,2,1,0:T(8,128)S(1)}, f32[3,24,8,128]{3,2,1,0:T(8,128)S(1)}, u32[]{:S(2)}, u32[]{:S(2)}) collective-permute-start(f32[3,24,8,128]{3,2,1,0:T(8,128)S(1)} %get-tuple-element.38), channel_id=1, source_target_pairs={{0,8},{8,16},{16,24},{24,0},{1,9},{9,17},{17,25},{25,1},{2,10},{10... | collective-permute-start | bytes 884744 | tf_op jit(solution)/shard_map/ppermute | solution.py:382
  31.7 11.6 %collective-permute-start.9 = (f32[3,24,8,128]{3,2,1,0:T(8,128)S(1)}, f32[3,24,8,128]{3,2,1,0:T(8,128)S(1)}, u32[]{:S(2)}, u32[]{:S(2)}) collective-permute-start(f32[3,24,8,128]{3,2,1,0:T(8,128)S(1)} %get-tuple-element.39), channel_id=1, source_target_pairs={{0,24},{8,0},{16,8},{24,16},{1,25},{9,1},{17,9},{25,17},{2,26},{10... | collective-permute-start | bytes 884744 | tf_op jit(solution)/shard_map/ppermute | solution.py:382
  34.9 6.5 %collective-permute-start = (f32[1,8,48,128]{3,2,1,0:T(8,128)S(1)}, f32[1,8,48,128]{3,2,1,0:T(8,128)S(1)}, u32[]{:S(2)}, u32[]{:S(2)}) collective-permute-start(f32[1,8,48,128]{3,2,1,0:T(8,128)S(1)} %get-tuple-element.26), channel_id=1, source_target_pairs={{0,32},{32,64},{64,96},{96,128},{128,160},{160,192},{192,224},{224... | collective-permute-start | bytes 589832 | tf_op jit(solution)/shard_map/ppermute | solution.py:382
  36.6 6.6 %collective-permute-start.1 = (f32[1,8,48,128]{3,2,1,0:T(8,128)S(1)}, f32[1,8,48,128]{3,2,1,0:T(8,128)S(1)}, u32[]{:S(2)}, u32[]{:S(2)}) collective-permute-start(f32[1,8,48,128]{3,2,1,0:T(8,128)S(1)} %get-tuple-element.27), channel_id=1, source_target_pairs={{0,224},{32,0},{64,32},{96,64},{128,96},{160,128},{192,160},{224,1... | collective-permute-start | bytes 589832 | tf_op jit(solution)/shard_map/ppermute | solution.py:382

commit v4 on v3

--- a/solution.py
+++ b/solution.py
@@ -11,7 +11,7 @@
 R_SMALL = 4
 R_LARGE = 8
 H = R_LARGE
-CHUNKS = ((0, 2), (2, 3))
+LATE = 3
 VMEM = pl.BlockSpec(memory_space=pltpu.VMEM)
 F32 = jnp.float32
 BF16 = jnp.bfloat16
@@ -129,32 +129,24 @@
 
 def pack_body(d_hbm, d, zr, zl, xeu, xed, sems):
     snaps, nx, ny, nz = d.shape
-    parts = [(s, p * H) for s in range(snaps) for p in range(nx // H)]
-    copies = [
-        pltpu.make_async_copy(d_hbm.at[s, pl.ds(p, H)], d.at[s, pl.ds(p, H)], sems.at[k])
-        for k, (s, p) in enumerate(parts)
-    ]
+    copies = [pltpu.make_async_copy(d_hbm.at[s], d.at[s], sems.at[s]) for s in range(snaps)]
     for copy in copies:
         copy.start()
     lane = lanes((ny, nz))
-    for (s, p), copy in zip(parts, copies):
-        copy.wait()
-        if p == 0:
-            right = jnp.zeros((ny, nz), F32)
-            left = jnp.zeros((ny, nz), F32)
-            xed[s, :, 0:H] = d[s, 0:H, 0:H]
-            xed[s, :, H:] = d[s, 0:H, ny - H :]
-        if p == nx - H:
-            xeu[s, :, 0:H] = d[s, p:, 0:H]
-            xeu[s, :, H:] = d[s, p:, ny - H :]
-        for x in range(p, p + H):
+    for s in range(snaps):
+        copies[s].wait()
+        for out, at in ((xeu, nx - H), (xed, 0)):
+            out[2 * s * H : (2 * s + 1) * H] = d[s, at : at + H, 0:H]
+            out[(2 * s + 1) * H : (2 * s + 2) * H] = d[s, at : at + H, ny - H :]
+        right = jnp.zeros((ny, nz), F32)
+        left = jnp.zeros((ny, nz), F32)
+        for x in range(nx):
             r = pltpu.roll(d[s, x], (H * x + H) % nz, 1)
             right = jnp.where((lane >= H * x) & (lane < H * x + H), r, right)
             at = (H * x + H) % nz
             left = jnp.where((lane >= at) & (lane < at + H), r, left)
-        if p == nx - H:
-            zr[s] = right
-            zl[s] = pltpu.roll(left, nz - H, 1)
+        zr[s] = right
+        zl[s] = pltpu.roll(left, nz - H, 1)
 
 
 def second_body(za, zb, xzu, xzd):
@@ -166,11 +158,17 @@
         xzd[s] = jnp.where(lane < half, za[s], pltpu.roll(zb[s], half, 1))
 
 
+def inner_blocks(snaps, ny):
+    return [(s, r * H) for s in range(snaps) for r in range(1, ny // H - 1)]
+
+
 def slab_body(d, *outs):
-    nx, ny = d.shape[1:3]
-    for (low, high), up, down in zip(CHUNKS, outs[0::2], outs[1::2]):
-        up[...] = d[low:high, nx - H :, H : ny - H]
-        down[...] = d[low:high, 0:H, H : ny - H]
+    snaps, nx, ny, _ = d.shape
+    jobs = inner_blocks(snaps, ny)
+    for part, up, down in ((jobs[:-LATE], *outs[0:2]), (jobs[-LATE:], *outs[2:4])):
+        for k, (s, row) in enumerate(part):
+            up[k * H : (k + 1) * H] = d[s, nx - H :, row : row + H]
+            down[k * H : (k + 1) * H] = d[s, 0:H, row : row + H]
 
 
 def put(ref, s, i, r, value):
@@ -193,9 +191,9 @@
 
     for s in range(snaps):
         packs = [ends(p[s]) for p in (xza, xzd, xzu, xzb)]
-        main = [xea[s, p] for p in range(H)]
+        main = [xea[(s * 2 + h) * H + p] for p in range(H) for h in (0, 1)]
         main += [ends(d[s, x]) for x in range(nx)]
-        main += [xeb[s, p] for p in range(H)]
+        main += [xeb[(s * 2 + h) * H + p] for p in range(H) for h in (0, 1)]
         side = [edge_of(packs[p // H], p % H) for p in range(nx + 2 * H)]
         out = mul(jnp.concatenate(main, axis=0), wm) + mul(jnp.concatenate(side, axis=0), we)
         out = out.reshape(nx + 2 * H, 2 * H, 2 * nz)
@@ -234,10 +232,10 @@
 def add_planes(xia, xib, acc_s, acc_l, us, ul, first, wm):
     nx, inner, nz = acc_s.shape
     cut = H - R_SMALL
-    za = mul(xia.reshape(H * inner, nz), wm).reshape(H, inner, 2 * nz)
-    zb = mul(xib.reshape(H * inner, nz), wm).reshape(H, inner, 2 * nz)
+    za = mul(xia.reshape(H * inner, nz), wm).reshape(inner // 8, H, 8, 2 * nz)
+    zb = mul(xib.reshape(H * inner, nz), wm).reshape(inner // 8, H, 8, 2 * nz)
     for r in range(0, inner, 8):
-        a, b = za[:, r : r + 8], zb[:, r : r + 8]
+        a, b = za[r // 8], zb[r // 8]
         at = slice(first + r, first + r + 8)
         for i in range(nx):
             us[i, at] = x_halo(
@@ -278,7 +276,7 @@
         ref[:, ny - H :] = w[:, H:]
 
 
-def inner_body(low, xia, xib, acc_s, acc_l, ws, wl, eff, out, es, el, us, ul, done, sems):
+def inner_body(xia, xib, acc_s, acc_l, ws, wl, eff, out, es, el, us, ul, done, sems):
     n, nx, ny, nz = us.shape
     half = nx // 2
     rows = slice(H, ny - H)
@@ -286,9 +284,11 @@
     band_s, band_l = rows_band(R_SMALL, ny), rows_band(R_LARGE, ny)
     copies = []
     for j in range(n):
-        s = low + j
+        s = j
         here = (acc_s.at[s], acc_l.at[s], ws.at[s], wl.at[s], us.at[j], ul.at[j])
-        prepare(xia[j], xib[j], *here, wm)
+        inner = ny - 2 * H
+        got = [x[j * inner : (j + 1) * inner] for x in (xia, xib)]
+        prepare(*got, *here, wm)
         for i in range(half):
             sums = own_sums(us.at[j], ul.at[j], band_s, band_l, i)
             for at, col in ((i, slice(0, nz)), (i + half, slice(nz, 2 * nz))):
@@ -303,17 +303,31 @@
         copy.wait()
 
 
-def final_body(low, xia, xib, acc_s, acc_l, ws, wl, eff, ya, yb, es, el, _, out, us, ul, rim, done, sems):
+def final_body(low, xia, xib, xja, xjb, acc_s, acc_l, ws, wl, eff, ya, yb, es, el, _, out, us, ul, rim, done, sems):
     n, nx, ny, nz = us.shape
     half = nx // 2
     wm, w = band(False), ends_band()
     band_s, band_l = rows_band(R_SMALL, ny), rows_band(R_LARGE, ny)
     sides = ((0, slice(0, nz)), (half, slice(nz, 2 * nz)))
     copies = []
+    for s in range(low):
+        for i in range(half):
+            more = halo_sums(ya, yb, s, i, half, w)
+            for step, col in sides:
+                at = i + step
+                add_s, add_l = more[0 : 2 * H, col], more[2 * H :, col]
+                rim[s, at] = level(es[s, at] + add_s, el[s, at] + add_l, rim_rows(eff[at]))
+        for k, start in enumerate((0, ny - H)):
+            source = rim.at[s, :, pl.ds(k * H, H), :]
+            target = out.at[s, :, pl.ds(start, H), :]
+            copies.append(pltpu.make_async_copy(source, target, sems.at[len(copies)]))
+            copies[-1].start()
     for j in range(n):
         s = low + j
         here = (acc_s.at[s], acc_l.at[s], ws.at[s], wl.at[s], us.at[j], ul.at[j])
-        prepare(xia[j], xib[j], *here, wm)
+        kept = low * (ny - 2 * H)
+        got = [jnp.concatenate([x[kept:], y[...]], axis=0) for x, y in ((xia, xja), (xib, xjb))]
+        prepare(*got, *here, wm)
         for i in range(half):
             sums = own_sums(us.at[j], ul.at[j], band_s, band_l, i)
             more = halo_sums(ya, yb, s, i, half, w)
@@ -326,20 +340,15 @@
                 ends = level(rim_rows(small) + add_s, rim_rows(large) + add_l, rim_rows(eff[at]))
                 done[j, at, 0:H] = ends[0:H]
                 done[j, at, ny - H :] = ends[H:]
-        copies.append(pltpu.make_async_copy(done.at[j], out.at[s], sems.at[len(copies)]))
-        copies[-1].start()
-    for s in range(low):
-        for i in range(half):
-            more = halo_sums(ya, yb, s, i, half, w)
-            for step, col in sides:
-                at = i + step
-                add_s, add_l = more[0 : 2 * H, col], more[2 * H :, col]
-                rim[s, at] = level(es[s, at] + add_s, el[s, at] + add_l, rim_rows(eff[at]))
-        for k, start in enumerate((0, ny - H)):
-            source = rim.at[s, :, pl.ds(k * H, H), :]
-            target = out.at[s, :, pl.ds(start, H), :]
-            copies.append(pltpu.make_async_copy(source, target, sems.at[len(copies)]))
-            copies[-1].start()
+            if i % 2:
+                for step, _ in sides:
+                    some = pl.ds(i - 1 + step, 2)
+                    copies.append(
+                        pltpu.make_async_copy(
+                            done.at[j, some], out.at[s, some], sems.at[len(copies)]
+                        )
+                    )
+                    copies[-1].start()
     for copy in copies:
         copy.wait()
 
@@ -348,7 +357,7 @@
     _, nx, ny, nz = shape
     ends = (high, nx, 2 * H, nz)
     return pl.pallas_call(
-        lambda *refs: inner_body(0, *refs),
+        inner_body,
         out_shape=[jax.ShapeDtypeStruct(shape, F32), pltpu.VMEM(ends, F32), pltpu.VMEM(ends, F32)],
         in_specs=[VMEM] * len(args),
         out_specs=[pl.BlockSpec(memory_space=pl.ANY), VMEM, VMEM],
@@ -370,7 +379,7 @@
         out_specs=any_space,
         scratch_shapes=[pltpu.VMEM((n, nx, ny, nz), F32)] * 2
         + [pltpu.VMEM((low, nx, 2 * H, nz), F32), pltpu.VMEM((n, nx, ny, nz), F32)]
-        + [pltpu.SemaphoreType.DMA((n + 2 * low,))],
+        + [pltpu.SemaphoreType.DMA((n * nx // 2 + 2 * low,))],
         input_output_aliases={len(args): 0},
         compiler_params=PARAMS,
         name="final",
@@ -391,25 +400,24 @@
     snaps, nx, ny, nz = block
     inner = ny - 2 * H
     zpack = (snaps, ny, nz)
-    xe = (snaps, H, 2 * H, nz)
+    xe = (2 * snaps * H, H, nz)
     own, zr, zl, xeu, xed = pl.pallas_call(
         pack_body,
         out_shape=[pltpu.VMEM(s, F32) for s in (block, zpack, zpack, xe, xe)],
         in_specs=[pl.BlockSpec(memory_space=pl.ANY)],
         out_specs=[VMEM] * 5,
-        scratch_shapes=[pltpu.SemaphoreType.DMA((snaps * nx // H,))],
+        scratch_shapes=[pltpu.SemaphoreType.DMA((snaps,))],
         compiler_params=PARAMS,
         name="pack",
     )(pltpu.with_memory_space_constraint(density, pltpu.HBM))
     za, zb = both("gz", zr, zl)
     xea, xeb = both("gx", xeu, xed)
-    slabs = []
-    for low, high in CHUNKS:
-        slabs += [(high - low, H, inner, nz)] * 2
+    blocks = (snaps * inner - LATE * H, LATE * H)
+    slabs = [(n, H, nz) for n in blocks for _ in (0, 1)]
     slabs = run(slab_body, (own,), slabs)
     xzu, xzd = run(second_body, (za, zb), (zpack, zpack))
     xza, xzb = both("gx", xzu, xzd)
-    halos = [both("gx", *slabs[2 * c : 2 * c + 2]) for c in range(len(CHUNKS))]
+    halos = [both("gx", *slabs[2 * c : 2 * c + 2]) for c in (0, 1)]
     wide = nx + 2 * H
     rim = [(snaps, nx, 2 * H, nz)] * 2 + [(snaps, nx + nx // 2, H, nz)] * 2
     ws, wl, yu, yd = run(rim_body, (own, xea, xeb, xza, xzd, xzu, xzb), rim)
@@ -421,9 +429,8 @@
         [pltpu.VMEM((snaps, wide, inner, nz), F32)] * 2,
     )
     shared = (acc_s, acc_l, ws, wl, efficiency)
-    (_, split_at), _ = CHUNKS
-    out, es, el = inner_call(split_at, halos[0] + shared, block)
-    out = final_call(split_at, halos[1] + shared + (ya, yb, es, el), out, block)
+    out, es, el = inner_call(snaps - 1, halos[0] + shared, block)
+    out = final_call(snaps - 1, halos[0] + halos[1] + shared + (ya, yb, es, el), out, block)
     return out
 
 

time: 45.2 us -> 45.6 us (level)
  the two profiles are of different devices: /device:TPU:56 before, /device:TPU:1 now
where the time goes in v4:
time: 45.6 us
  starting transfers between devices  23.6 us (52%)
  waiting for transfers between devices  12.6 us (28%)
  Pallas kernels  9.02 us (20%)
    ppermute x12, starting transfers between devices, shift(): return lax.ppermute(block, axis, [(i, (i + step) % n) for i in range(n)])  23.6 us
    ppermute x12, waiting for transfers between devices, shift(): return lax.ppermute(block, axis, [(i, (i + step) % n) for i in range(n)])  12.6 us
    pallas_call x4, Pallas kernels, run(): pl.pallas_call(body, out_shape=[pltpu.VMEM(s, F32) for s in outs], in_spe...  3.59 us
    pallas_call x1, Pallas kernels, inner_call(): pl.pallas_call(inner_body, out_shape=[jax.ShapeDtypeStruct(shape, F32), p...  1.95 us
    pallas_call x1, Pallas kernels, steps(): pl.pallas_call(pack_body, out_shape=[pltpu.VMEM(s, F32) for s in (block,...  1.88 us
    pallas_call x1, Pallas kernels, final_call(): pl.pallas_call(lambda *refs: final_body(low, *refs), out_shape=jax.ShapeD...  1.61 us
  transfers between devices with their start and end apart: 12, of which 3 were waited for; matrix products, arithmetic and copies ran while one was open for 0% of the time, Pallas kernels for 12%

profile of v4, /device:TPU:1, one launch (start us, length us, event | category | flops | bytes accessed | tf_op | source)
XLA Modules:
  0.0 45.6 jit_solution(16336321753213952480)
XLA Ops:
  0.0 1.9 %pack.1 = (f32[3,16,64,128]{3,2,1,0:T(8,128)S(1)}, f32[3,64,128]{2,1,0:T(8,128)S(1)}, f32[3,64,128]{2,1,0:T(8,128)S(1)}, f32[48,8,128]{2,1,0:T(8,128)S(1)}, f32[48,8,128]{2,1,0:T(8,128)S(1)}) custom-call(f32[3,16,64,128]{3,2,1,0:T(8,128)} %d_hbm.1), custom_call_target="tpu_custom_call" | custom-call | tf_op jit(solution)/shard_map/pack/pallas_call | solution.py:404
  1.9 2.2 %collective-permute-start.4 = (f32[3,64,128]{2,1,0:T(8,128)S(1)}, f32[3,64,128]{2,1,0:T(8,128)S(1)}, u32[]{:S(2)}, u32[]{:S(2)}) collective-permute-start(f32[3,64,128]{2,1,0:T(8,128)S(1)} %get-tuple-element.30), channel_id=1, source_target_pairs={{0,1},{1,2},{2,3},{3,4},{4,5},{5,6},{6,7},{7,0},{8,9},{9,10},{10,1... | collective-permute-start | bytes 294920 | tf_op jit(solution)/shard_map/ppermute | solution.py:391
  4.1 2.5 %collective-permute-start.5 = (f32[3,64,128]{2,1,0:T(8,128)S(1)}, f32[3,64,128]{2,1,0:T(8,128)S(1)}, u32[]{:S(2)}, u32[]{:S(2)}) collective-permute-start(f32[3,64,128]{2,1,0:T(8,128)S(1)} %get-tuple-element.31), channel_id=1, source_target_pairs={{0,7},{1,0},{2,1},{3,2},{4,3},{5,4},{6,5},{7,6},{8,15},{9,8},{10,9... | collective-permute-start | bytes 294920 | tf_op jit(solution)/shard_map/ppermute | solution.py:391
  6.5 0.1 shard_map.28
  6.6 1.7 %collective-permute-start = (f32[120,8,128]{2,1,0:T(8,128)S(1)}, f32[120,8,128]{2,1,0:T(8,128)S(1)}, u32[]{:S(2)}, u32[]{:S(2)}) collective-permute-start(f32[120,8,128]{2,1,0:T(8,128)S(1)} %get-tuple-element.26), channel_id=1, source_target_pairs={{0,32},{32,64},{64,96},{96,128},{128,160},{160,192},{192,224},{224... | collective-permute-start | bytes 1474568 | tf_op jit(solution)/shard_map/ppermute | solution.py:391
  8.3 4.0 %collective-permute-start.1 = (f32[120,8,128]{2,1,0:T(8,128)S(1)}, f32[120,8,128]{2,1,0:T(8,128)S(1)}, u32[]{:S(2)}, u32[]{:S(2)}) collective-permute-start(f32[120,8,128]{2,1,0:T(8,128)S(1)} %get-tuple-element.27), channel_id=1, source_target_pairs={{0,224},{32,0},{64,32},{96,64},{128,96},{160,128},{192,160},{224,1... | collective-permute-start | bytes 1474568 | tf_op jit(solution)/shard_map/ppermute | solution.py:391
  12.4 0.0 collective-permute-done.4.za
  12.4 0.0 collective-permute-done.5.zb
  12.4 0.1 shard_map.29
  12.5 0.1 collective-permute-start.6
  12.6 0.1 collective-permute-start.8
  12.7 2.7 %collective-permute-start.9 = (f32[48,8,128]{2,1,0:T(8,128)S(1)}, f32[48,8,128]{2,1,0:T(8,128)S(1)}, u32[]{:S(2)}, u32[]{:S(2)}) collective-permute-start(f32[48,8,128]{2,1,0:T(8,128)S(1)} %get-tuple-element.37), channel_id=1, source_target_pairs={{0,224},{32,0},{64,32},{96,64},{128,96},{160,128},{192,160},{224,1... | collective-permute-start | bytes 589832 | tf_op jit(solution)/shard_map/ppermute | solution.py:391
  15.3 9.6 %collective-permute-done.6.xza = f32[3,64,128]{2,1,0:T(8,128)S(1)} collective-permute-done((f32[3,64,128]{2,1,0:T(8,128)S(1)}, f32[3,64,128]{2,1,0:T(8,128)S(1)}, u32[]{:S(2)}, u32[]{:S(2)}) %collective-permute-start.6) | collective-permute-done | bytes 98336 | tf_op jit(solution)/shard_map/ppermute | solution.py:391
  24.9 1.2 %collective-permute-start.7 = (f32[3,64,128]{2,1,0:T(8,128)S(1)}, f32[3,64,128]{2,1,0:T(8,128)S(1)}, u32[]{:S(2)}, u32[]{:S(2)}) collective-permute-start(f32[3,64,128]{2,1,0:T(8,128)S(1)} %get-tuple-element.33.xzd), channel_id=1, source_target_pairs={{0,224},{32,0},{64,32},{96,64},{128,96},{160,128},{192,160},{224,1... | collective-permute-start | bytes 294920 | tf_op jit(solution)/shard_map/ppermute | solution.py:391
  26.1 2.6 %collective-permute-done.7.xzb = f32[3,64,128]{2,1,0:T(8,128)S(1)} collective-permute-done((f32[3,64,128]{2,1,0:T(8,128)S(1)}, f32[3,64,128]{2,1,0:T(8,128)S(1)}, u32[]{:S(2)}, u32[]{:S(2)}) %collective-permute-start.7) | collective-permute-done | bytes 98336 | tf_op jit(solution)/shard_map/ppermute | solution.py:391
  28.7 0.4 collective-permute-done.8.xea
  29.1 0.0 collective-permute-done.9.xeb
  29.1 1.0 %shard_map.31 = (f32[3,16,16,128]{3,2,1,0:T(8,128)S(1)}, f32[3,16,16,128]{3,2,1,0:T(8,128)S(1)}, f32[3,24,8,128]{3,2,1,0:T(8,128)S(1)}, f32[3,24,8,128]{3,2,1,0:T(8,128)S(1)}) custom-call(f32[3,16,64,128]{3,2,1,0:T(8,128)S(1)} %get-tuple-element.25.d, f32[48,8,128]{2,1,0:T(8,128)S(1)} %collective-permute-done.8.xea, ...), custom_call_target="tpu_custom_call" | custom-call | tf_op jit(solution)/shard_map/pallas_call | solution.py:36
  30.1 0.0 copy-start
  30.1 6.0 %collective-permute-start.10 = (f32[3,24,8,128]{3,2,1,0:T(8,128)S(1)}, f32[3,24,8,128]{3,2,1,0:T(8,128)S(1)}, u32[]{:S(2)}, u32[]{:S(2)}) collective-permute-start(f32[3,24,8,128]{3,2,1,0:T(8,128)S(1)} %get-tuple-element.40), channel_id=1, source_target_pairs={{0,8},{8,16},{16,24},{24,0},{1,9},{9,17},{17,25},{25,1},{2,10},{10... | collective-permute-start | bytes 884744 | tf_op jit(solution)/shard_map/ppermute | solution.py:391
  36.1 0.0 collective-permute-start.11
  36.1 0.0 collective-permute-start.2
  36.1 0.0 collective-permute-done.xia.refs_0_
  36.1 3.2 %collective-permute-start.3 = (f32[24,8,128]{2,1,0:T(8,128)S(1)}, f32[24,8,128]{2,1,0:T(8,128)S(1)}, u32[]{:S(2)}, u32[]{:S(2)}) collective-permute-start(f32[24,8,128]{2,1,0:T(8,128)S(1)} %get-tuple-element.29), channel_id=1, source_target_pairs={{0,224},{32,0},{64,32},{96,64},{128,96},{160,128},{192,160},{224,1... | collective-permute-start | bytes 294920 | tf_op jit(solution)/shard_map/ppermute | solution.py:391
  39.3 2.4 %shard_map.30 = (f32[3,16,48,128]{3,2,1,0:T(8,128)S(1)}, f32[3,16,48,128]{3,2,1,0:T(8,128)S(1)}) custom-call(f32[3,16,64,128]{3,2,1,0:T(8,128)S(1)} %get-tuple-element.25.d, f32[3,64,128]{2,1,0:T(8,128)S(1)} %collective-permute-done.6.xza, f32[3,64,128]{2,1,0:T(8,128)S(1)} %get-tuple-element.33.xzd, f32[3,64,128]{2,1,0:T(8,128)S(1)} %get-tuple-element.32.xzu, ...), custom_call_target="tpu_custom_call" | custom-call | tf_op jit(solution)/shard_map/pallas_call | solution.py:36
  41.8 0.0 collective-permute-done.1.xib.refs_1_
  41.8 0.0 copy-done
  41.8 1.9 %inner.1 = (f32[3,16,64,128]{3,2,1,0:T(8,128)}, f32[2,16,16,128]{3,2,1,0:T(8,128)S(1)}, f32[2,16,16,128]{3,2,1,0:T(8,128)S(1)}) custom-call(f32[120,8,128]{2,1,0:T(8,128)S(1)} %collective-permute-done.xia.refs_0_, f32[120,8,128]{2,1,0:T(8,128)S(1)} %collective-permute-done.1.xib.refs_1_, f32[3,16,48,128]{3,2,1,0:T(8,128)S(1)} %get-tuple-element.34.acc_s.refs_4_, ...), custom_call_target="tpu_custom_call" | custom-call | tf_op jit(solution)/shard_map/inner/pallas_call | solution.py:359
  43.7 0.0 collective-permute-done.2.refs_2_
  43.8 0.0 collective-permute-done.3.refs_3_
  43.8 0.0 collective-permute-done.10.refs_9_
  43.8 0.0 collective-permute-done.11.refs_10_
  43.8 1.6 %final.1 = f32[3,16,64,128]{3,2,1,0:T(8,128)} custom-call(f32[120,8,128]{2,1,0:T(8,128)S(1)} %collective-permute-done.xia.refs_0_, f32[120,8,128]{2,1,0:T(8,128)S(1)} %collective-permute-done.1.xib.refs_1_, f32[24,8,128]{2,1,0:T(8,128)S(1)} %collective-permute-done.2.refs_2_, ...), custom_call_target="tpu_custom_call", output_to_operand_aliasing={{}: (13, {})} | custom-call | tf_op jit(solution)/shard_map/final/pallas_call | solution.py:375
Async XLA Ops:
  1.9 10.5 %collective-permute-start.4 = (f32[3,64,128]{2,1,0:T(8,128)S(1)}, f32[3,64,128]{2,1,0:T(8,128)S(1)}, u32[]{:S(2)}, u32[]{:S(2)}) collective-permute-start(f32[3,64,128]{2,1,0:T(8,128)S(1)} %get-tuple-element.30), channel_id=1, source_target_pairs={{0,1},{1,2},{2,3},{3,4},{4,5},{5,6},{6,7},{7,0},{8,9},{9,10},{10,1... | collective-permute-start | bytes 294920 | tf_op jit(solution)/shard_map/ppermute | solution.py:391
  4.1 8.3 %collective-permute-start.5 = (f32[3,64,128]{2,1,0:T(8,128)S(1)}, f32[3,64,128]{2,1,0:T(8,128)S(1)}, u32[]{:S(2)}, u32[]{:S(2)}) collective-permute-start(f32[3,64,128]{2,1,0:T(8,128)S(1)} %get-tuple-element.31), channel_id=1, source_target_pairs={{0,7},{1,0},{2,1},{3,2},{4,3},{5,4},{6,5},{7,6},{8,15},{9,8},{10,9... | collective-permute-start | bytes 294920 | tf_op jit(solution)/shard_map/ppermute | solution.py:391
  6.6 29.5 %collective-permute-start = (f32[120,8,128]{2,1,0:T(8,128)S(1)}, f32[120,8,128]{2,1,0:T(8,128)S(1)}, u32[]{:S(2)}, u32[]{:S(2)}) collective-permute-start(f32[120,8,128]{2,1,0:T(8,128)S(1)} %get-tuple-element.26), channel_id=1, source_target_pairs={{0,32},{32,64},{64,96},{96,128},{128,160},{160,192},{192,224},{224... | collective-permute-start | bytes 1474568 | tf_op jit(solution)/shard_map/ppermute | solution.py:391
  8.3 33.4 %collective-permute-start.1 = (f32[120,8,128]{2,1,0:T(8,128)S(1)}, f32[120,8,128]{2,1,0:T(8,128)S(1)}, u32[]{:S(2)}, u32[]{:S(2)}) collective-permute-start(f32[120,8,128]{2,1,0:T(8,128)S(1)} %get-tuple-element.27), channel_id=1, source_target_pairs={{0,224},{32,0},{64,32},{96,64},{128,96},{160,128},{192,160},{224,1... | collective-permute-start | bytes 1474568 | tf_op jit(solution)/shard_map/ppermute | solution.py:391
  12.5 12.4 %collective-permute-start.6 = (f32[3,64,128]{2,1,0:T(8,128)S(1)}, f32[3,64,128]{2,1,0:T(8,128)S(1)}, u32[]{:S(2)}, u32[]{:S(2)}) collective-permute-start(f32[3,64,128]{2,1,0:T(8,128)S(1)} %get-tuple-element.32.xzu), channel_id=1, source_target_pairs={{0,32},{32,64},{64,96},{96,128},{128,160},{160,192},{192,224},{224... | collective-permute-start | bytes 294920 | tf_op jit(solution)/shard_map/ppermute | solution.py:391
  12.6 16.5 %collective-permute-start.8 = (f32[48,8,128]{2,1,0:T(8,128)S(1)}, f32[48,8,128]{2,1,0:T(8,128)S(1)}, u32[]{:S(2)}, u32[]{:S(2)}) collective-permute-start(f32[48,8,128]{2,1,0:T(8,128)S(1)} %get-tuple-element.36), channel_id=1, source_target_pairs={{0,32},{32,64},{64,96},{96,128},{128,160},{160,192},{192,224},{224... | collective-permute-start | bytes 589832 | tf_op jit(solution)/shard_map/ppermute | solution.py:391
  12.7 16.5 %collective-permute-start.9 = (f32[48,8,128]{2,1,0:T(8,128)S(1)}, f32[48,8,128]{2,1,0:T(8,128)S(1)}, u32[]{:S(2)}, u32[]{:S(2)}) collective-permute-start(f32[48,8,128]{2,1,0:T(8,128)S(1)} %get-tuple-element.37), channel_id=1, source_target_pairs={{0,224},{32,0},{64,32},{96,64},{128,96},{160,128},{192,160},{224,1... | collective-permute-start | bytes 589832 | tf_op jit(solution)/shard_map/ppermute | solution.py:391
  24.9 3.8 %collective-permute-start.7 = (f32[3,64,128]{2,1,0:T(8,128)S(1)}, f32[3,64,128]{2,1,0:T(8,128)S(1)}, u32[]{:S(2)}, u32[]{:S(2)}) collective-permute-start(f32[3,64,128]{2,1,0:T(8,128)S(1)} %get-tuple-element.33.xzd), channel_id=1, source_target_pairs={{0,224},{32,0},{64,32},{96,64},{128,96},{160,128},{192,160},{224,1... | collective-permute-start | bytes 294920 | tf_op jit(solution)/shard_map/ppermute | solution.py:391
  30.1 11.7 %copy-start = (f32[16,64,128]{2,1,0:T(8,128)S(1)}, f32[16,64,128]{2,1,0:T(8,128)}, u32[]{:S(2)}) copy-start(f32[16,64,128]{2,1,0:T(8,128)} %refs_8_.1) | copy-start | bytes 1572868
  30.1 13.7 %collective-permute-start.10 = (f32[3,24,8,128]{3,2,1,0:T(8,128)S(1)}, f32[3,24,8,128]{3,2,1,0:T(8,128)S(1)}, u32[]{:S(2)}, u32[]{:S(2)}) collective-permute-start(f32[3,24,8,128]{3,2,1,0:T(8,128)S(1)} %get-tuple-element.40), channel_id=1, source_target_pairs={{0,8},{8,16},{16,24},{24,0},{1,9},{9,17},{17,25},{25,1},{2,10},{10... | collective-permute-start | bytes 884744 | tf_op jit(solution)/shard_map/ppermute | solution.py:391
  36.1 7.7 %collective-permute-start.11 = (f32[3,24,8,128]{3,2,1,0:T(8,128)S(1)}, f32[3,24,8,128]{3,2,1,0:T(8,128)S(1)}, u32[]{:S(2)}, u32[]{:S(2)}) collective-permute-start(f32[3,24,8,128]{3,2,1,0:T(8,128)S(1)} %get-tuple-element.41), channel_id=1, source_target_pairs={{0,24},{8,0},{16,8},{24,16},{1,25},{9,1},{17,9},{25,17},{2,26},{10... | collective-permute-start | bytes 884744 | tf_op jit(solution)/shard_map/ppermute | solution.py:391
  36.1 7.6 %collective-permute-start.2 = (f32[24,8,128]{2,1,0:T(8,128)S(1)}, f32[24,8,128]{2,1,0:T(8,128)S(1)}, u32[]{:S(2)}, u32[]{:S(2)}) collective-permute-start(f32[24,8,128]{2,1,0:T(8,128)S(1)} %get-tuple-element.28), channel_id=1, source_target_pairs={{0,32},{32,64},{64,96},{96,128},{128,160},{160,192},{192,224},{224... | collective-permute-start | bytes 294920 | tf_op jit(solution)/shard_map/ppermute | solution.py:391
  36.1 7.6 %collective-permute-start.3 = (f32[24,8,128]{2,1,0:T(8,128)S(1)}, f32[24,8,128]{2,1,0:T(8,128)S(1)}, u32[]{:S(2)}, u32[]{:S(2)}) collective-permute-start(f32[24,8,128]{2,1,0:T(8,128)S(1)} %get-tuple-element.29), channel_id=1, source_target_pairs={{0,224},{32,0},{64,32},{96,64},{128,96},{160,128},{192,160},{224,1... | collective-permute-start | bytes 294920 | tf_op jit(solution)/shard_map/ppermute | solution.py:391

commit v5 on v4

--- a/solution.py
+++ b/solution.py
@@ -276,13 +276,12 @@
         ref[:, ny - H :] = w[:, H:]
 
 
-def inner_body(xia, xib, acc_s, acc_l, ws, wl, eff, out, es, el, us, ul, done, sems):
+def inner_body(xia, xib, acc_s, acc_l, ws, wl, eff, done, es, el, us, ul):
     n, nx, ny, nz = us.shape
     half = nx // 2
     rows = slice(H, ny - H)
     wm = band(False)
     band_s, band_l = rows_band(R_SMALL, ny), rows_band(R_LARGE, ny)
-    copies = []
     for j in range(n):
         s = j
         here = (acc_s.at[s], acc_l.at[s], ws.at[s], wl.at[s], us.at[j], ul.at[j])
@@ -296,20 +295,19 @@
                 done[j, at] = level(small[rows], large[rows], eff[at, rows])
                 es[j, at] = rim_rows(small)
                 el[j, at] = rim_rows(large)
-        copy = pltpu.make_async_copy(done.at[j], out.at[s, :, pl.ds(H, ny - 2 * H), :], sems.at[j])
-        copy.start()
-        copies.append(copy)
-    for copy in copies:
-        copy.wait()
-
-
-def final_body(low, xia, xib, xja, xjb, acc_s, acc_l, ws, wl, eff, ya, yb, es, el, _, out, us, ul, rim, done, sems):
+
+
+def final_body(low, xia, xib, xja, xjb, acc_s, acc_l, ws, wl, eff, ya, yb, kept_rows, es, el, out, us, ul, rim, done, sems):
     n, nx, ny, nz = us.shape
     half = nx // 2
     wm, w = band(False), ends_band()
     band_s, band_l = rows_band(R_SMALL, ny), rows_band(R_LARGE, ny)
     sides = ((0, slice(0, nz)), (half, slice(nz, 2 * nz)))
     copies = []
+    for s in range(low):
+        target = out.at[s, :, pl.ds(H, ny - 2 * H), :]
+        copies.append(pltpu.make_async_copy(kept_rows.at[s], target, sems.at[len(copies)]))
+        copies[-1].start()
     for s in range(low):
         for i in range(half):
             more = halo_sums(ya, yb, s, i, half, w)
@@ -355,35 +353,24 @@
 
 def inner_call(high, args, shape):
     _, nx, ny, nz = shape
-    ends = (high, nx, 2 * H, nz)
-    return pl.pallas_call(
-        inner_body,
-        out_shape=[jax.ShapeDtypeStruct(shape, F32), pltpu.VMEM(ends, F32), pltpu.VMEM(ends, F32)],
-        in_specs=[VMEM] * len(args),
-        out_specs=[pl.BlockSpec(memory_space=pl.ANY), VMEM, VMEM],
-        scratch_shapes=[pltpu.VMEM((high, nx, ny, nz), F32)] * 2
-        + [pltpu.VMEM((high, nx, ny - 2 * H, nz), F32), pltpu.SemaphoreType.DMA((high,))],
-        compiler_params=PARAMS,
-        name="inner",
-    )(*[near(a) for a in args])
-
-
-def final_call(low, args, before, shape):
+    outs = [(high, nx, ny - 2 * H, nz)] + [(high, nx, 2 * H, nz)] * 2
+    return run(inner_body, args, outs, [pltpu.VMEM((high, nx, ny, nz), F32)] * 2)
+
+
+def final_call(low, args, shape):
     snaps, nx, ny, nz = shape
     n = snaps - low
-    any_space = pl.BlockSpec(memory_space=pl.ANY)
     return pl.pallas_call(
         lambda *refs: final_body(low, *refs),
         out_shape=jax.ShapeDtypeStruct(shape, F32),
-        in_specs=[VMEM] * len(args) + [any_space],
-        out_specs=any_space,
+        in_specs=[VMEM] * len(args),
+        out_specs=pl.BlockSpec(memory_space=pl.ANY),
         scratch_shapes=[pltpu.VMEM((n, nx, ny, nz), F32)] * 2
         + [pltpu.VMEM((low, nx, 2 * H, nz), F32), pltpu.VMEM((n, nx, ny, nz), F32)]
-        + [pltpu.SemaphoreType.DMA((n * nx // 2 + 2 * low,))],
-        input_output_aliases={len(args): 0},
+        + [pltpu.SemaphoreType.DMA((n * nx // 2 + 3 * low,))],
         compiler_params=PARAMS,
         name="final",
-    )(*[near(a) for a in args], before)
+    )(*[near(a) for a in args])
 
 
 def shift(block, axis, step):
@@ -429,8 +416,8 @@
         [pltpu.VMEM((snaps, wide, inner, nz), F32)] * 2,
     )
     shared = (acc_s, acc_l, ws, wl, efficiency)
-    out, es, el = inner_call(snaps - 1, halos[0] + shared, block)
-    out = final_call(snaps - 1, halos[0] + halos[1] + shared + (ya, yb, es, el), out, block)
+    ready = inner_call(snaps - 1, halos[0] + shared, block)
+    out = final_call(snaps - 1, halos[0] + halos[1] + shared + (ya, yb, *ready), block)
     return out
 
 

time: 45.6 us -> 45.6 us (level)
  waiting for transfers between devices: 12.6 us -> 13.4 us
  Pallas kernels: 9.02 us -> 8.28 us
    pallas_call x1 -> x0, Pallas kernels: 1.95 us -> none  [inner_call(): pl.pallas_call(inner_body, out_shape=[jax.ShapeDtypeStruct(shape, F32), p...]
    pallas_call x4 -> x5, Pallas kernels: 3.59 us -> 4.79 us  [run(): pl.pallas_call(body, out_shape=[pltpu.VMEM(s, F32) for s in outs], in_spe...]
    ppermute x12, waiting for transfers between devices: 12.6 us -> 13.4 us  [shift(): return lax.ppermute(block, axis, [(i, (i + step) % n) for i in range(n)])]
  transfers between devices with their start and end apart: 12 -> 12, of which waited for: 3 -> 4; matrix products, arithmetic and copies ran while one was open for 0% -> 0% of each run, Pallas kernels for 12% -> 11%
where the time goes in v5:
time: 45.6 us; the launch traced here: 45.5 us
  starting transfers between devices  23.6 us (52%)
  waiting for transfers between devices  13.4 us (29%)
  Pallas kernels  8.28 us (18%)
    ppermute x12, starting transfers between devices, shift(): return lax.ppermute(block, axis, [(i, (i + step) % n) for i in range(n)])  23.6 us
    ppermute x12, waiting for transfers between devices, shift(): return lax.ppermute(block, axis, [(i, (i + step) % n) for i in range(n)])  13.4 us
    pallas_call x5, Pallas kernels, run(): pl.pallas_call(body, out_shape=[pltpu.VMEM(s, F32) for s in outs], in_spe...  4.79 us
    pallas_call x1, Pallas kernels, steps(): pl.pallas_call(pack_body, out_shape=[pltpu.VMEM(s, F32) for s in (block,...  1.88 us
    pallas_call x1, Pallas kernels, final_call(): pl.pallas_call(lambda *refs: final_body(low, *refs), out_shape=jax.ShapeD...  1.62 us
  transfers between devices with their start and end apart: 12, of which 4 were waited for; matrix products, arithmetic and copies ran while one was open for 0% of the time, Pallas kernels for 11%

profile of v5, /device:TPU:1, one launch (start us, length us, event | category | flops | bytes accessed | tf_op | source)
XLA Modules:
  0.0 45.5 jit_solution(8068080141332654696)
XLA Ops:
  0.0 1.9 %pack.1 = (f32[3,16,64,128]{3,2,1,0:T(8,128)S(1)}, f32[3,64,128]{2,1,0:T(8,128)S(1)}, f32[3,64,128]{2,1,0:T(8,128)S(1)}, f32[48,8,128]{2,1,0:T(8,128)S(1)}, f32[48,8,128]{2,1,0:T(8,128)S(1)}) custom-call(f32[3,16,64,128]{3,2,1,0:T(8,128)} %d_hbm.1), custom_call_target="tpu_custom_call" | custom-call | tf_op jit(solution)/shard_map/pack/pallas_call | solution.py:391
  1.9 2.2 %collective-permute-start.4 = (f32[3,64,128]{2,1,0:T(8,128)S(1)}, f32[3,64,128]{2,1,0:T(8,128)S(1)}, u32[]{:S(2)}, u32[]{:S(2)}) collective-permute-start(f32[3,64,128]{2,1,0:T(8,128)S(1)} %get-tuple-element.30), channel_id=1, source_target_pairs={{0,1},{1,2},{2,3},{3,4},{4,5},{5,6},{6,7},{7,0},{8,9},{9,10},{10,1... | collective-permute-start | bytes 294920 | tf_op jit(solution)/shard_map/ppermute | solution.py:378
  4.1 2.5 %collective-permute-start.5 = (f32[3,64,128]{2,1,0:T(8,128)S(1)}, f32[3,64,128]{2,1,0:T(8,128)S(1)}, u32[]{:S(2)}, u32[]{:S(2)}) collective-permute-start(f32[3,64,128]{2,1,0:T(8,128)S(1)} %get-tuple-element.31), channel_id=1, source_target_pairs={{0,7},{1,0},{2,1},{3,2},{4,3},{5,4},{6,5},{7,6},{8,15},{9,8},{10,9... | collective-permute-start | bytes 294920 | tf_op jit(solution)/shard_map/ppermute | solution.py:378
  6.5 0.1 shard_map.28
  6.6 1.7 %collective-permute-start = (f32[120,8,128]{2,1,0:T(8,128)S(1)}, f32[120,8,128]{2,1,0:T(8,128)S(1)}, u32[]{:S(2)}, u32[]{:S(2)}) collective-permute-start(f32[120,8,128]{2,1,0:T(8,128)S(1)} %get-tuple-element.26), channel_id=1, source_target_pairs={{0,32},{32,64},{64,96},{96,128},{128,160},{160,192},{192,224},{224... | collective-permute-start | bytes 1474568 | tf_op jit(solution)/shard_map/ppermute | solution.py:378
  8.3 4.0 %collective-permute-start.1 = (f32[120,8,128]{2,1,0:T(8,128)S(1)}, f32[120,8,128]{2,1,0:T(8,128)S(1)}, u32[]{:S(2)}, u32[]{:S(2)}) collective-permute-start(f32[120,8,128]{2,1,0:T(8,128)S(1)} %get-tuple-element.27), channel_id=1, source_target_pairs={{0,224},{32,0},{64,32},{96,64},{128,96},{160,128},{192,160},{224,1... | collective-permute-start | bytes 1474568 | tf_op jit(solution)/shard_map/ppermute | solution.py:378
  12.4 0.0 collective-permute-done.4.za
  12.4 0.0 collective-permute-done.5.zb
  12.4 0.1 shard_map.29
  12.5 0.1 collective-permute-start.6
  12.6 0.1 collective-permute-start.8
  12.7 2.7 %collective-permute-start.9 = (f32[48,8,128]{2,1,0:T(8,128)S(1)}, f32[48,8,128]{2,1,0:T(8,128)S(1)}, u32[]{:S(2)}, u32[]{:S(2)}) collective-permute-start(f32[48,8,128]{2,1,0:T(8,128)S(1)} %get-tuple-element.37), channel_id=1, source_target_pairs={{0,224},{32,0},{64,32},{96,64},{128,96},{160,128},{192,160},{224,1... | collective-permute-start | bytes 589832 | tf_op jit(solution)/shard_map/ppermute | solution.py:378
  15.3 9.6 %collective-permute-done.6.xza = f32[3,64,128]{2,1,0:T(8,128)S(1)} collective-permute-done((f32[3,64,128]{2,1,0:T(8,128)S(1)}, f32[3,64,128]{2,1,0:T(8,128)S(1)}, u32[]{:S(2)}, u32[]{:S(2)}) %collective-permute-start.6) | collective-permute-done | bytes 98336 | tf_op jit(solution)/shard_map/ppermute | solution.py:378
  24.9 1.2 %collective-permute-start.7 = (f32[3,64,128]{2,1,0:T(8,128)S(1)}, f32[3,64,128]{2,1,0:T(8,128)S(1)}, u32[]{:S(2)}, u32[]{:S(2)}) collective-permute-start(f32[3,64,128]{2,1,0:T(8,128)S(1)} %get-tuple-element.33.xzd), channel_id=1, source_target_pairs={{0,224},{32,0},{64,32},{96,64},{128,96},{160,128},{192,160},{224,1... | collective-permute-start | bytes 294920 | tf_op jit(solution)/shard_map/ppermute | solution.py:378
  26.1 2.6 %collective-permute-done.7.xzb = f32[3,64,128]{2,1,0:T(8,128)S(1)} collective-permute-done((f32[3,64,128]{2,1,0:T(8,128)S(1)}, f32[3,64,128]{2,1,0:T(8,128)S(1)}, u32[]{:S(2)}, u32[]{:S(2)}) %collective-permute-start.7) | collective-permute-done | bytes 98336 | tf_op jit(solution)/shard_map/ppermute | solution.py:378
  28.7 0.4 collective-permute-done.8.xea
  29.1 0.0 collective-permute-done.9.xeb
  29.1 1.0 %shard_map.31 = (f32[3,16,16,128]{3,2,1,0:T(8,128)S(1)}, f32[3,16,16,128]{3,2,1,0:T(8,128)S(1)}, f32[3,24,8,128]{3,2,1,0:T(8,128)S(1)}, f32[3,24,8,128]{3,2,1,0:T(8,128)S(1)}) custom-call(f32[3,16,64,128]{3,2,1,0:T(8,128)S(1)} %get-tuple-element.25.d, f32[48,8,128]{2,1,0:T(8,128)S(1)} %collective-permute-done.8.xea, ...), custom_call_target="tpu_custom_call" | custom-call | tf_op jit(solution)/shard_map/pallas_call | solution.py:36
  30.1 0.0 copy-start
  30.1 6.0 %collective-permute-start.10 = (f32[3,24,8,128]{3,2,1,0:T(8,128)S(1)}, f32[3,24,8,128]{3,2,1,0:T(8,128)S(1)}, u32[]{:S(2)}, u32[]{:S(2)}) collective-permute-start(f32[3,24,8,128]{3,2,1,0:T(8,128)S(1)} %get-tuple-element.40), channel_id=1, source_target_pairs={{0,8},{8,16},{16,24},{24,0},{1,9},{9,17},{17,25},{25,1},{2,10},{10... | collective-permute-start | bytes 884744 | tf_op jit(solution)/shard_map/ppermute | solution.py:378
  36.1 0.0 collective-permute-start.11
  36.1 0.0 collective-permute-start.2
  36.1 0.0 collective-permute-done.xia.refs_0_
  36.1 3.2 %collective-permute-start.3 = (f32[24,8,128]{2,1,0:T(8,128)S(1)}, f32[24,8,128]{2,1,0:T(8,128)S(1)}, u32[]{:S(2)}, u32[]{:S(2)}) collective-permute-start(f32[24,8,128]{2,1,0:T(8,128)S(1)} %get-tuple-element.29), channel_id=1, source_target_pairs={{0,224},{32,0},{64,32},{96,64},{128,96},{160,128},{192,160},{224,1... | collective-permute-start | bytes 294920 | tf_op jit(solution)/shard_map/ppermute | solution.py:378
  39.3 2.4 %shard_map.30 = (f32[3,16,48,128]{3,2,1,0:T(8,128)S(1)}, f32[3,16,48,128]{3,2,1,0:T(8,128)S(1)}) custom-call(f32[3,16,64,128]{3,2,1,0:T(8,128)S(1)} %get-tuple-element.25.d, f32[3,64,128]{2,1,0:T(8,128)S(1)} %collective-permute-done.6.xza, f32[3,64,128]{2,1,0:T(8,128)S(1)} %get-tuple-element.33.xzd, f32[3,64,128]{2,1,0:T(8,128)S(1)} %get-tuple-element.32.xzu, ...), custom_call_target="tpu_custom_call" | custom-call | tf_op jit(solution)/shard_map/pallas_call | solution.py:36
  41.8 0.0 collective-permute-done.1.xib.refs_1_
  41.8 0.0 copy-done
  41.8 1.2 %shard_map.32 = (f32[2,16,48,128]{3,2,1,0:T(8,128)S(1)}, f32[2,16,16,128]{3,2,1,0:T(8,128)S(1)}, f32[2,16,16,128]{3,2,1,0:T(8,128)S(1)}) custom-call(f32[120,8,128]{2,1,0:T(8,128)S(1)} %collective-permute-done.xia.refs_0_, f32[120,8,128]{2,1,0:T(8,128)S(1)} %collective-permute-done.1.xib.refs_1_, f32[3,16,48,128]{3,2,1,0:T(8,128)S(1)} %get-tuple-element.34.acc_s.refs_4_, ...), custom_call_target="tpu_custom_call" | custom-call | tf_op jit(solution)/shard_map/pallas_call | solution.py:36
  43.0 0.0 collective-permute-done.2.refs_2_
  43.0 0.0 collective-permute-done.3.refs_3_
  43.0 0.0 collective-permute-done.10.refs_9_
  43.0 0.7 %collective-permute-done.11.refs_10_ = f32[3,24,8,128]{3,2,1,0:T(8,128)S(1)} collective-permute-done((f32[3,24,8,128]{3,2,1,0:T(8,128)S(1)}, f32[3,24,8,128]{3,2,1,0:T(8,128)S(1)}, u32[]{:S(2)}, u32[]{:S(2)}) %collective-permute-start.11) | collective-permute-done | bytes 294944 | tf_op jit(solution)/shard_map/ppermute | solution.py:378
  43.8 1.6 %final.1 = f32[3,16,64,128]{3,2,1,0:T(8,128)} custom-call(f32[120,8,128]{2,1,0:T(8,128)S(1)} %collective-permute-done.xia.refs_0_, f32[120,8,128]{2,1,0:T(8,128)S(1)} %collective-permute-done.1.xib.refs_1_, f32[24,8,128]{2,1,0:T(8,128)S(1)} %collective-permute-done.2.refs_2_, f32[24,8,128]{2,1,0:T(8,128)S(1)} %collective-permute-done.3.refs_3_, ...), custom_call_target="tpu_custom_call" | custom-call | tf_op jit(solution)/shard_map/final/pallas_call | solution.py:363
Async XLA Ops:
  1.9 10.5 %collective-permute-start.4 = (f32[3,64,128]{2,1,0:T(8,128)S(1)}, f32[3,64,128]{2,1,0:T(8,128)S(1)}, u32[]{:S(2)}, u32[]{:S(2)}) collective-permute-start(f32[3,64,128]{2,1,0:T(8,128)S(1)} %get-tuple-element.30), channel_id=1, source_target_pairs={{0,1},{1,2},{2,3},{3,4},{4,5},{5,6},{6,7},{7,0},{8,9},{9,10},{10,1... | collective-permute-start | bytes 294920 | tf_op jit(solution)/shard_map/ppermute | solution.py:378
  4.1 8.3 %collective-permute-start.5 = (f32[3,64,128]{2,1,0:T(8,128)S(1)}, f32[3,64,128]{2,1,0:T(8,128)S(1)}, u32[]{:S(2)}, u32[]{:S(2)}) collective-permute-start(f32[3,64,128]{2,1,0:T(8,128)S(1)} %get-tuple-element.31), channel_id=1, source_target_pairs={{0,7},{1,0},{2,1},{3,2},{4,3},{5,4},{6,5},{7,6},{8,15},{9,8},{10,9... | collective-permute-start | bytes 294920 | tf_op jit(solution)/shard_map/ppermute | solution.py:378
  6.6 29.5 %collective-permute-start = (f32[120,8,128]{2,1,0:T(8,128)S(1)}, f32[120,8,128]{2,1,0:T(8,128)S(1)}, u32[]{:S(2)}, u32[]{:S(2)}) collective-permute-start(f32[120,8,128]{2,1,0:T(8,128)S(1)} %get-tuple-element.26), channel_id=1, source_target_pairs={{0,32},{32,64},{64,96},{96,128},{128,160},{160,192},{192,224},{224... | collective-permute-start | bytes 1474568 | tf_op jit(solution)/shard_map/ppermute | solution.py:378
  8.3 33.4 %collective-permute-start.1 = (f32[120,8,128]{2,1,0:T(8,128)S(1)}, f32[120,8,128]{2,1,0:T(8,128)S(1)}, u32[]{:S(2)}, u32[]{:S(2)}) collective-permute-start(f32[120,8,128]{2,1,0:T(8,128)S(1)} %get-tuple-element.27), channel_id=1, source_target_pairs={{0,224},{32,0},{64,32},{96,64},{128,96},{160,128},{192,160},{224,1... | collective-permute-start | bytes 1474568 | tf_op jit(solution)/shard_map/ppermute | solution.py:378
  12.5 12.4 %collective-permute-start.6 = (f32[3,64,128]{2,1,0:T(8,128)S(1)}, f32[3,64,128]{2,1,0:T(8,128)S(1)}, u32[]{:S(2)}, u32[]{:S(2)}) collective-permute-start(f32[3,64,128]{2,1,0:T(8,128)S(1)} %get-tuple-element.32.xzu), channel_id=1, source_target_pairs={{0,32},{32,64},{64,96},{96,128},{128,160},{160,192},{192,224},{224... | collective-permute-start | bytes 294920 | tf_op jit(solution)/shard_map/ppermute | solution.py:378
  12.6 16.5 %collective-permute-start.8 = (f32[48,8,128]{2,1,0:T(8,128)S(1)}, f32[48,8,128]{2,1,0:T(8,128)S(1)}, u32[]{:S(2)}, u32[]{:S(2)}) collective-permute-start(f32[48,8,128]{2,1,0:T(8,128)S(1)} %get-tuple-element.36), channel_id=1, source_target_pairs={{0,32},{32,64},{64,96},{96,128},{128,160},{160,192},{192,224},{224... | collective-permute-start | bytes 589832 | tf_op jit(solution)/shard_map/ppermute | solution.py:378
  12.7 16.5 %collective-permute-start.9 = (f32[48,8,128]{2,1,0:T(8,128)S(1)}, f32[48,8,128]{2,1,0:T(8,128)S(1)}, u32[]{:S(2)}, u32[]{:S(2)}) collective-permute-start(f32[48,8,128]{2,1,0:T(8,128)S(1)} %get-tuple-element.37), channel_id=1, source_target_pairs={{0,224},{32,0},{64,32},{96,64},{128,96},{160,128},{192,160},{224,1... | collective-permute-start | bytes 589832 | tf_op jit(solution)/shard_map/ppermute | solution.py:378
  24.9 3.8 %collective-permute-start.7 = (f32[3,64,128]{2,1,0:T(8,128)S(1)}, f32[3,64,128]{2,1,0:T(8,128)S(1)}, u32[]{:S(2)}, u32[]{:S(2)}) collective-permute-start(f32[3,64,128]{2,1,0:T(8,128)S(1)} %get-tuple-element.33.xzd), channel_id=1, source_target_pairs={{0,224},{32,0},{64,32},{96,64},{128,96},{160,128},{192,160},{224,1... | collective-permute-start | bytes 294920 | tf_op jit(solution)/shard_map/ppermute | solution.py:378
  30.1 11.7 %copy-start = (f32[16,64,128]{2,1,0:T(8,128)S(1)}, f32[16,64,128]{2,1,0:T(8,128)}, u32[]{:S(2)}) copy-start(f32[16,64,128]{2,1,0:T(8,128)} %refs_8_.1) | copy-start | bytes 1572868
  30.1 12.9 %collective-permute-start.10 = (f32[3,24,8,128]{3,2,1,0:T(8,128)S(1)}, f32[3,24,8,128]{3,2,1,0:T(8,128)S(1)}, u32[]{:S(2)}, u32[]{:S(2)}) collective-permute-start(f32[3,24,8,128]{3,2,1,0:T(8,128)S(1)} %get-tuple-element.40), channel_id=1, source_target_pairs={{0,8},{8,16},{16,24},{24,0},{1,9},{9,17},{17,25},{25,1},{2,10},{10... | collective-permute-start | bytes 884744 | tf_op jit(solution)/shard_map/ppermute | solution.py:378
  36.1 7.7 %collective-permute-start.11 = (f32[3,24,8,128]{3,2,1,0:T(8,128)S(1)}, f32[3,24,8,128]{3,2,1,0:T(8,128)S(1)}, u32[]{:S(2)}, u32[]{:S(2)}) collective-permute-start(f32[3,24,8,128]{3,2,1,0:T(8,128)S(1)} %get-tuple-element.41), channel_id=1, source_target_pairs={{0,24},{8,0},{16,8},{24,16},{1,25},{9,1},{17,9},{25,17},{2,26},{10... | collective-permute-start | bytes 884744 | tf_op jit(solution)/shard_map/ppermute | solution.py:378
  36.1 6.9 %collective-permute-start.2 = (f32[24,8,128]{2,1,0:T(8,128)S(1)}, f32[24,8,128]{2,1,0:T(8,128)S(1)}, u32[]{:S(2)}, u32[]{:S(2)}) collective-permute-start(f32[24,8,128]{2,1,0:T(8,128)S(1)} %get-tuple-element.28), channel_id=1, source_target_pairs={{0,32},{32,64},{64,96},{96,128},{128,160},{160,192},{192,224},{224... | collective-permute-start | bytes 294920 | tf_op jit(solution)/shard_map/ppermute | solution.py:378
  36.1 6.9 %collective-permute-start.3 = (f32[24,8,128]{2,1,0:T(8,128)S(1)}, f32[24,8,128]{2,1,0:T(8,128)S(1)}, u32[]{:S(2)}, u32[]{:S(2)}) collective-permute-start(f32[24,8,128]{2,1,0:T(8,128)S(1)} %get-tuple-element.29), channel_id=1, source_target_pairs={{0,224},{32,0},{64,32},{96,64},{128,96},{160,128},{192,160},{224,1... | collective-permute-start | bytes 294920 | tf_op jit(solution)/shard_map/ppermute | solution.py:378

commit v6 on v5

--- a/solution.py
+++ b/solution.py
@@ -276,17 +276,22 @@
         ref[:, ny - H :] = w[:, H:]
 
 
-def inner_body(xia, xib, acc_s, acc_l, ws, wl, eff, done, es, el, us, ul):
+def inner_body(low, xia, xib, *refs):
+    late, refs = (refs[:2], refs[2:]) if low else ((), refs)
+    acc_s, acc_l, ws, wl, eff = refs[:5]
+    done, es, el, us, ul = refs[-5:]
     n, nx, ny, nz = us.shape
     half = nx // 2
+    inner = ny - 2 * H
     rows = slice(H, ny - H)
     wm = band(False)
     band_s, band_l = rows_band(R_SMALL, ny), rows_band(R_LARGE, ny)
     for j in range(n):
-        s = j
+        s = low + j
         here = (acc_s.at[s], acc_l.at[s], ws.at[s], wl.at[s], us.at[j], ul.at[j])
-        inner = ny - 2 * H
-        got = [x[j * inner : (j + 1) * inner] for x in (xia, xib)]
+        got = [x[s * inner : min((s + 1) * inner, x.shape[0])] for x in (xia, xib)]
+        if late:
+            got = [jnp.concatenate([x, y[...]], axis=0) for x, y in zip(got, late)]
         prepare(*got, *here, wm)
         for i in range(half):
             sums = own_sums(us.at[j], ul.at[j], band_s, band_l, i)
@@ -297,79 +302,58 @@
                 el[j, at] = rim_rows(large)
 
 
-def final_body(low, xia, xib, xja, xjb, acc_s, acc_l, ws, wl, eff, ya, yb, kept_rows, es, el, out, us, ul, rim, done, sems):
-    n, nx, ny, nz = us.shape
-    half = nx // 2
-    wm, w = band(False), ends_band()
-    band_s, band_l = rows_band(R_SMALL, ny), rows_band(R_LARGE, ny)
-    sides = ((0, slice(0, nz)), (half, slice(nz, 2 * nz)))
+def ends_body(eff, ya, yb, *refs):
+    out, rim, sems = refs[-3:]
+    parts = refs[:-3]
+    ny, nz = eff.shape[1:]
+    half = eff.shape[0] // 2
+    w = ends_band()
+    trios = list(zip(parts[0::3], parts[1::3], parts[2::3]))
+    sums = [(es.at[j], el.at[j]) for _, es, el in trios for j in range(es.shape[0])]
     copies = []
-    for s in range(low):
-        target = out.at[s, :, pl.ds(H, ny - 2 * H), :]
-        copies.append(pltpu.make_async_copy(kept_rows.at[s], target, sems.at[len(copies)]))
+    first = 0
+    for ready, _, _ in trios:
+        n = ready.shape[0]
+        target = out.at[pl.ds(first, n), :, pl.ds(H, ny - 2 * H), :]
+        copies.append(pltpu.make_async_copy(ready, target, sems.at[len(copies)]))
         copies[-1].start()
-    for s in range(low):
+        first += n
+    for s, (es, el) in enumerate(sums):
         for i in range(half):
             more = halo_sums(ya, yb, s, i, half, w)
-            for step, col in sides:
-                at = i + step
+            for at, col in ((i, slice(0, nz)), (i + half, slice(nz, 2 * nz))):
                 add_s, add_l = more[0 : 2 * H, col], more[2 * H :, col]
-                rim[s, at] = level(es[s, at] + add_s, el[s, at] + add_l, rim_rows(eff[at]))
+                rim[s, at] = level(es[at] + add_s, el[at] + add_l, rim_rows(eff[at]))
         for k, start in enumerate((0, ny - H)):
             source = rim.at[s, :, pl.ds(k * H, H), :]
             target = out.at[s, :, pl.ds(start, H), :]
             copies.append(pltpu.make_async_copy(source, target, sems.at[len(copies)]))
             copies[-1].start()
-    for j in range(n):
-        s = low + j
-        here = (acc_s.at[s], acc_l.at[s], ws.at[s], wl.at[s], us.at[j], ul.at[j])
-        kept = low * (ny - 2 * H)
-        got = [jnp.concatenate([x[kept:], y[...]], axis=0) for x, y in ((xia, xja), (xib, xjb))]
-        prepare(*got, *here, wm)
-        for i in range(half):
-            sums = own_sums(us.at[j], ul.at[j], band_s, band_l, i)
-            more = halo_sums(ya, yb, s, i, half, w)
-            for step, col in sides:
-                at = i + step
-                small, large = sums[0][:, col], sums[1][:, col]
-                add_s, add_l = more[0 : 2 * H, col], more[2 * H :, col]
-                rows = slice(H, ny - H)
-                done[j, at, rows] = level(small[rows], large[rows], eff[at, rows])
-                ends = level(rim_rows(small) + add_s, rim_rows(large) + add_l, rim_rows(eff[at]))
-                done[j, at, 0:H] = ends[0:H]
-                done[j, at, ny - H :] = ends[H:]
-            if i % 2:
-                for step, _ in sides:
-                    some = pl.ds(i - 1 + step, 2)
-                    copies.append(
-                        pltpu.make_async_copy(
-                            done.at[j, some], out.at[s, some], sems.at[len(copies)]
-                        )
-                    )
-                    copies[-1].start()
     for copy in copies:
         copy.wait()
 
 
-def inner_call(high, args, shape):
+def inner_call(low, high, args, shape):
     _, nx, ny, nz = shape
-    outs = [(high, nx, ny - 2 * H, nz)] + [(high, nx, 2 * H, nz)] * 2
-    return run(inner_body, args, outs, [pltpu.VMEM((high, nx, ny, nz), F32)] * 2)
-
-
-def final_call(low, args, shape):
-    snaps, nx, ny, nz = shape
-    n = snaps - low
+    n = high - low
+    outs = [(n, nx, ny - 2 * H, nz)] + [(n, nx, 2 * H, nz)] * 2
+    scratch = [pltpu.VMEM((n, nx, ny, nz), F32)] * 2
+    return run(lambda *refs: inner_body(low, *refs), args, outs, scratch)
+
+
+def ends_call(args, shape):
+    snaps, nx, _, nz = shape
     return pl.pallas_call(
-        lambda *refs: final_body(low, *refs),
+        ends_body,
         out_shape=jax.ShapeDtypeStruct(shape, F32),
         in_specs=[VMEM] * len(args),
         out_specs=pl.BlockSpec(memory_space=pl.ANY),
-        scratch_shapes=[pltpu.VMEM((n, nx, ny, nz), F32)] * 2
-        + [pltpu.VMEM((low, nx, 2 * H, nz), F32), pltpu.VMEM((n, nx, ny, nz), F32)]
-        + [pltpu.SemaphoreType.DMA((n * nx // 2 + 3 * low,))],
+        scratch_shapes=[
+            pltpu.VMEM((snaps, nx, 2 * H, nz), F32),
+            pltpu.SemaphoreType.DMA((2 * snaps + 2,)),
+        ],
         compiler_params=PARAMS,
-        name="final",
+        name="ends",
     )(*[near(a) for a in args])
 
 
@@ -416,8 +400,10 @@
         [pltpu.VMEM((snaps, wide, inner, nz), F32)] * 2,
     )
     shared = (acc_s, acc_l, ws, wl, efficiency)
-    ready = inner_call(snaps - 1, halos[0] + shared, block)
-    out = final_call(snaps - 1, halos[0] + halos[1] + shared + (ya, yb, *ready), block)
+    last = snaps - 1
+    first = inner_call(0, last, halos[0] + shared, block)
+    second = inner_call(last, snaps, halos[0] + halos[1] + shared, block)
+    out = ends_call((efficiency, ya, yb, *first, *second), block)
     return out
 
 

time: 45.6 us -> 45.2 us (level)
  waiting for transfers between devices: 13.4 us -> 12.7 us
    ppermute x12, waiting for transfers between devices: 13.4 us -> 12.7 us  [shift(): return lax.ppermute(block, axis, [(i, (i + step) % n) for i in range(n)])]
    pallas_call x5 -> x6, Pallas kernels: 4.79 us -> 5.45 us  [run(): pl.pallas_call(body, out_shape=[pltpu.VMEM(s, F32) for s in outs], in_spe...]
  transfers between devices with their start and end apart: 12 -> 12, of which waited for: 4 -> 4; matrix products, arithmetic and copies ran while one was open for 0% -> 0% of each run, Pallas kernels for 11% -> 12%
where the time goes in v6:
time: 45.2 us; the launch traced here: 45.1 us
  starting transfers between devices  23.6 us (52%)
  waiting for transfers between devices  12.7 us (28%)
  Pallas kernels  8.53 us (19%)
    ppermute x12, starting transfers between devices, shift(): return lax.ppermute(block, axis, [(i, (i + step) % n) for i in range(n)])  23.6 us
    ppermute x12, waiting for transfers between devices, shift(): return lax.ppermute(block, axis, [(i, (i + step) % n) for i in range(n)])  12.7 us
    pallas_call x6, Pallas kernels, run(): pl.pallas_call(body, out_shape=[pltpu.VMEM(s, F32) for s in outs], in_spe...  5.45 us
    pallas_call x1, Pallas kernels, steps(): pl.pallas_call(pack_body, out_shape=[pltpu.VMEM(s, F32) for s in (block,...  1.88 us
    pallas_call x1, Pallas kernels, ends_call(): pl.pallas_call(ends_body, out_shape=jax.ShapeDtypeStruct(shape, F32), in_...  1.2 us
  transfers between devices with their start and end apart: 12, of which 4 were waited for; matrix products, arithmetic and copies ran while one was open for 0% of the time, Pallas kernels for 12%

profile of v6, /device:TPU:1, one launch (start us, length us, event | category | flops | bytes accessed | tf_op | source)
XLA Modules:
  0.0 45.1 jit_solution(5526507647312788955)
XLA Ops:
  0.0 1.9 %pack.1 = (f32[3,16,64,128]{3,2,1,0:T(8,128)S(1)}, f32[3,64,128]{2,1,0:T(8,128)S(1)}, f32[3,64,128]{2,1,0:T(8,128)S(1)}, f32[48,8,128]{2,1,0:T(8,128)S(1)}, f32[48,8,128]{2,1,0:T(8,128)S(1)}) custom-call(f32[3,16,64,128]{3,2,1,0:T(8,128)} %d_hbm.1), custom_call_target="tpu_custom_call" | custom-call | tf_op jit(solution)/shard_map/pack/pallas_call | solution.py:375
  1.9 2.2 %collective-permute-start.2 = (f32[3,64,128]{2,1,0:T(8,128)S(1)}, f32[3,64,128]{2,1,0:T(8,128)S(1)}, u32[]{:S(2)}, u32[]{:S(2)}) collective-permute-start(f32[3,64,128]{2,1,0:T(8,128)S(1)} %get-tuple-element.31), channel_id=1, source_target_pairs={{0,1},{1,2},{2,3},{3,4},{4,5},{5,6},{6,7},{7,0},{8,9},{9,10},{10,1... | collective-permute-start | bytes 294920 | tf_op jit(solution)/shard_map/ppermute | solution.py:362
  4.1 2.5 %collective-permute-start.3 = (f32[3,64,128]{2,1,0:T(8,128)S(1)}, f32[3,64,128]{2,1,0:T(8,128)S(1)}, u32[]{:S(2)}, u32[]{:S(2)}) collective-permute-start(f32[3,64,128]{2,1,0:T(8,128)S(1)} %get-tuple-element.32), channel_id=1, source_target_pairs={{0,7},{1,0},{2,1},{3,2},{4,3},{5,4},{6,5},{7,6},{8,15},{9,8},{10,9... | collective-permute-start | bytes 294920 | tf_op jit(solution)/shard_map/ppermute | solution.py:362
  6.5 0.1 shard_map.30
  6.6 1.7 %collective-permute-start.8 = (f32[120,8,128]{2,1,0:T(8,128)S(1)}, f32[120,8,128]{2,1,0:T(8,128)S(1)}, u32[]{:S(2)}, u32[]{:S(2)}) collective-permute-start(f32[120,8,128]{2,1,0:T(8,128)S(1)} %get-tuple-element.37), channel_id=1, source_target_pairs={{0,32},{32,64},{64,96},{96,128},{128,160},{160,192},{192,224},{224... | collective-permute-start | bytes 1474568 | tf_op jit(solution)/shard_map/ppermute | solution.py:362
  8.3 4.0 %collective-permute-start.9 = (f32[120,8,128]{2,1,0:T(8,128)S(1)}, f32[120,8,128]{2,1,0:T(8,128)S(1)}, u32[]{:S(2)}, u32[]{:S(2)}) collective-permute-start(f32[120,8,128]{2,1,0:T(8,128)S(1)} %get-tuple-element.38), channel_id=1, source_target_pairs={{0,224},{32,0},{64,32},{96,64},{128,96},{160,128},{192,160},{224,1... | collective-permute-start | bytes 1474568 | tf_op jit(solution)/shard_map/ppermute | solution.py:362
  12.4 0.0 collective-permute-done.2.za
  12.4 0.0 collective-permute-done.3.zb
  12.4 0.1 shard_map.28
  12.5 0.1 collective-permute-start.4
  12.6 0.1 collective-permute-start
  12.7 2.7 %collective-permute-start.1 = (f32[48,8,128]{2,1,0:T(8,128)S(1)}, f32[48,8,128]{2,1,0:T(8,128)S(1)}, u32[]{:S(2)}, u32[]{:S(2)}) collective-permute-start(f32[48,8,128]{2,1,0:T(8,128)S(1)} %get-tuple-element.30), channel_id=1, source_target_pairs={{0,224},{32,0},{64,32},{96,64},{128,96},{160,128},{192,160},{224,1... | collective-permute-start | bytes 589832 | tf_op jit(solution)/shard_map/ppermute | solution.py:362
  15.3 9.6 %collective-permute-done.4.xza = f32[3,64,128]{2,1,0:T(8,128)S(1)} collective-permute-done((f32[3,64,128]{2,1,0:T(8,128)S(1)}, f32[3,64,128]{2,1,0:T(8,128)S(1)}, u32[]{:S(2)}, u32[]{:S(2)}) %collective-permute-start.4) | collective-permute-done | bytes 98336 | tf_op jit(solution)/shard_map/ppermute | solution.py:362
  24.9 1.2 %collective-permute-start.5 = (f32[3,64,128]{2,1,0:T(8,128)S(1)}, f32[3,64,128]{2,1,0:T(8,128)S(1)}, u32[]{:S(2)}, u32[]{:S(2)}) collective-permute-start(f32[3,64,128]{2,1,0:T(8,128)S(1)} %get-tuple-element.34.xzd), channel_id=1, source_target_pairs={{0,224},{32,0},{64,32},{96,64},{128,96},{160,128},{192,160},{224,1... | collective-permute-start | bytes 294920 | tf_op jit(solution)/shard_map/ppermute | solution.py:362
  26.1 2.6 %collective-permute-done.5.xzb = f32[3,64,128]{2,1,0:T(8,128)S(1)} collective-permute-done((f32[3,64,128]{2,1,0:T(8,128)S(1)}, f32[3,64,128]{2,1,0:T(8,128)S(1)}, u32[]{:S(2)}, u32[]{:S(2)}) %collective-permute-start.5) | collective-permute-done | bytes 98336 | tf_op jit(solution)/shard_map/ppermute | solution.py:362
  28.7 0.4 collective-permute-done.xea
  29.1 0.0 collective-permute-done.1.xeb
  29.1 1.0 %shard_map.29 = (f32[3,16,16,128]{3,2,1,0:T(8,128)S(1)}, f32[3,16,16,128]{3,2,1,0:T(8,128)S(1)}, f32[3,24,8,128]{3,2,1,0:T(8,128)S(1)}, f32[3,24,8,128]{3,2,1,0:T(8,128)S(1)}) custom-call(f32[3,16,64,128]{3,2,1,0:T(8,128)S(1)} %get-tuple-element.28.d, f32[48,8,128]{2,1,0:T(8,128)S(1)} %collective-permute-done.xea, ...), custom_call_target="tpu_custom_call" | custom-call | tf_op jit(solution)/shard_map/pallas_call | solution.py:36
  30.1 0.0 copy-start
  30.1 6.0 %collective-permute-start.6 = (f32[3,24,8,128]{3,2,1,0:T(8,128)S(1)}, f32[3,24,8,128]{3,2,1,0:T(8,128)S(1)}, u32[]{:S(2)}, u32[]{:S(2)}) collective-permute-start(f32[3,24,8,128]{3,2,1,0:T(8,128)S(1)} %get-tuple-element.35), channel_id=1, source_target_pairs={{0,8},{8,16},{16,24},{24,0},{1,9},{9,17},{17,25},{25,1},{2,10},{10... | collective-permute-start | bytes 884744 | tf_op jit(solution)/shard_map/ppermute | solution.py:362
  36.1 0.0 collective-permute-start.7
  36.1 0.0 collective-permute-start.10
  36.1 0.0 collective-permute-done.8.refs_0_
  36.1 3.2 %collective-permute-start.11 = (f32[24,8,128]{2,1,0:T(8,128)S(1)}, f32[24,8,128]{2,1,0:T(8,128)S(1)}, u32[]{:S(2)}, u32[]{:S(2)}) collective-permute-start(f32[24,8,128]{2,1,0:T(8,128)S(1)} %get-tuple-element.47), channel_id=1, source_target_pairs={{0,224},{32,0},{64,32},{96,64},{128,96},{160,128},{192,160},{224,1... | collective-permute-start | bytes 294920 | tf_op jit(solution)/shard_map/ppermute | solution.py:362
  39.3 2.4 %shard_map.31 = (f32[3,16,48,128]{3,2,1,0:T(8,128)S(1)}, f32[3,16,48,128]{3,2,1,0:T(8,128)S(1)}) custom-call(f32[3,16,64,128]{3,2,1,0:T(8,128)S(1)} %get-tuple-element.28.d, f32[3,64,128]{2,1,0:T(8,128)S(1)} %collective-permute-done.4.xza, f32[3,64,128]{2,1,0:T(8,128)S(1)} %get-tuple-element.34.xzd, f32[3,64,128]{2,1,0:T(8,128)S(1)} %get-tuple-element.33.xzu, ...), custom_call_target="tpu_custom_call" | custom-call | tf_op jit(solution)/shard_map/pallas_call | solution.py:36
  41.8 0.0 collective-permute-done.9.refs_1_
  41.8 0.0 copy-done
  41.8 1.2 %shard_map.32 = (f32[2,16,48,128]{3,2,1,0:T(8,128)S(1)}, f32[2,16,16,128]{3,2,1,0:T(8,128)S(1)}, f32[2,16,16,128]{3,2,1,0:T(8,128)S(1)}) custom-call(f32[120,8,128]{2,1,0:T(8,128)S(1)} %collective-permute-done.8.refs_0_, f32[120,8,128]{2,1,0:T(8,128)S(1)} %collective-permute-done.9.refs_1_, f32[3,16,48,128]{3,2,1,0:T(8,128)S(1)} %get-tuple-element.39.refs_2_.refs_4_, ...), custom_call_target="tpu_custom_call" | custom-call | tf_op jit(solution)/shard_map/pallas_call | solution.py:36
  43.0 0.0 collective-permute-done.10.refs_2_
  43.0 0.0 collective-permute-done.11.refs_3_
  43.0 0.7 %shard_map.33 = (f32[1,16,48,128]{3,2,1,0:T(8,128)S(1)}, f32[1,16,16,128]{3,2,1,0:T(8,128)S(1)}, f32[1,16,16,128]{3,2,1,0:T(8,128)S(1)}) custom-call(f32[120,8,128]{2,1,0:T(8,128)S(1)} %collective-permute-done.8.refs_0_, f32[120,8,128]{2,1,0:T(8,128)S(1)} %collective-permute-done.9.refs_1_, f32[24,8,128]{2,1,0:T(8,128)S(1)} %collective-permute-done.10.refs_2_, ...), custom_call_target="tpu_custom_call" | custom-call | tf_op jit(solution)/shard_map/pallas_call | solution.py:36
  43.7 0.0 collective-permute-done.6.ya
  43.7 0.1 collective-permute-done.7.yb
  43.8 1.2 %ends.1 = f32[3,16,64,128]{3,2,1,0:T(8,128)} custom-call(f32[16,64,128]{2,1,0:T(8,128)S(1)} %copy-done, f32[3,24,8,128]{3,2,1,0:T(8,128)S(1)} %collective-permute-done.6.ya, f32[3,24,8,128]{3,2,1,0:T(8,128)S(1)} %collective-permute-done.7.yb, f32[2,16,48,128]{3,2,1,0:T(8,128)S(1)} %get-tuple-element.43.refs_0_, ...), custom_call_target="tpu_custom_call" | custom-call | tf_op jit(solution)/shard_map/ends/pallas_call | solution.py:346
Async XLA Ops:
  1.9 10.5 %collective-permute-start.2 = (f32[3,64,128]{2,1,0:T(8,128)S(1)}, f32[3,64,128]{2,1,0:T(8,128)S(1)}, u32[]{:S(2)}, u32[]{:S(2)}) collective-permute-start(f32[3,64,128]{2,1,0:T(8,128)S(1)} %get-tuple-element.31), channel_id=1, source_target_pairs={{0,1},{1,2},{2,3},{3,4},{4,5},{5,6},{6,7},{7,0},{8,9},{9,10},{10,1... | collective-permute-start | bytes 294920 | tf_op jit(solution)/shard_map/ppermute | solution.py:362
  4.1 8.3 %collective-permute-start.3 = (f32[3,64,128]{2,1,0:T(8,128)S(1)}, f32[3,64,128]{2,1,0:T(8,128)S(1)}, u32[]{:S(2)}, u32[]{:S(2)}) collective-permute-start(f32[3,64,128]{2,1,0:T(8,128)S(1)} %get-tuple-element.32), channel_id=1, source_target_pairs={{0,7},{1,0},{2,1},{3,2},{4,3},{5,4},{6,5},{7,6},{8,15},{9,8},{10,9... | collective-permute-start | bytes 294920 | tf_op jit(solution)/shard_map/ppermute | solution.py:362
  6.6 29.5 %collective-permute-start.8 = (f32[120,8,128]{2,1,0:T(8,128)S(1)}, f32[120,8,128]{2,1,0:T(8,128)S(1)}, u32[]{:S(2)}, u32[]{:S(2)}) collective-permute-start(f32[120,8,128]{2,1,0:T(8,128)S(1)} %get-tuple-element.37), channel_id=1, source_target_pairs={{0,32},{32,64},{64,96},{96,128},{128,160},{160,192},{192,224},{224... | collective-permute-start | bytes 1474568 | tf_op jit(solution)/shard_map/ppermute | solution.py:362
  8.3 33.4 %collective-permute-start.9 = (f32[120,8,128]{2,1,0:T(8,128)S(1)}, f32[120,8,128]{2,1,0:T(8,128)S(1)}, u32[]{:S(2)}, u32[]{:S(2)}) collective-permute-start(f32[120,8,128]{2,1,0:T(8,128)S(1)} %get-tuple-element.38), channel_id=1, source_target_pairs={{0,224},{32,0},{64,32},{96,64},{128,96},{160,128},{192,160},{224,1... | collective-permute-start | bytes 1474568 | tf_op jit(solution)/shard_map/ppermute | solution.py:362
  12.5 12.4 %collective-permute-start.4 = (f32[3,64,128]{2,1,0:T(8,128)S(1)}, f32[3,64,128]{2,1,0:T(8,128)S(1)}, u32[]{:S(2)}, u32[]{:S(2)}) collective-permute-start(f32[3,64,128]{2,1,0:T(8,128)S(1)} %get-tuple-element.33.xzu), channel_id=1, source_target_pairs={{0,32},{32,64},{64,96},{96,128},{128,160},{160,192},{192,224},{224... | collective-permute-start | bytes 294920 | tf_op jit(solution)/shard_map/ppermute | solution.py:362
  12.6 16.5 %collective-permute-start = (f32[48,8,128]{2,1,0:T(8,128)S(1)}, f32[48,8,128]{2,1,0:T(8,128)S(1)}, u32[]{:S(2)}, u32[]{:S(2)}) collective-permute-start(f32[48,8,128]{2,1,0:T(8,128)S(1)} %get-tuple-element.29), channel_id=1, source_target_pairs={{0,32},{32,64},{64,96},{96,128},{128,160},{160,192},{192,224},{224... | collective-permute-start | bytes 589832 | tf_op jit(solution)/shard_map/ppermute | solution.py:362
  12.7 16.5 %collective-permute-start.1 = (f32[48,8,128]{2,1,0:T(8,128)S(1)}, f32[48,8,128]{2,1,0:T(8,128)S(1)}, u32[]{:S(2)}, u32[]{:S(2)}) collective-permute-start(f32[48,8,128]{2,1,0:T(8,128)S(1)} %get-tuple-element.30), channel_id=1, source_target_pairs={{0,224},{32,0},{64,32},{96,64},{128,96},{160,128},{192,160},{224,1... | collective-permute-start | bytes 589832 | tf_op jit(solution)/shard_map/ppermute | solution.py:362
  24.9 3.8 %collective-permute-start.5 = (f32[3,64,128]{2,1,0:T(8,128)S(1)}, f32[3,64,128]{2,1,0:T(8,128)S(1)}, u32[]{:S(2)}, u32[]{:S(2)}) collective-permute-start(f32[3,64,128]{2,1,0:T(8,128)S(1)} %get-tuple-element.34.xzd), channel_id=1, source_target_pairs={{0,224},{32,0},{64,32},{96,64},{128,96},{160,128},{192,160},{224,1... | collective-permute-start | bytes 294920 | tf_op jit(solution)/shard_map/ppermute | solution.py:362
  30.1 11.7 %copy-start = (f32[16,64,128]{2,1,0:T(8,128)S(1)}, f32[16,64,128]{2,1,0:T(8,128)}, u32[]{:S(2)}) copy-start(f32[16,64,128]{2,1,0:T(8,128)} %eff.1) | copy-start | bytes 1572868
  30.1 13.6 %collective-permute-start.6 = (f32[3,24,8,128]{3,2,1,0:T(8,128)S(1)}, f32[3,24,8,128]{3,2,1,0:T(8,128)S(1)}, u32[]{:S(2)}, u32[]{:S(2)}) collective-permute-start(f32[3,24,8,128]{3,2,1,0:T(8,128)S(1)} %get-tuple-element.35), channel_id=1, source_target_pairs={{0,8},{8,16},{16,24},{24,0},{1,9},{9,17},{17,25},{25,1},{2,10},{10... | collective-permute-start | bytes 884744 | tf_op jit(solution)/shard_map/ppermute | solution.py:362
  36.1 7.7 %collective-permute-start.7 = (f32[3,24,8,128]{3,2,1,0:T(8,128)S(1)}, f32[3,24,8,128]{3,2,1,0:T(8,128)S(1)}, u32[]{:S(2)}, u32[]{:S(2)}) collective-permute-start(f32[3,24,8,128]{3,2,1,0:T(8,128)S(1)} %get-tuple-element.36), channel_id=1, source_target_pairs={{0,24},{8,0},{16,8},{24,16},{1,25},{9,1},{17,9},{25,17},{2,26},{10... | collective-permute-start | bytes 884744 | tf_op jit(solution)/shard_map/ppermute | solution.py:362
  36.1 6.9 %collective-permute-start.10 = (f32[24,8,128]{2,1,0:T(8,128)S(1)}, f32[24,8,128]{2,1,0:T(8,128)S(1)}, u32[]{:S(2)}, u32[]{:S(2)}) collective-permute-start(f32[24,8,128]{2,1,0:T(8,128)S(1)} %get-tuple-element.46), channel_id=1, source_target_pairs={{0,32},{32,64},{64,96},{96,128},{128,160},{160,192},{192,224},{224... | collective-permute-start | bytes 294920 | tf_op jit(solution)/shard_map/ppermute | solution.py:362
  36.1 6.9 %collective-permute-start.11 = (f32[24,8,128]{2,1,0:T(8,128)S(1)}, f32[24,8,128]{2,1,0:T(8,128)S(1)}, u32[]{:S(2)}, u32[]{:S(2)}) collective-permute-start(f32[24,8,128]{2,1,0:T(8,128)S(1)} %get-tuple-element.47), channel_id=1, source_target_pairs={{0,224},{32,0},{64,32},{96,64},{128,96},{160,128},{192,160},{224,1... | collective-permute-start | bytes 294920 | tf_op jit(solution)/shard_map/ppermute | solution.py:362
